TPU v7x, 32 devices: a whole 2x2x4 slice. The times are simulated.
32 devices in a mesh: ctx: 8 (over z, x), fsdp: 4 (over y, core).
Axes of the slice: x: 2, y: 2, z: 4, core: 2. Of those that a mesh axis runs over, the one named last changes fastest.
Arguments:
- tokens: bfloat16 [4, 1024, 1536], P('fsdp', 'ctx'), may hold values from -6 to 6
- cotangent: bfloat16 [4, 1024, 1536], P('fsdp', 'ctx'), may hold values from -6 to 6
- lengths: int32 [4, 4], P('fsdp'), may hold values from 1 to 512, 1024 in all within a row
- tile_order: int32 [4, 8], P('fsdp'), may hold values from 0 to 7, each once within a row
- routes: int32 [2, 4, 1024, 8], P(None, 'fsdp', 'ctx'), may hold values from 0 to 15, all different within a row; in each aligned block of 128 rows (0 to 127, 128 to 255, ..., all dimensions but the last counted through in order) at most 80 rows name the same one
- gates: float32 [2, 4, 1024, 8], P(None, 'fsdp', 'ctx'), may hold values from 0.1 to 1
- query_weight: float32 [2, 1536, 1536], P(None, ('ctx', 'fsdp')), may hold values from -0.15625 to 0.15625
- key_weight: float32 [2, 1536, 512], P(None, ('ctx', 'fsdp')), may hold values from -0.15625 to 0.15625
- value_weight: float32 [2, 1536, 512], P(None, ('ctx', 'fsdp')), may hold values from -0.15625 to 0.15625
- out_weight: float32 [2, 1536, 1536], P(None, ('ctx', 'fsdp')), may hold values from -0.625 to 0.625
- attn_gain: float32 [2, 1536], P(None, ('ctx', 'fsdp')), may hold values from 0.5 to 1.5
- moe_gain: float32 [2, 1536], P(None, ('ctx', 'fsdp')), may hold values from 0.5 to 1.5
- gate_weight: float32 [2, 16, 1536, 512], P(None, None, ('ctx', 'fsdp')), may hold values from -0.15625 to 0.15625
- up_weight: float32 [2, 16, 1536, 512], P(None, None, ('ctx', 'fsdp')), may hold values from -0.15625 to 0.15625
- down_weight: float32 [2, 16, 1536, 512], P(None, None, ('ctx', 'fsdp')), may hold values from -0.5 to 0.5
Outputs:
- output: bfloat16 [4, 1024, 1536], P('fsdp', 'ctx')
- grad_tokens: float32 [4, 1024, 1536], P('fsdp', 'ctx')
- grad_query_weight: float32 [2, 1536, 1536], P(None, ('ctx', 'fsdp'))
- grad_key_weight: float32 [2, 1536, 512], P(None, ('ctx', 'fsdp'))
- grad_value_weight: float32 [2, 1536, 512], P(None, ('ctx', 'fsdp'))
- grad_out_weight: float32 [2, 1536, 1536], P(None, ('ctx', 'fsdp'))
- grad_attn_gain: float32 [2, 1536], P(None, ('ctx', 'fsdp'))
- grad_moe_gain: float32 [2, 1536], P(None, ('ctx', 'fsdp'))
- grad_gate_weight: float32 [2, 16, 1536, 512], P(None, None, ('ctx', 'fsdp'))
- grad_up_weight: float32 [2, 16, 1536, 512], P(None, None, ('ctx', 'fsdp'))
- grad_down_weight: float32 [2, 16, 1536, 512], P(None, None, ('ctx', 'fsdp'))
Inputs may be any that keep to these rules, and one draw needn't show every extreme that they name: The 4 lengths of a batch sum to 1024 and the longest is 512. `tile_order`: each batch's row holds every tile number once. `routes`: each token names 8 different experts; among the rows of one device in one layer (aligned blocks of 128 rows) no expert is named more than 80 times, and in some blocks one is named exactly 80 times.
All inputs are finite; a program needn't handle non-finite values.
Results may differ from a plain program's by a relative error of at most 0.028.
Values may be sent and summed in bfloat16 or wider, within the bound.
A program may use at most 384 MiB of HBM per device.

v0:
```python
from functools import partial
import math

import jax
import jax.numpy as jnp
from jax import lax
from jax.sharding import PartitionSpec as P

HEAD_DIM = 64
EXPERTS = 16
LAYERS = 2
TILE = 128
CAP = 80


EPSILON = 1e-06
NEGATIVE = -1e30


def layout(lengths, tile_order, group_rows):
    tile_count = tile_order.shape[0]
    row_ids = jnp.arange(group_rows, dtype=jnp.int32)
    in_tile = (row_ids // TILE)[:, None] == jnp.arange(tile_count, dtype=jnp.int32)[None, :]
    tile_of = jnp.sum(jnp.where(in_tile, tile_order[None, :], 0), axis=1, dtype=jnp.int32)
    anchor = tile_of * TILE + row_ids % TILE
    seq_ends = jnp.cumsum(lengths, dtype=jnp.int32)
    seq_starts = seq_ends - lengths
    segment = jnp.sum(
        (anchor[:, None] >= seq_ends[None, :]).astype(jnp.int32), axis=1, dtype=jnp.int32
    )
    picked = segment[:, None] == jnp.arange(lengths.shape[0], dtype=jnp.int32)[None, :]
    offset = jnp.sum(jnp.where(picked, seq_starts[None, :], 0), axis=1, dtype=jnp.int32)
    return (segment, anchor - offset)


def rms_norm(values, gain_vec):
    return (
        values * lax.rsqrt(jnp.mean(values * values, axis=-1, keepdims=True) + EPSILON) * gain_vec
    )


def rotate(values, places):
    half_dim = values.shape[-1] // 2
    freq_steps = jnp.arange(half_dim, dtype=jnp.float32)
    inverse = jnp.exp(freq_steps * (-2.0 * math.log(10000.0) / values.shape[-1]))
    angles = places[:, None] * inverse[None, :]
    cos_part = jnp.cos(angles)[:, None, :]
    sin_part = jnp.sin(angles)[:, None, :]
    first_half = values[..., :half_dim]
    second_half = values[..., half_dim:]
    return jnp.concatenate(
        [
            first_half * cos_part - second_half * sin_part,
            second_half * cos_part + first_half * sin_part,
        ],
        axis=-1,
    )


def rotate_back(grads_in, places):
    return jax.vjp(partial(rotate, places=places), jnp.zeros(grads_in.shape, jnp.float32))[1](
        grads_in
    )[0]


def mix_inner(gate_act, up_act):
    return jax.nn.silu(gate_act) * up_act


def split_halves(master):
    experts_here, rows_here, hidden_units = master.shape
    return (
        master.astype(jnp.bfloat16)
        .reshape(experts_here, rows_here, 2, hidden_units // 2)
        .transpose(0, 2, 1, 3)
        .reshape(2 * experts_here, rows_here, hidden_units // 2)
    )


def merge_halves(grads_in):
    halves_all, rows_here, half_units = grads_in.shape
    return (
        grads_in.reshape(halves_all // 2, 2, rows_here, half_units)
        .transpose(0, 2, 1, 3)
        .reshape(halves_all // 2, rows_here, 2 * half_units)
    )


def doubled(slots):
    return jnp.broadcast_to(slots[:, None], (slots.shape[0], 2) + slots.shape[1:]).reshape(
        (2 * slots.shape[0],) + slots.shape[1:]
    )


def fold_halves(parts):
    return jnp.sum(parts.reshape((parts.shape[0] // 2, 2) + parts.shape[1:]), axis=1)


def send_out(slots):
    return lax.all_to_all(slots, "ctx", split_axis=0, concat_axis=1, tiled=True)


def send_back(parts):
    return lax.all_to_all(
        parts.astype(jnp.bfloat16), "ctx", split_axis=1, concat_axis=0, tiled=True
    ).astype(parts.dtype)


def routing(route_ids, gate_share, rows_here):
    expert_ids = jnp.arange(EXPERTS, dtype=jnp.int32)
    chosen = (route_ids[:, :, None] == expert_ids[None, None, :]).astype(jnp.int32)
    member = jnp.sum(chosen, axis=1, dtype=jnp.int32)
    before = jnp.cumsum(member, axis=0, dtype=jnp.int32) - member
    rank_of = jnp.sum(chosen * before[:, None, :], axis=2, dtype=jnp.int32)
    slot_of = route_ids * CAP + rank_of
    token_ids = jnp.broadcast_to(jnp.arange(rows_here, dtype=jnp.int32)[:, None], route_ids.shape)
    flat_slots = slot_of.reshape(-1)
    slot_token = (
        jnp.full((EXPERTS * CAP,), rows_here, jnp.int32).at[flat_slots].set(token_ids.reshape(-1))
    )
    slot_share = jnp.zeros((EXPERTS * CAP,), jnp.float32).at[flat_slots].set(gate_share.reshape(-1))
    return (slot_of, slot_token, slot_share)


def key_block(key_rows, value_rows, token_meta, block_index, block_rows):
    seg_local, pos_local, seg_all, pos_all = token_meta
    first_row = block_index * block_rows
    key_part = lax.dynamic_slice_in_dim(key_rows, first_row, block_rows, 0)
    value_part = lax.dynamic_slice_in_dim(value_rows, first_row, block_rows, 0)
    seg_part = lax.dynamic_slice_in_dim(seg_all, first_row, block_rows, 0)
    pos_part = lax.dynamic_slice_in_dim(pos_all, first_row, block_rows, 0)
    visible = (seg_local[:, None] == seg_part[None, :]) & (pos_part[None, :] <= pos_local[:, None])
    return (key_part, value_part, visible)


def scores(queries, key_part, visible, score_scale):
    raw_scores = (
        jnp.einsum("qhgd,khd->hgqk", queries, key_part, preferred_element_type=jnp.float32)
        * score_scale
    )
    return jnp.where(visible[None, None], raw_scores, NEGATIVE)


def keep_same(running):
    return running


def attention_forward(queries, key_rows, value_rows, token_meta, block_rows, score_scale):
    block_count = key_rows.shape[0] // block_rows
    rows_here, heads_kv, groups = (queries.shape[0], queries.shape[1], queries.shape[2])

    def stat_step(block_index, running):
        key_part, value_part, visible = key_block(
            key_rows, value_rows, token_meta, block_index, block_rows
        )

        def stat_update(current):
            row_peak, denom_sum = current
            logits = scores(queries, key_part, visible, score_scale)
            new_peak = jnp.maximum(row_peak, jnp.max(logits, axis=-1))
            denom_sum = denom_sum * jnp.exp(row_peak - new_peak) + jnp.sum(
                jnp.exp(logits - new_peak[..., None]), axis=-1
            )
            return (new_peak, denom_sum)

        return lax.cond(jnp.any(visible), stat_update, keep_same, running)

    start_stats = (
        jnp.full((heads_kv, groups, rows_here), NEGATIVE, jnp.float32),
        jnp.zeros((heads_kv, groups, rows_here), jnp.float32),
    )
    row_peak, denom_sum = lax.fori_loop(0, block_count, stat_step, start_stats)

    def out_step(block_index, partial_sum):
        key_part, value_part, visible = key_block(
            key_rows, value_rows, token_meta, block_index, block_rows
        )

        def out_update(current):
            attn_probs = (
                jnp.exp(scores(queries, key_part, visible, score_scale) - row_peak[..., None])
                / denom_sum[..., None]
            )
            return current + jnp.einsum(
                "hgqk,khd->qhgd",
                attn_probs.astype(jnp.bfloat16),
                value_part,
                preferred_element_type=jnp.float32,
            )

        return lax.cond(jnp.any(visible), out_update, keep_same, partial_sum)

    attended = lax.fori_loop(
        0, block_count, out_step, jnp.zeros((rows_here, heads_kv, groups, HEAD_DIM), jnp.float32)
    )
    return ((row_peak, denom_sum), attended)


def attention_backward(
    queries, key_rows, value_rows, token_meta, softmax_stats, grad_attended, block_rows, score_scale
):
    row_peak, denom_sum = softmax_stats
    block_count = key_rows.shape[0] // block_rows

    def probs_for(key_part, visible):
        return (
            jnp.exp(scores(queries, key_part, visible, score_scale) - row_peak[..., None])
            / denom_sum[..., None]
        )

    def delta_step(block_index, partial_sum):
        key_part, value_part, visible = key_block(
            key_rows, value_rows, token_meta, block_index, block_rows
        )

        def delta_update(current):
            attn_probs = probs_for(key_part, visible)
            grad_probs = jnp.einsum(
                "qhgd,khd->hgqk", grad_attended, value_part, preferred_element_type=jnp.float32
            )
            return current + jnp.sum(attn_probs * grad_probs, axis=-1)

        return lax.cond(jnp.any(visible), delta_update, keep_same, partial_sum)

    delta_sum = lax.fori_loop(0, block_count, delta_step, jnp.zeros(denom_sum.shape, jnp.float32))

    def grad_step(block_index, running):
        key_part, value_part, visible = key_block(
            key_rows, value_rows, token_meta, block_index, block_rows
        )
        first_row = block_index * block_rows

        def grad_update(current):
            grad_queries, grad_keys, grad_values = current
            attn_probs = probs_for(key_part, visible)
            grad_probs = jnp.einsum(
                "qhgd,khd->hgqk", grad_attended, value_part, preferred_element_type=jnp.float32
            )
            grad_scores = (attn_probs * (grad_probs - delta_sum[..., None])).astype(jnp.bfloat16)
            grad_queries = grad_queries + jnp.einsum(
                "hgqk,khd->qhgd", grad_scores, key_part, preferred_element_type=jnp.float32
            )
            key_term = jnp.einsum(
                "hgqk,qhgd->khd", grad_scores, queries, preferred_element_type=jnp.float32
            )
            value_term = jnp.einsum(
                "hgqk,qhgd->khd",
                attn_probs.astype(jnp.bfloat16),
                grad_attended,
                preferred_element_type=jnp.float32,
            )
            grad_keys = lax.dynamic_update_slice_in_dim(
                grad_keys,
                lax.dynamic_slice_in_dim(grad_keys, first_row, block_rows, 0) + key_term,
                first_row,
                0,
            )
            grad_values = lax.dynamic_update_slice_in_dim(
                grad_values,
                lax.dynamic_slice_in_dim(grad_values, first_row, block_rows, 0) + value_term,
                first_row,
                0,
            )
            return (grad_queries, grad_keys, grad_values)

        return lax.cond(jnp.any(visible), grad_update, keep_same, running)

    start_grads = (
        jnp.zeros(queries.shape, jnp.float32),
        jnp.zeros(key_rows.shape, jnp.float32),
        jnp.zeros(value_rows.shape, jnp.float32),
    )
    return lax.fori_loop(0, block_count, grad_step, start_grads)


def fetch_layer(master_set, layer_index):
    (
        query_weight,
        key_weight,
        value_weight,
        out_weight,
        attn_gain,
        moe_gain,
        gate_weight,
        up_weight,
        down_weight,
    ) = master_set
    attn_set = (
        lax.all_gather(
            query_weight[layer_index].astype(jnp.bfloat16), ("ctx", "fsdp"), axis=0, tiled=True
        ),
        lax.all_gather(
            key_weight[layer_index].astype(jnp.bfloat16), ("ctx", "fsdp"), axis=0, tiled=True
        ),
        lax.all_gather(
            value_weight[layer_index].astype(jnp.bfloat16), ("ctx", "fsdp"), axis=0, tiled=True
        ),
        lax.all_gather(
            out_weight[layer_index].astype(jnp.bfloat16), ("ctx", "fsdp"), axis=0, tiled=True
        ),
        lax.all_gather(
            attn_gain[layer_index].astype(jnp.bfloat16), ("ctx", "fsdp"), axis=0, tiled=True
        ),
        lax.all_gather(
            moe_gain[layer_index].astype(jnp.bfloat16), ("ctx", "fsdp"), axis=0, tiled=True
        ),
    )
    row_set = (
        lax.all_gather(split_halves(gate_weight[layer_index]), "fsdp", axis=1, tiled=True),
        lax.all_gather(split_halves(up_weight[layer_index]), "fsdp", axis=1, tiled=True),
        lax.all_gather(split_halves(down_weight[layer_index]), "fsdp", axis=1, tiled=True),
    )
    expert_set = (
        lax.all_to_all(row_set[0], "ctx", split_axis=0, concat_axis=1, tiled=True),
        lax.all_to_all(row_set[1], "ctx", split_axis=0, concat_axis=1, tiled=True),
        lax.all_to_all(row_set[2], "ctx", split_axis=0, concat_axis=1, tiled=True),
    )
    return tuple(attn_set) + tuple(expert_set)


def layer_forward(hidden, weights, route_ids, gate_share, token_meta, places, block_rows):
    (
        query_full,
        key_full,
        value_full,
        out_full,
        attn_norm,
        moe_norm,
        gate_full,
        up_full,
        down_full,
    ) = weights
    rows_here, model_width = hidden.shape
    heads_all = query_full.shape[1] // HEAD_DIM
    heads_kv = key_full.shape[1] // HEAD_DIM
    groups = heads_all // heads_kv
    score_scale = HEAD_DIM ** (-0.5)
    normed = rms_norm(hidden, attn_norm.astype(jnp.float32)).astype(jnp.bfloat16)
    queries = rotate(
        jnp.dot(normed, query_full, preferred_element_type=jnp.float32).reshape(
            rows_here, heads_all, HEAD_DIM
        ),
        places,
    ).astype(jnp.bfloat16)
    key_new = (
        rotate(
            jnp.dot(normed, key_full, preferred_element_type=jnp.float32).reshape(
                rows_here, heads_kv, HEAD_DIM
            ),
            places,
        )
        .astype(jnp.bfloat16)
        .reshape(rows_here, heads_kv * HEAD_DIM)
    )
    value_new = jnp.dot(normed, value_full, preferred_element_type=jnp.float32).astype(jnp.bfloat16)
    key_rows, value_rows = (
        lax.all_gather(key_new, "ctx", axis=0, tiled=True),
        lax.all_gather(value_new, "ctx", axis=0, tiled=True),
    )
    key_rows = key_rows.reshape(-1, heads_kv, HEAD_DIM)
    value_rows = value_rows.reshape(-1, heads_kv, HEAD_DIM)
    queries = queries.reshape(rows_here, heads_kv, groups, HEAD_DIM)
    softmax_stats, attended = attention_forward(
        queries, key_rows, value_rows, token_meta, block_rows, score_scale
    )
    attended = attended.reshape(rows_here, heads_all * HEAD_DIM).astype(jnp.bfloat16)
    middle = hidden + jnp.einsum(
        "tx,dx->td", attended, out_full, preferred_element_type=jnp.float32
    )
    moe_in = rms_norm(middle, moe_norm.astype(jnp.float32)).astype(jnp.bfloat16)
    slot_of, slot_token, slot_share = routing(route_ids, gate_share, rows_here)
    padded = jnp.concatenate([moe_in, jnp.zeros((1, model_width), jnp.bfloat16)], axis=0)
    dispatched = jnp.take(padded, slot_token, axis=0).reshape(EXPERTS, CAP, model_width)
    owner_rows = send_out(doubled(dispatched))
    gate_act = jnp.einsum("ecd,edf->ecf", owner_rows, gate_full, preferred_element_type=jnp.float32)
    up_act = jnp.einsum("ecd,edf->ecf", owner_rows, up_full, preferred_element_type=jnp.float32)
    inner_act = mix_inner(gate_act, up_act).astype(jnp.bfloat16)
    expert_part = jnp.einsum(
        "ecf,edf->ecd", inner_act, down_full, preferred_element_type=jnp.float32
    )
    expert_out = fold_halves(send_back(expert_part))
    expert_out = expert_out.reshape(EXPERTS * CAP, model_width)
    moe_out = jnp.sum(jnp.take(expert_out, slot_of, axis=0) * gate_share[..., None], axis=1)
    record = (
        hidden,
        normed,
        queries,
        key_rows,
        value_rows,
        softmax_stats,
        attended,
        middle,
        moe_in,
        slot_of,
        slot_token,
        slot_share,
        owner_rows,
        gate_act,
        up_act,
        inner_act,
    )
    return (record, middle + moe_out)


def layer_backward(grad_hidden, record, weights, token_meta, places, block_rows):
    (
        hidden,
        normed,
        queries,
        key_rows,
        value_rows,
        softmax_stats,
        attended,
        middle,
        moe_in,
        slot_of,
        slot_token,
        slot_share,
        owner_rows,
        gate_act,
        up_act,
        inner_act,
    ) = record
    (
        query_full,
        key_full,
        value_full,
        out_full,
        attn_norm,
        moe_norm,
        gate_full,
        up_full,
        down_full,
    ) = weights
    rows_here, model_width = hidden.shape
    heads_kv, groups = (queries.shape[1], queries.shape[2])
    group_rows = key_rows.shape[0]
    score_scale = HEAD_DIM ** (-0.5)
    grad_padded = jnp.concatenate([grad_hidden, jnp.zeros((1, model_width), jnp.float32)], axis=0)
    grad_expert = (
        (jnp.take(grad_padded, slot_token, axis=0) * slot_share[:, None])
        .astype(jnp.bfloat16)
        .reshape(EXPERTS, CAP, model_width)
    )
    grad_owner = send_out(doubled(grad_expert))
    grad_down = jnp.einsum(
        "ecd,ecf->edf", grad_owner, inner_act, preferred_element_type=jnp.float32
    )
    grad_inner = jnp.einsum(
        "ecd,edf->ecf", grad_owner, down_full, preferred_element_type=jnp.float32
    )
    grad_gate_act, grad_up_act = jax.vjp(mix_inner, gate_act, up_act)[1](grad_inner)
    grad_gate_act = grad_gate_act.astype(jnp.bfloat16)
    grad_up_act = grad_up_act.astype(jnp.bfloat16)
    grad_gate = jnp.einsum(
        "ecd,ecf->edf", owner_rows, grad_gate_act, preferred_element_type=jnp.float32
    )
    grad_up = jnp.einsum(
        "ecd,ecf->edf", owner_rows, grad_up_act, preferred_element_type=jnp.float32
    )
    grad_owner_rows = jnp.einsum(
        "ecf,edf->ecd", grad_gate_act, gate_full, preferred_element_type=jnp.float32
    ) + jnp.einsum("ecf,edf->ecd", grad_up_act, up_full, preferred_element_type=jnp.float32)
    grad_dispatched = fold_halves(send_back(grad_owner_rows))
    home_set = (
        lax.all_to_all(
            grad_gate.astype(jnp.bfloat16), "ctx", split_axis=1, concat_axis=0, tiled=True
        ).astype(grad_gate.dtype),
        lax.all_to_all(
            grad_up.astype(jnp.bfloat16), "ctx", split_axis=1, concat_axis=0, tiled=True
        ).astype(grad_up.dtype),
        lax.all_to_all(
            grad_down.astype(jnp.bfloat16), "ctx", split_axis=1, concat_axis=0, tiled=True
        ).astype(grad_down.dtype),
    )
    summed_set = (
        lax.psum_scatter(
            home_set[0].astype(jnp.bfloat16), "fsdp", scatter_dimension=1, tiled=True
        ).astype(jnp.float32),
        lax.psum_scatter(
            home_set[1].astype(jnp.bfloat16), "fsdp", scatter_dimension=1, tiled=True
        ).astype(jnp.float32),
        lax.psum_scatter(
            home_set[2].astype(jnp.bfloat16), "fsdp", scatter_dimension=1, tiled=True
        ).astype(jnp.float32),
    )
    expert_grads = (
        merge_halves(summed_set[0]),
        merge_halves(summed_set[1]),
        merge_halves(summed_set[2]),
    )
    grad_moe_in = jnp.sum(
        jnp.take(grad_dispatched.reshape(EXPERTS * CAP, model_width), slot_of, axis=0), axis=1
    )
    grad_middle_part, grad_moe_norm = jax.vjp(rms_norm, middle, moe_norm.astype(jnp.float32))[1](
        grad_moe_in
    )
    grad_middle = grad_hidden + grad_middle_part
    grad_rounded = grad_middle.astype(jnp.bfloat16)
    grad_out_full = jnp.einsum(
        "td,tx->dx", grad_rounded, attended, preferred_element_type=jnp.float32
    )
    grad_attended = (
        jnp.dot(grad_rounded, out_full, preferred_element_type=jnp.float32)
        .astype(jnp.bfloat16)
        .reshape(rows_here, heads_kv, groups, HEAD_DIM)
    )
    grad_queries, grad_keys, grad_values = attention_backward(
        queries,
        key_rows,
        value_rows,
        token_meta,
        softmax_stats,
        grad_attended,
        block_rows,
        score_scale,
    )
    key_sums, value_sums = (
        lax.psum_scatter(
            grad_keys.reshape(group_rows, heads_kv * HEAD_DIM).astype(jnp.bfloat16),
            "ctx",
            scatter_dimension=0,
            tiled=True,
        ).astype(jnp.float32),
        lax.psum_scatter(
            grad_values.reshape(group_rows, heads_kv * HEAD_DIM).astype(jnp.bfloat16),
            "ctx",
            scatter_dimension=0,
            tiled=True,
        ).astype(jnp.float32),
    )
    grad_query_rows = (
        rotate_back(
            grad_queries.reshape(rows_here, heads_kv * groups, HEAD_DIM) * score_scale, places
        )
        .astype(jnp.bfloat16)
        .reshape(rows_here, heads_kv * groups * HEAD_DIM)
    )
    grad_key_rows = (
        rotate_back(key_sums.reshape(rows_here, heads_kv, HEAD_DIM) * score_scale, places)
        .astype(jnp.bfloat16)
        .reshape(rows_here, heads_kv * HEAD_DIM)
    )
    grad_value_rows = value_sums.astype(jnp.bfloat16)
    grad_query_full = jnp.einsum(
        "td,tx->dx", normed, grad_query_rows, preferred_element_type=jnp.float32
    )
    grad_key_full = jnp.einsum(
        "td,tx->dx", normed, grad_key_rows, preferred_element_type=jnp.float32
    )
    grad_value_full = jnp.einsum(
        "td,tx->dx", normed, grad_value_rows, preferred_element_type=jnp.float32
    )
    grad_normed = jnp.einsum(
        "tx,dx->td", grad_query_rows, query_full, preferred_element_type=jnp.float32
    )
    grad_normed = grad_normed + jnp.einsum(
        "tx,dx->td", grad_key_rows, key_full, preferred_element_type=jnp.float32
    )
    grad_normed = grad_normed + jnp.einsum(
        "tx,dx->td", grad_value_rows, value_full, preferred_element_type=jnp.float32
    )
    grad_hidden_part, grad_attn_norm = jax.vjp(rms_norm, hidden, attn_norm.astype(jnp.float32))[1](
        grad_normed
    )
    attn_grads = (
        lax.psum_scatter(grad_query_full, ("ctx", "fsdp"), scatter_dimension=0, tiled=True),
        lax.psum_scatter(grad_key_full, ("ctx", "fsdp"), scatter_dimension=0, tiled=True),
        lax.psum_scatter(grad_value_full, ("ctx", "fsdp"), scatter_dimension=0, tiled=True),
        lax.psum_scatter(grad_out_full, ("ctx", "fsdp"), scatter_dimension=0, tiled=True),
        lax.psum_scatter(grad_attn_norm, ("ctx", "fsdp"), scatter_dimension=0, tiled=True),
        lax.psum_scatter(grad_moe_norm, ("ctx", "fsdp"), scatter_dimension=0, tiled=True),
    )
    return (grad_middle + grad_hidden_part, attn_grads, expert_grads)


def body(
    tokens,
    cotangent,
    lengths,
    tile_order,
    routes,
    gates,
    query_weight,
    key_weight,
    value_weight,
    out_weight,
    attn_gain,
    moe_gain,
    gate_weight,
    up_weight,
    down_weight,
):
    rows_here = tokens.shape[1]
    group_rows = rows_here * lax.axis_size("ctx")
    seg_all, pos_all = layout(lengths[0], tile_order[0], group_rows)
    first_row = lax.axis_index("ctx") * rows_here
    seg_local = lax.dynamic_slice_in_dim(seg_all, first_row, rows_here, 0)
    pos_local = lax.dynamic_slice_in_dim(pos_all, first_row, rows_here, 0)
    token_meta = (seg_local, pos_local, seg_all, pos_all)
    places = pos_local.astype(jnp.float32)
    block_rows = math.gcd(group_rows, 512)
    master_set = (
        query_weight,
        key_weight,
        value_weight,
        out_weight,
        attn_gain,
        moe_gain,
        gate_weight,
        up_weight,
        down_weight,
    )
    hidden = tokens[0].astype(jnp.float32)
    records = []
    for layer_index in range(LAYERS):
        weights = fetch_layer(master_set, layer_index)
        record, hidden = layer_forward(
            hidden,
            weights,
            routes[layer_index, 0],
            gates[layer_index, 0],
            token_meta,
            places,
            block_rows,
        )
        records.append(record)
    grad_hidden = cotangent[0].astype(jnp.float32)
    attn_layers = []
    expert_layers = []
    for layer_index in reversed(range(LAYERS)):
        weights = fetch_layer(master_set, layer_index)
        grad_hidden, attn_grads, expert_grads = layer_backward(
            grad_hidden, records[layer_index], weights, token_meta, places, block_rows
        )
        attn_layers.insert(0, attn_grads)
        expert_layers.insert(0, expert_grads)
    grad_query_weight = jnp.stack([layer_grads[0] for layer_grads in attn_layers])
    grad_key_weight = jnp.stack([layer_grads[1] for layer_grads in attn_layers])
    grad_value_weight = jnp.stack([layer_grads[2] for layer_grads in attn_layers])
    grad_out_weight = jnp.stack([layer_grads[3] for layer_grads in attn_layers])
    grad_attn_gain = jnp.stack([layer_grads[4] for layer_grads in attn_layers])
    grad_moe_gain = jnp.stack([layer_grads[5] for layer_grads in attn_layers])
    grad_gate_weight = jnp.stack([layer_grads[0] for layer_grads in expert_layers])
    grad_up_weight = jnp.stack([layer_grads[1] for layer_grads in expert_layers])
    grad_down_weight = jnp.stack([layer_grads[2] for layer_grads in expert_layers])
    return (
        hidden.astype(jnp.bfloat16)[None],
        grad_hidden[None],
        grad_query_weight,
        grad_key_weight,
        grad_value_weight,
        grad_out_weight,
        grad_attn_gain,
        grad_moe_gain,
        grad_gate_weight,
        grad_up_weight,
        grad_down_weight,
    )


def solution(mesh):
    placed = (
        P("fsdp", "ctx", None),
        P("fsdp", "ctx", None),
        P("fsdp", None),
        P("fsdp", None),
        P(None, "fsdp", "ctx", None),
        P(None, "fsdp", "ctx", None),
        P(None, ("ctx", "fsdp"), None),
        P(None, ("ctx", "fsdp"), None),
        P(None, ("ctx", "fsdp"), None),
        P(None, ("ctx", "fsdp"), None),
        P(None, ("ctx", "fsdp")),
        P(None, ("ctx", "fsdp")),
        P(None, None, ("ctx", "fsdp"), None),
        P(None, None, ("ctx", "fsdp"), None),
        P(None, None, ("ctx", "fsdp"), None),
    )
    return jax.shard_map(
        body,
        mesh=mesh,
        in_specs=placed,
        out_specs=(
            P("fsdp", "ctx", None),
            P("fsdp", "ctx", None),
            P(None, ("ctx", "fsdp"), None),
            P(None, ("ctx", "fsdp"), None),
            P(None, ("ctx", "fsdp"), None),
            P(None, ("ctx", "fsdp"), None),
            P(None, ("ctx", "fsdp")),
            P(None, ("ctx", "fsdp")),
            P(None, None, ("ctx", "fsdp"), None),
            P(None, None, ("ctx", "fsdp"), None),
            P(None, None, ("ctx", "fsdp"), None),
        ),
        check_vma=False,
    )
```

profile of v0, /device:TPU:11, one launch (start us, length us, event | category | flops | bytes accessed | tf_op | source)
XLA Modules:
  0.0 4429.6 jit_solution(16656153418441647625)
XLA Ops:
  21.2 40.5 all-reduce.21
  70.3 27.5 all-gather.35.cloned.1.call-done
  103.3 25.2 all-gather.37.cloned.1.call-done
  128.5 44.6 %all-to-all-done.1 = bf16[32,192,256]{2,1,0:T(8,128)(2,1)} async-done(((bf16[32,192,256]{2,1,0:T(8,128)(2,1)}), bf16[32,192,256]{2,1,0:T(8,128)(2,1)}, u32[]{:S(2)}, u32[]{:S(2)}) %all-to-all-start.1) | async-done | bytes 3145760 | tf_op jit(solution)/shard_map/all_to_all | solution.py:314
  183.8 41.5 all-gather.51.cloned.1.call-done
  230.4 23.9 all-gather.39.cloned.1.call-done
  259.8 25.0 all-gather.45.cloned.1.call-done
  284.8 47.3 %all-to-all-done.3 = bf16[32,192,256]{2,1,0:T(8,128)(2,1)} async-done(((bf16[32,192,256]{2,1,0:T(8,128)(2,1)}), bf16[32,192,256]{2,1,0:T(8,128)(2,1)}, u32[]{:S(2)}, u32[]{:S(2)}) %all-to-all-start.3) | async-done | bytes 3145760 | tf_op jit(solution)/shard_map/all_to_all | solution.py:316
  347.1 28.2 all-gather.33.cloned.1.call-done
  377.6 84.9 %all-gather.53.cloned.1.call-done = bf16[1,1536,1536]{2,1,0:T(8,128)(2,1)} async-done(((bf16[1,48,1536]{2,1,0:T(8,128)(2,1)}), bf16[1,1536,1536]{2,1,0:T(8,128)(2,1)}) %all-gather.53.cloned.1.call-update) | async-done | bytes 4718608 | tf_op jit(solution)/shard_map/all_gather | solution.py:289
  473.2 27.2 all-gather.31.cloned.1.call-done
  501.6 19.5 while.128
  521.2 14.1 while.129
  535.5 33.3 all-gather.57.cloned.1.call-done
  595.5 31.6 all-gather.49.cloned.1.call-done
  627.1 136.7 %all-to-all-done = bf16[32,80,1536]{2,1,0:T(8,128)(2,1)} async-done(((bf16[32,80,1536]{2,1,0:T(8,128)(2,1)}), bf16[32,80,1536]{2,1,0:T(8,128)(2,1)}, u32[]{:S(2)}, u32[]{:S(2)}) %all-to-all-start) | async-done | bytes 7864352 | tf_op jit(solution)/shard_map/all_to_all | solution.py:100
  807.0 12.7 copy.365
  819.7 19.1 all-to-all-done.8
  847.9 173.8 %all-to-all-done.4 = bf16[4,640,1536]{2,0,1:T(4,128)(2,1)} async-done(((bf16[4,640,1536]{2,0,1:T(4,128)(2,1)}), bf16[4,640,1536]{2,0,1:T(4,128)(2,1)}, u32[]{:S(2)}, u32[]{:S(2)}) %all-to-all-start.4) | async-done | bytes 7864352 | tf_op jit(solution)/shard_map/all_to_all | solution.py:104
  1057.2 13.6 copy.367
  1123.5 199.6 %all-gather.61.cloned.1.call-done = bf16[1,1536,1536]{2,1,0:T(8,128)(2,1)} async-done(((bf16[1,48,1536]{2,1,0:T(8,128)(2,1)}), bf16[1,1536,1536]{2,1,0:T(8,128)(2,1)}) %all-gather.61.cloned.1.call-update) | async-done | bytes 4718608 | tf_op jit(solution)/shard_map/all_gather | solution.py:289
  1327.6 33.7 all-gather.43.cloned.1.call-done
  1363.5 38.9 all-gather.41.cloned.1.call-done
  1403.7 19.6 while.130
  1423.3 14.1 while.131
  1437.5 33.3 all-gather.65.cloned.1.call-done
  1521.4 145.3 %all-to-all-done.5 = bf16[32,80,1536]{2,1,0:T(8,128)(2,1)} async-done(((bf16[32,80,1536]{2,1,0:T(8,128)(2,1)}), bf16[32,80,1536]{2,1,0:T(8,128)(2,1)}, u32[]{:S(2)}, u32[]{:S(2)}) %all-to-all-start.5) | async-done | bytes 7864352 | tf_op jit(solution)/shard_map/all_to_all | solution.py:100
  1694.9 12.8 copy.383
  1736.3 12.3 copy.391
  1748.6 135.9 %all-to-all-done.9 = bf16[4,640,1536]{2,0,1:T(4,128)(2,1)} async-done(((bf16[4,640,1536]{2,0,1:T(4,128)(2,1)}), bf16[4,640,1536]{2,0,1:T(4,128)(2,1)}, u32[]{:S(2)}, u32[]{:S(2)}) %all-to-all-start.9) | async-done | bytes 7864352 | tf_op jit(solution)/shard_map/all_to_all | solution.py:104
  1904.0 13.6 copy.385
  1917.7 142.4 %all-to-all-done.11 = bf16[4,640,1536]{2,0,1:T(4,128)(2,1)} async-done(((bf16[4,640,1536]{2,0,1:T(4,128)(2,1)}), bf16[4,640,1536]{2,0,1:T(4,128)(2,1)}, u32[]{:S(2)}, u32[]{:S(2)}) %all-to-all-start.11) | async-done | bytes 7864352 | tf_op jit(solution)/shard_map/all_to_all | solution.py:104
  2072.5 13.6 copy.393
  2145.4 18.1 while.132
  2167.6 41.9 while.133
  2171.7 17.0 conditional.21
  2192.5 17.0 conditional.21
  2227.6 49.2 %reduce-scatter.55.cloned.1.call-done = bf16[128,512]{1,0:T(8,128)(2,1)} async-done(((bf16[1024,512]{1,0:T(8,128)(2,1)}), bf16[128,512]{1,0:T(8,128)(2,1)}) %reduce-scatter.55.cloned.1.call-update) | async-done | bytes 131088
  2281.8 62.1 %reduce-scatter.57.cloned.1.call-done = bf16[128,512]{1,0:T(8,128)(2,1)} async-done(((bf16[1024,512]{1,0:T(8,128)(2,1)}), bf16[128,512]{1,0:T(8,128)(2,1)}) %reduce-scatter.57.cloned.1.call-update) | async-done | bytes 131088
  2361.4 172.2 %all_to_all.354 = bf16[32,80,1536]{2,1,0:T(8,128)(2,1)} all-to-all(bf16[32,80,1536]{2,1,0:T(8,128)(2,1)S(1)} %bitcast.678), channel_id=1, replica_groups=mesh['ctx'=8,'fsdp'=4] {'ctx'}, dimensions={0} | all-to-all | bytes 15728640 | tf_op jit(solution)/shard_map/all_to_all | solution.py:100
  2568.1 12.7 copy.399
  2594.9 13.1 copy.430
  2608.0 149.7 %all-to-all-done.13 = bf16[4,640,1536]{2,0,1:T(4,128)(2,1)} async-done(((bf16[4,640,1536]{2,0,1:T(4,128)(2,1)}), bf16[4,640,1536]{2,0,1:T(4,128)(2,1)}, u32[]{:S(2)}, u32[]{:S(2)}) %all-to-all-start.13) | async-done | bytes 7864352 | tf_op jit(solution)/shard_map/all_to_all | solution.py:104
  2777.0 13.6 copy.401
  2824.5 18.3 while.134
  2846.9 41.7 while.135
  2850.8 17.0 conditional.23
  2871.6 17.0 conditional.23
  2907.2 12.0 copy.420
  2919.2 84.4 %all_to_all.355 = bf16[4,1536,256]{2,0,1:T(4,128)(2,1)S(1)} all-to-all(bf16[4,1536,256]{2,0,1:T(4,128)(2,1)S(1)} %copy.420), channel_id=1, replica_groups=mesh['ctx'=8,'fsdp'=4] {'ctx'}, dimensions={1} | all-to-all | bytes 6291456 | tf_op jit(solution)/shard_map/all_to_all | solution.py:469
  3013.8 12.0 copy.410
  3025.9 73.8 %all_to_all.356 = bf16[4,1536,256]{2,0,1:T(4,128)(2,1)S(1)} all-to-all(bf16[4,1536,256]{2,0,1:T(4,128)(2,1)S(1)} %copy.410), channel_id=1, replica_groups=mesh['ctx'=8,'fsdp'=4] {'ctx'}, dimensions={1} | all-to-all | bytes 6291456 | tf_op jit(solution)/shard_map/all_to_all | solution.py:466
  3121.9 73.5 %all_to_all.357 = bf16[4,1536,256]{2,0,1:T(4,128)(2,1)S(1)} all-to-all(bf16[4,1536,256]{2,0,1:T(4,128)(2,1)S(1)} %copy.425), channel_id=1, replica_groups=mesh['ctx'=8,'fsdp'=4] {'ctx'}, dimensions={1} | all-to-all | bytes 6291456 | tf_op jit(solution)/shard_map/all_to_all | solution.py:472
  3217.7 73.7 %all_to_all.358 = bf16[4,1536,256]{2,0,1:T(4,128)(2,1)S(1)} all-to-all(bf16[4,1536,256]{2,0,1:T(4,128)(2,1)S(1)} %copy.415), channel_id=1, replica_groups=mesh['ctx'=8,'fsdp'=4] {'ctx'}, dimensions={1} | all-to-all | bytes 6291456 | tf_op jit(solution)/shard_map/all_to_all | solution.py:469
  3313.7 73.7 %all_to_all.359 = bf16[4,1536,256]{2,0,1:T(4,128)(2,1)S(1)} all-to-all(bf16[4,1536,256]{2,0,1:T(4,128)(2,1)S(1)} %copy.405), channel_id=1, replica_groups=mesh['ctx'=8,'fsdp'=4] {'ctx'}, dimensions={1} | all-to-all | bytes 6291456 | tf_op jit(solution)/shard_map/all_to_all | solution.py:466
  3470.1 43.9 all-reduce.20
  3516.6 20.5 reduce-scatter.37.cloned.1.call-done
  3537.1 106.5 %reduce-scatter.35.cloned.1.call-done = f32[48,512]{1,0:T(8,128)} async-done(((f32[1536,512]{1,0:T(8,128)}), f32[48,512]{1,0:T(8,128)}) %reduce-scatter.35.cloned.1.call-update) | async-done | bytes 98320 | tf_op jit(solution)/shard_map/reduce_scatter | solution.py:569
  3645.3 105.0 %reduce-scatter.33.cloned.1.call-done = f32[48,512]{1,0:T(8,128)} async-done(((f32[1536,512]{1,0:T(8,128)}), f32[48,512]{1,0:T(8,128)}) %reduce-scatter.33.cloned.1.call-update) | async-done | bytes 98320 | tf_op jit(solution)/shard_map/reduce_scatter | solution.py:568
  3750.3 106.7 %reduce-scatter.31.cloned.1.call-done = f32[48,512]{1,0:T(8,128)} async-done(((f32[1536,512]{1,0:T(8,128)}), f32[48,512]{1,0:T(8,128)}) %reduce-scatter.31.cloned.1.call-update) | async-done | bytes 98320 | tf_op jit(solution)/shard_map/reduce_scatter | solution.py:568
  3858.6 139.1 %reduce-scatter.41.cloned.1.call-done = f32[48,1536]{1,0:T(8,128)} async-done(((f32[1536,1536]{1,0:T(8,128)}), f32[48,1536]{1,0:T(8,128)}) %reduce-scatter.41.cloned.1.call-update) | async-done | bytes 294928 | tf_op jit(solution)/shard_map/reduce_scatter | solution.py:570
  3997.8 141.0 %reduce-scatter.39.cloned.1.call-done = f32[48,1536]{1,0:T(8,128)} async-done(((f32[1536,1536]{1,0:T(8,128)}), f32[48,1536]{1,0:T(8,128)}) %reduce-scatter.39.cloned.1.call-update) | async-done | bytes 294928 | tf_op jit(solution)/shard_map/reduce_scatter | solution.py:570
  4140.7 139.1 %reduce-scatter.29.cloned.1.call-done = f32[48,1536]{1,0:T(8,128)} async-done(((f32[1536,1536]{1,0:T(8,128)}), f32[48,1536]{1,0:T(8,128)}) %reduce-scatter.29.cloned.1.call-update) | async-done | bytes 294928 | tf_op jit(solution)/shard_map/reduce_scatter | solution.py:567
  4279.8 140.9 %reduce-scatter.27.cloned.1.call-done = f32[48,1536]{1,0:T(8,128)} async-done(((f32[1536,1536]{1,0:T(8,128)}), f32[48,1536]{1,0:T(8,128)}) %reduce-scatter.27.cloned.1.call-update) | async-done | bytes 294928 | tf_op jit(solution)/shard_map/reduce_scatter | solution.py:567
  (780 shorter events, 1023.1 us)
Async XLA Ops:
  7.2 59.8 %all-gather.55.cloned.1.call-start = ((), (), s32[]{:S(2)}) async-start(), calls=%async_computation.64 | async-start | bytes 1622016 | tf_op jit(solution)/shard_map/all_gather | solution.py:295
  8.8 89.0 %all-gather.35.cloned.1.call-start = ((), (), s32[]{:S(2)}) async-start(), calls=%async_computation.40 | async-start | bytes 3932160 | tf_op jit(solution)/shard_map/all_gather | solution.py:309
  13.1 115.4 %all-gather.37.cloned.1.call-start = ((), (), s32[]{:S(2)}) async-start(), calls=%async_computation.41 | async-start | bytes 3932160 | tf_op jit(solution)/shard_map/all_gather | solution.py:310
  15.8 209.6 %all-gather.51.cloned.1.call-start = ((), (), s32[]{:S(2)}) async-start(), calls=%async_computation.62 | async-start | bytes 1622016 | tf_op jit(solution)/shard_map/all_gather | solution.py:292
  17.5 236.8 %all-gather.39.cloned.1.call-start = ((), (), s32[]{:S(2)}) async-start(), calls=%async_computation.42 | async-start | bytes 3932160 | tf_op jit(solution)/shard_map/all_gather | solution.py:311
  19.1 265.8 %all-gather.45.cloned.1.call-start = ((), (), s32[]{:S(2)}) async-start(), calls=%async_computation.45 | async-start | bytes 3932160 | tf_op jit(solution)/shard_map/all_gather | solution.py:309
  20.1 355.2 %all-gather.33.cloned.1.call-start = ((), (), s32[]{:S(2)}) async-start(), calls=%async_computation.39 | async-start | bytes 1179648 | tf_op jit(solution)/shard_map/all_gather | solution.py:358
  61.7 407.4 %copy-start.72 = (f32[1536]{0:T(1024)}, f32[1536]{0:T(1024)S(1)}, u32[]{:S(2)}) copy-start(f32[1536]{0:T(1024)S(1)} %convert_element_type.575) | copy-start | bytes 18436
  61.9 407.3 %copy-start.91 = (f32[128]{0:T(128)}, f32[128]{0:T(128)S(1)}, u32[]{:S(2)}) copy-start(f32[128]{0:T(128)S(1)} %fusion.246) | copy-start | bytes 1540
  69.5 393.0 %all-gather.53.cloned.1.call-start = ((), (), s32[]{:S(2)}) async-start(), calls=%async_computation.63 | async-start | bytes 4866048 | tf_op jit(solution)/shard_map/all_gather | solution.py:289
  97.8 75.3 %all-to-all-start.1 = ((bf16[32,192,256]{2,1,0:T(8,128)(2,1)}), bf16[32,192,256]{2,1,0:T(8,128)(2,1)}, u32[]{:S(2)}, u32[]{:S(2)}) async-start(bf16[32,192,256]{2,1,0:T(8,128)(2,1)} %all-gather.35.cloned.1.call-done), calls=%async_computation.1 | async-start | bytes 6291456 | tf_op jit(solution)/shard_map/all_to_all | solution.py:314
  173.1 81.2 %all-to-all-start.2 = ((bf16[32,192,256]{2,1,0:T(8,128)(2,1)}), bf16[32,192,256]{2,1,0:T(8,128)(2,1)}, u32[]{:S(2)}, u32[]{:S(2)}) async-start(bf16[32,192,256]{2,1,0:T(8,128)(2,1)} %all-gather.37.cloned.1.call-done), calls=%async_computation.2 | async-start | bytes 6291456 | tf_op jit(solution)/shard_map/all_to_all | solution.py:315
  180.0 320.4 %all-gather.31.cloned.1.call-start = ((), (), s32[]{:S(2)}) async-start(), calls=%async_computation.38 | async-start | bytes 1179648 | tf_op jit(solution)/shard_map/all_gather | solution.py:357
  183.8 289.2 %copy-start.56 = (f32[128,32]{0,1:T(8,128)}, f32[128,32]{0,1:T(8,128)S(1)}, u32[]{:S(2)}) copy-start(f32[128,32]{0,1:T(8,128)S(1)} %get-tuple-element.2607) | copy-start | bytes 49156
  183.8 289.2 %copy-start.60 = (f32[128,32]{0,1:T(8,128)}, f32[128,32]{0,1:T(8,128)S(1)}, u32[]{:S(2)}) copy-start(f32[128,32]{0,1:T(8,128)S(1)} %get-tuple-element.2608) | copy-start | bytes 49156
  228.5 340.3 %all-gather.57.cloned.1.call-start = ((), (), s32[]{:S(2)}) async-start(), calls=%async_computation.65 | async-start | bytes 4866048 | tf_op jit(solution)/shard_map/all_gather | solution.py:298
  254.3 77.9 %all-to-all-start.3 = ((bf16[32,192,256]{2,1,0:T(8,128)(2,1)}), bf16[32,192,256]{2,1,0:T(8,128)(2,1)}, u32[]{:S(2)}, u32[]{:S(2)}) async-start(bf16[32,192,256]{2,1,0:T(8,128)(2,1)} %all-gather.39.cloned.1.call-done), calls=%async_computation.3 | async-start | bytes 6291456 | tf_op jit(solution)/shard_map/all_to_all | solution.py:316
  332.2 250.9 %all-to-all-start.6 = ((bf16[32,192,256]{2,1,0:T(8,128)(2,1)}), bf16[32,192,256]{2,1,0:T(8,128)(2,1)}, u32[]{:S(2)}, u32[]{:S(2)}) async-start(bf16[32,192,256]{2,1,0:T(8,128)(2,1)} %all-gather.45.cloned.1.call-done), calls=%async_computation.6 | async-start | bytes 6291456 | tf_op jit(solution)/shard_map/all_to_all | solution.py:314
  340.0 232.9 %copy-start.79 = (f32[1536]{0:T(1024)}, f32[1536]{0:T(1024)S(1)}, u32[]{:S(2)}) copy-start(f32[1536]{0:T(1024)S(1)} %convert_element_type.576) | copy-start | bytes 18436
  347.1 226.0 %copy-start.85 = (s32[2048]{0:T(1024)}, s32[2048]{0:T(1024)S(1)}, u32[]{:S(2)}) copy-start(s32[2048]{0:T(1024)S(1)} %pad_clamp_fusion.1) | copy-start | bytes 24580
  347.1 231.5 %copy-start.93 = (pred[1280]{0:T(1024)(128)(4,1)}, pred[1280]{0:T(1024)(128)(4,1)S(1)}, u32[]{:S(2)}) copy-start(pred[1280]{0:T(1024)(128)(4,1)S(1)} %compare_and_fusion.9) | copy-start | bytes 3844
  572.9 524.7 %copy-start.12 = (f32[128,1536]{1,0:T(8,128)}, f32[128,1536]{1,0:T(8,128)S(1)}, u32[]{:S(2)}) copy-start(f32[128,1536]{1,0:T(8,128)S(1)} %get-tuple-element.2614) | copy-start | bytes 2359300
  589.4 174.5 %all-to-all-start = ((bf16[32,80,1536]{2,1,0:T(8,128)(2,1)}), bf16[32,80,1536]{2,1,0:T(8,128)(2,1)}, u32[]{:S(2)}, u32[]{:S(2)}) async-start(bf16[32,80,1536]{2,1,0:T(8,128)(2,1)} %bitcast.673), calls=%async_computation | async-start | bytes 15728640 | tf_op jit(solution)/shard_map/all_to_all | solution.py:100
  594.5 32.6 all-gather.49.cloned.1.call-start
  763.8 75.0 %all-to-all-start.8 = ((bf16[32,192,256]{2,1,0:T(8,128)(2,1)}), bf16[32,192,256]{2,1,0:T(8,128)(2,1)}, u32[]{:S(2)}, u32[]{:S(2)}) async-start(bf16[32,192,256]{2,1,0:T(8,128)(2,1)} %all-gather.49.cloned.1.call-done), calls=%async_computation.8 | async-start | bytes 6291456 | tf_op jit(solution)/shard_map/all_to_all | solution.py:316
  770.6 77.3 %all-gather.47.cloned.1.call-start = ((), (), s32[]{:S(2)}) async-start(), calls=%async_computation.46 | async-start | bytes 3932160 | tf_op jit(solution)/shard_map/all_gather | solution.py:310
  838.8 182.9 %all-to-all-start.4 = ((bf16[4,640,1536]{2,0,1:T(4,128)(2,1)}), bf16[4,640,1536]{2,0,1:T(4,128)(2,1)}, u32[]{:S(2)}, u32[]{:S(2)}) async-start(bf16[4,640,1536]{2,0,1:T(4,128)(2,1)} %copy.365), calls=%async_computation.4 | async-start | bytes 15728640 | tf_op jit(solution)/shard_map/all_to_all | solution.py:104
  845.3 252.7 %all-gather.63.cloned.1.call-start = ((), (), s32[]{:S(2)}) async-start(), calls=%async_computation.68 | async-start | bytes 1622016 | tf_op jit(solution)/shard_map/all_gather | solution.py:295
  846.0 273.9 %all-gather.59.cloned.1.call-start = ((), (), s32[]{:S(2)}) async-start(), calls=%async_computation.66 | async-start | bytes 1622016 | tf_op jit(solution)/shard_map/all_gather | solution.py:292
  846.6 476.5 %all-gather.61.cloned.1.call-start = ((), (), s32[]{:S(2)}) async-start(), calls=%async_computation.67 | async-start | bytes 4866048 | tf_op jit(solution)/shard_map/all_gather | solution.py:289
  847.9 180.3 %copy-start.99 = (f32[2,1,128,8]{2,3,1,0:T(8,128)S(1)}, f32[2,1,128,8]{2,3,1,0:T(8,128)}, u32[]{:S(2)}) copy-start(f32[2,1,128,8]{2,3,1,0:T(8,128)} %param.58) | copy-start | bytes 24580
  847.9 181.4 %copy-start.108 = (bf16[1536]{0:T(1024)(128)(2,1)S(1)}, bf16[1536]{0:T(1024)(128)(2,1)}, u32[]{:S(2)}) copy-start(bf16[1536]{0:T(1024)(128)(2,1)} %get-tuple-element.2518) | copy-start | bytes 9220
  847.9 181.5 %copy-start.98 = (s32[1,1,128,8]{2,3,1,0:T(8,128)S(1)}, s32[1,1,128,8]{2,3,1,0:T(8,128)}, u32[]{:S(2)}) copy-start(s32[1,1,128,8]{2,3,1,0:T(8,128)} %get-tuple-element.2605) | copy-start | bytes 12292
  1021.7 84.0 %all-to-all-start.7 = ((bf16[32,192,256]{2,1,0:T(8,128)(2,1)}), bf16[32,192,256]{2,1,0:T(8,128)(2,1)}, u32[]{:S(2)}, u32[]{:S(2)}) async-start(bf16[32,192,256]{2,1,0:T(8,128)(2,1)} %all-gather.47.cloned.1.call-done), calls=%async_computation.7 | async-start | bytes 6291456 | tf_op jit(solution)/shard_map/all_to_all | solution.py:315
  1028.2 333.1 %all-gather.43.cloned.1.call-start = ((), (), s32[]{:S(2)}) async-start(), calls=%async_computation.44 | async-start | bytes 1179648 | tf_op jit(solution)/shard_map/all_gather | solution.py:358
  1097.8 373.1 %copy-start.14 = (f32[128,1536]{1,0:T(8,128)}, f32[128,1536]{1,0:T(8,128)S(1)}, u32[]{:S(2)}) copy-start(f32[128,1536]{1,0:T(8,128)S(1)} %get-tuple-element.2539) | copy-start | bytes 2359300
  1097.9 225.2 %copy-start.8 = (bf16[128,1536]{1,0:T(8,128)(2,1)}, bf16[128,1536]{1,0:T(8,128)(2,1)S(1)}, u32[]{:S(2)}) copy-start(bf16[128,1536]{1,0:T(8,128)(2,1)S(1)} %multiply_convert_fusion.5) | copy-start | bytes 1179652
  1112.3 373.7 %all-to-all-start.10 = ((bf16[32,80,1536]{2,1,0:T(8,128)(2,1)}), bf16[32,80,1536]{2,1,0:T(8,128)(2,1)}, u32[]{:S(2)}, u32[]{:S(2)}) async-start(bf16[32,80,1536]{2,1,0:T(8,128)(2,1)} %bitcast.672), calls=%async_computation.10 | async-start | bytes 15728640 | tf_op jit(solution)/shard_map/all_to_all | solution.py:100
  1117.9 284.6 %all-gather.41.cloned.1.call-start = ((), (), s32[]{:S(2)}) async-start(), calls=%async_computation.43 | async-start | bytes 1179648 | tf_op jit(solution)/shard_map/all_gather | solution.py:357
  1122.9 348.0 %all-gather.65.cloned.1.call-start = ((), (), s32[]{:S(2)}) async-start(), calls=%async_computation.69 | async-start | bytes 4866048 | tf_op jit(solution)/shard_map/all_gather | solution.py:298
  1123.5 351.5 %copy-start.83 = (f32[1536]{0:T(1024)}, f32[1536]{0:T(1024)S(1)}, u32[]{:S(2)}) copy-start(f32[1536]{0:T(1024)S(1)} %convert_element_type.578) | copy-start | bytes 18436
  1492.2 174.5 %all-to-all-start.5 = ((bf16[32,80,1536]{2,1,0:T(8,128)(2,1)}), bf16[32,80,1536]{2,1,0:T(8,128)(2,1)}, u32[]{:S(2)}, u32[]{:S(2)}) async-start(bf16[32,80,1536]{2,1,0:T(8,128)(2,1)} %bitcast.674), calls=%async_computation.5 | async-start | bytes 15728640 | tf_op jit(solution)/shard_map/all_to_all | solution.py:100
  1707.7 176.8 %all-to-all-start.9 = ((bf16[4,640,1536]{2,0,1:T(4,128)(2,1)}), bf16[4,640,1536]{2,0,1:T(4,128)(2,1)}, u32[]{:S(2)}, u32[]{:S(2)}) async-start(bf16[4,640,1536]{2,0,1:T(4,128)(2,1)} %copy.383), calls=%async_computation.9 | async-start | bytes 15728640 | tf_op jit(solution)/shard_map/all_to_all | solution.py:104
  1884.5 175.6 %all-to-all-start.11 = ((bf16[4,640,1536]{2,0,1:T(4,128)(2,1)}), bf16[4,640,1536]{2,0,1:T(4,128)(2,1)}, u32[]{:S(2)}, u32[]{:S(2)}) async-start(bf16[4,640,1536]{2,0,1:T(4,128)(2,1)} %copy.391), calls=%async_computation.11 | async-start | bytes 15728640 | tf_op jit(solution)/shard_map/all_to_all | solution.py:104
  1891.0 385.8 %reduce-scatter.55.cloned.1.call-start = ((), (), s32[]{:S(2)}) async-start(), calls=%async_computation.70 | async-start | bytes 1179648
  2212.6 131.3 %reduce-scatter.57.cloned.1.call-start = ((), (), s32[]{:S(2)}) async-start(), calls=%async_computation.71 | async-start | bytes 1179648
  2580.8 176.9 %all-to-all-start.13 = ((bf16[4,640,1536]{2,0,1:T(4,128)(2,1)}), bf16[4,640,1536]{2,0,1:T(4,128)(2,1)}, u32[]{:S(2)}, u32[]{:S(2)}) async-start(bf16[4,640,1536]{2,0,1:T(4,128)(2,1)} %copy.399), calls=%async_computation.13 | async-start | bytes 15728640 | tf_op jit(solution)/shard_map/all_to_all | solution.py:104
  2757.7 137.3 %all-to-all-start.19 = ((bf16[4,1536,256]{2,0,1:T(4,128)(2,1)}), bf16[4,1536,256]{2,0,1:T(4,128)(2,1)}, u32[]{:S(2)}, u32[]{:S(2)}) async-start(bf16[4,1536,256]{2,0,1:T(4,128)(2,1)} %copy.430), calls=%async_computation.32 | async-start | bytes 6291456 | tf_op jit(solution)/shard_map/all_to_all | solution.py:472
  2764.1 629.0 %reduce-scatter.61.cloned.1.call-start = ((), (), s32[]{:S(2)}) async-start(), calls=%async_computation.73 | async-start | bytes 1179648
  2891.8 507.0 %reduce-scatter.59.cloned.1.call-start = ((), (), s32[]{:S(2)}) async-start(), calls=%async_computation.72 | async-start | bytes 1179648
  2895.0 531.7 %reduce-scatter.53.cloned.1.call-start = ((), (), s32[]{:S(2)}) async-start(), calls=%async_computation.61 | async-start | bytes 3932160 | tf_op jit(solution)/shard_map/reduce_scatter | solution.py:483
  2899.3 529.8 %reduce-scatter.49.cloned.1.call-start = ((), (), s32[]{:S(2)}) async-start(), calls=%async_computation.59 | async-start | bytes 3932160 | tf_op jit(solution)/shard_map/reduce_scatter | solution.py:480
  3006.1 428.5 %reduce-scatter.45.cloned.1.call-start = ((), (), s32[]{:S(2)}) async-start(), calls=%async_computation.57 | async-start | bytes 3932160 | tf_op jit(solution)/shard_map/reduce_scatter | solution.py:477
  3102.1 338.4 %reduce-scatter.51.cloned.1.call-start = ((), (), s32[]{:S(2)}) async-start(), calls=%async_computation.60 | async-start | bytes 3932160 | tf_op jit(solution)/shard_map/reduce_scatter | solution.py:483
  3197.9 248.5 %reduce-scatter.47.cloned.1.call-start = ((), (), s32[]{:S(2)}) async-start(), calls=%async_computation.58 | async-start | bytes 3932160 | tf_op jit(solution)/shard_map/reduce_scatter | solution.py:480
  3293.8 158.5 %reduce-scatter.43.cloned.1.call-start = ((), (), s32[]{:S(2)}) async-start(), calls=%async_computation.56 | async-start | bytes 3932160 | tf_op jit(solution)/shard_map/reduce_scatter | solution.py:477
  3389.8 147.3 %reduce-scatter.37.cloned.1.call-start = ((), (), s32[]{:S(2)}) async-start(), calls=%async_computation.53 | async-start | bytes 3244032 | tf_op jit(solution)/shard_map/reduce_scatter | solution.py:569
  3393.1 250.6 %reduce-scatter.35.cloned.1.call-start = ((), (), s32[]{:S(2)}) async-start(), calls=%async_computation.52 | async-start | bytes 3244032 | tf_op jit(solution)/shard_map/reduce_scatter | solution.py:569
  3396.4 353.9 %reduce-scatter.33.cloned.1.call-start = ((), (), s32[]{:S(2)}) async-start(), calls=%async_computation.51 | async-start | bytes 3244032 | tf_op jit(solution)/shard_map/reduce_scatter | solution.py:568
  3398.7 458.3 %reduce-scatter.31.cloned.1.call-start = ((), (), s32[]{:S(2)}) async-start(), calls=%async_computation.50 | async-start | bytes 3244032 | tf_op jit(solution)/shard_map/reduce_scatter | solution.py:568
  3402.4 595.4 %reduce-scatter.41.cloned.1.call-start = ((), (), s32[]{:S(2)}) async-start(), calls=%async_computation.55 | async-start | bytes 9732096 | tf_op jit(solution)/shard_map/reduce_scatter | solution.py:570
  3407.8 731.0 %reduce-scatter.39.cloned.1.call-start = ((), (), s32[]{:S(2)}) async-start(), calls=%async_computation.54 | async-start | bytes 9732096 | tf_op jit(solution)/shard_map/reduce_scatter | solution.py:570
  3414.2 865.6 %reduce-scatter.29.cloned.1.call-start = ((), (), s32[]{:S(2)}) async-start(), calls=%async_computation.49 | async-start | bytes 9732096 | tf_op jit(solution)/shard_map/reduce_scatter | solution.py:567
  3420.1 1000.6 %reduce-scatter.27.cloned.1.call-start = ((), (), s32[]{:S(2)}) async-start(), calls=%async_computation.48 | async-start | bytes 9732096 | tf_op jit(solution)/shard_map/reduce_scatter | solution.py:567
  (116 other events, 2391.3 us)
Sparse Core Ops, SparseCore 0:
  11.4 55.4 all-gather.54
  69.1 28.6 all-gather.34
  100.0 28.4 all-gather.36
  131.2 94.0 all-gather.50
  227.4 26.8 all-gather.38
  256.3 28.4 all-gather.44
  287.0 88.3 all-gather.32
  378.8 83.6 all-gather.52
  465.1 35.2 all-gather.30
  503.7 64.9 all-gather.56
  597.5 29.6 all-gather.48
  773.3 30.5 all-gather.46
  849.0 158.1 all-gather.62
  1009.9 110.0 all-gather.58
  1123.3 199.7 all-gather.60
  1325.7 35.5 all-gather.42
  1363.7 38.6 all-gather.40
  1405.8 65.0 all-gather.64
  2212.7 64.0 reduce-scatter.54
  2280.6 63.2 reduce-scatter.56
  2891.9 70.0 reduce-scatter.60
  2965.4 64.9 reduce-scatter.58
  3033.0 38.6 reduce-scatter.52
  3074.7 37.7 reduce-scatter.48
  3115.5 37.7 reduce-scatter.44
  3198.0 40.8 reduce-scatter.50
  3294.0 40.8 reduce-scatter.46
  3389.9 40.8 reduce-scatter.42
  3436.2 100.8 reduce-scatter.36
  3542.4 101.2 reduce-scatter.34
  3649.1 101.1 reduce-scatter.32
  3755.7 101.1 reduce-scatter.30
  3862.7 134.9 reduce-scatter.40
  4003.7 135.0 reduce-scatter.38
  4144.7 135.0 reduce-scatter.28
  4285.5 135.0 reduce-scatter.26
where the time goes:
time: 4450 us; the launch traced here: 4430 us
  waiting for transfers between devices  2670 us (60%)
  blocking collectives  636 us (14%)
  local copies, waits for them, and re-layouts  491 us (11%)
  matrix products  313 us (7%)
  other arithmetic  201 us (5%)
  starting transfers between devices  91.7 us (2%)
    all_to_all x4, waiting for transfers between devices, send_back(): lax.all_to_all(parts.astype(jnp.bfloat16), 'ctx', split_axis=1, concat_ax...  602 us
    all_gather x2, waiting for transfers between devices, fetch_layer(): lax.all_gather(query_weight[layer_index].astype(jnp.bfloat16), ('ctx', 'f...  285 us
    all_to_all x3, waiting for transfers between devices, send_out(): return lax.all_to_all(slots, 'ctx', split_axis=0, concat_axis=1, tiled=True)  282 us
    reduce_scatter x2, waiting for transfers between devices, layer_backward(): lax.psum_scatter(grad_out_full, ('ctx', 'fsdp'), scatter_dimension=0, til...  280 us
    reduce_scatter x2, waiting for transfers between devices, layer_backward(): lax.psum_scatter(grad_query_full, ('ctx', 'fsdp'), scatter_dimension=0, t...  280 us
    reduce_scatter x2, waiting for transfers between devices, layer_backward(): lax.psum_scatter(grad_key_full, ('ctx', 'fsdp'), scatter_dimension=0, til...  212 us
    all_to_all x1, blocking collectives, send_out(): return lax.all_to_all(slots, 'ctx', split_axis=0, concat_axis=1, tiled=True)  172 us
    all_to_all x2, blocking collectives, layer_backward(): lax.all_to_all(grad_up.astype(jnp.bfloat16), 'ctx', split_axis=1, concat_...  158 us
  transfers between devices with their start and end apart: 50, of which 35 were waited for; matrix products, arithmetic and copies ran while one was open for 16% of the time, Pallas kernels for 0%

commit v1 on v0

--- a/solution.py
+++ b/solution.py
@@ -1,9 +1,12 @@
 from functools import partial
+import functools
 import math
 
 import jax
 import jax.numpy as jnp
 from jax import lax
+from jax.experimental import pallas as pl
+from jax.experimental.pallas import tpu as pltpu
 from jax.sharding import PartitionSpec as P
 
 HEAD_DIM = 64
@@ -659,6 +662,691 @@
     )
 
 
+BF = jnp.bfloat16
+F32 = jnp.float32
+NX = 2
+NCORE = 2
+
+
+def at_device(ctx, fsdp):
+    return {"ctx": ctx, "fsdp": fsdp}
+
+
+def remote(src, dst, send_sem, recv_sem, ctx, fsdp):
+    return pltpu.make_async_remote_copy(
+        src_ref=src, dst_ref=dst, send_sem=send_sem, recv_sem=recv_sem,
+        device_id={"ctx": ctx, "fsdp": fsdp}, device_id_type=pl.DeviceIdType.MESH,
+    )
+
+
+def greet_line(nz, z, x, fsdp):
+    barrier = pltpu.get_barrier_semaphore()
+    pl.semaphore_signal(barrier, inc=1, device_id={"ctx": z * NX + 1 - x, "fsdp": fsdp}, device_id_type=pl.DeviceIdType.MESH)
+
+    @pl.when(z > 0)
+    def _():
+        pl.semaphore_signal(barrier, inc=1, device_id={"ctx": (z - 1) * NX + x, "fsdp": fsdp}, device_id_type=pl.DeviceIdType.MESH)
+
+    @pl.when(z < nz - 1)
+    def _():
+        pl.semaphore_signal(barrier, inc=1, device_id={"ctx": (z + 1) * NX + x, "fsdp": fsdp}, device_id_type=pl.DeviceIdType.MESH)
+
+    pl.semaphore_wait(barrier, 1 + jnp.where(z > 0, 1, 0) + jnp.where(z < nz - 1, 1, 0))
+
+
+def gather_kernel(nz, x_ref, o_ref, own_sem, up_send, up_recv, down_send, down_recv, x_send, x_recv):
+    ctx, fsdp = lax.axis_index("ctx"), lax.axis_index("fsdp")
+    z, x = ctx // NX, ctx % NX
+    greet_line(nz, z, x, fsdp)
+    other = 1 - x
+
+    def up(t):
+        src = x_ref if t == 0 else o_ref.at[(z - t) * NX + x]
+        return remote(src, o_ref.at[(z - t) * NX + x], up_send.at[t], up_recv.at[t], (z + 1) * NX + x, fsdp)
+
+    def down(t):
+        src = x_ref if t == 0 else o_ref.at[(z + t) * NX + x]
+        return remote(src, o_ref.at[(z + t) * NX + x], down_send.at[t], down_recv.at[t], (z - 1) * NX + x, fsdp)
+
+    def up_in(t):
+        return remote(x_ref, o_ref.at[(z - 1 - t) * NX + x], up_send.at[t], up_recv.at[t], (z + 1) * NX + x, fsdp)
+
+    def down_in(t):
+        return remote(x_ref, o_ref.at[(z + 1 + t) * NX + x], down_send.at[t], down_recv.at[t], (z - 1) * NX + x, fsdp)
+
+    def across(row, src=None):
+        return remote(o_ref.at[row * NX + x] if src is None else src, o_ref.at[row * NX + x], x_send.at[row], x_recv.at[row], z * NX + other, fsdp)
+
+    def across_in(row):
+        return remote(x_ref, o_ref.at[row * NX + other], x_send.at[row], x_recv.at[row], z * NX + other, fsdp)
+
+    own = pltpu.make_async_copy(x_ref, o_ref.at[ctx], own_sem)
+
+    @pl.when(z < nz - 1)
+    def _():
+        up(0).start()
+
+    @pl.when(z > 0)
+    def _():
+        down(0).start()
+
+    across(z, x_ref).start()
+    own.start()
+    for t in range(nz - 1):
+        @pl.when(z - 1 - t >= 0)
+        def _():
+            up_in(t).wait_recv()
+
+            @pl.when(z < nz - 1)
+            def _():
+                up(t + 1).start()
+
+            across(z - 1 - t).start()
+
+        @pl.when(z + 1 + t < nz)
+        def _():
+            down_in(t).wait_recv()
+
+            @pl.when(z > 0)
+            def _():
+                down(t + 1).start()
+
+            across(z + 1 + t).start()
+
+    own.wait()
+    for t in range(nz - 1):
+        @pl.when((z - t >= 0) & (z < nz - 1))
+        def _():
+            up(t).wait_send()
+
+        @pl.when((z + t < nz) & (z > 0))
+        def _():
+            down(t).wait_send()
+
+    for row in range(nz):
+        across(row).wait_send()
+        across_in(row).wait_recv()
+
+
+def gather_rows(block, nz):
+    rows, width = block.shape
+    return pl.pallas_call(
+        functools.partial(gather_kernel, nz),
+        out_shape=jax.ShapeDtypeStruct((nz * NX, rows, width), block.dtype),
+        in_specs=[pl.BlockSpec(memory_space=pltpu.VMEM)],
+        out_specs=pl.BlockSpec(memory_space=pl.ANY),
+        scratch_shapes=[
+            pltpu.SemaphoreType.DMA,
+            pltpu.SemaphoreType.DMA((nz,)),
+            pltpu.SemaphoreType.DMA((nz,)),
+            pltpu.SemaphoreType.DMA((nz,)),
+            pltpu.SemaphoreType.DMA((nz,)),
+            pltpu.SemaphoreType.DMA((nz,)),
+            pltpu.SemaphoreType.DMA((nz,)),
+        ],
+        compiler_params=pltpu.CompilerParams(collective_id=1, has_side_effects=True),
+        name="gather_rows",
+    )(block)
+
+
+def scatter_kernel(nz, p_ref, o_ref, xin, acc, up_in, down_in, x_send, x_recv, up_send, up_recv, down_send, down_recv):
+    ctx, fsdp = lax.axis_index("ctx"), lax.axis_index("fsdp")
+    z, x = ctx // NX, ctx % NX
+    greet_line(nz, z, x, fsdp)
+    other = 1 - x
+
+    def across(row):
+        return remote(p_ref.at[row * NX + other], xin.at[row], x_send.at[row], x_recv.at[row], z * NX + other, fsdp)
+
+    def up(row):
+        return remote(acc.at[row], up_in.at[row], up_send.at[row], up_recv.at[row], (z + 1) * NX + x, fsdp)
+
+    def down(row):
+        return remote(acc.at[row], down_in.at[row], down_send.at[row], down_recv.at[row], (z - 1) * NX + x, fsdp)
+
+    far_up = [nz - 1 - i for i in range(nz)]
+
+    def order(i):
+        low = jnp.where(z == 0, nz - 1 - i, jnp.where(z == nz - 1, i, 0))
+        if nz == 4:
+            mid1 = (3, 0, 2, 1)[i]
+            mid2 = (0, 3, 1, 2)[i]
+            return jnp.where((z == 0) | (z == 3), low, jnp.where(z == 1, mid1, mid2))
+        return low
+
+    for i in range(nz):
+        across(order(i)).start()
+    for i in range(nz):
+        row = order(i)
+        across(row).wait_recv()
+        mine = p_ref[row * NX + x].astype(F32) + xin[row].astype(F32)
+
+        @pl.when(row > z)
+        def _():
+            @pl.when(z == 0)
+            def _():
+                acc[row] = mine.astype(BF)
+
+            @pl.when(z > 0)
+            def _():
+                up(row).wait_recv()
+                acc[row] = (mine + up_in[row].astype(F32)).astype(BF)
+
+            up(row).start()
+
+        @pl.when(row < z)
+        def _():
+            @pl.when(z == nz - 1)
+            def _():
+                acc[row] = mine.astype(BF)
+
+            @pl.when(z < nz - 1)
+            def _():
+                down(row).wait_recv()
+                acc[row] = (mine + down_in[row].astype(F32)).astype(BF)
+
+            down(row).start()
+
+        @pl.when(row == z)
+        def _():
+            o_ref[...] = mine
+
+    @pl.when(z > 0)
+    def _():
+        up(z).wait_recv()
+        o_ref[...] += up_in[z].astype(F32)
+
+    @pl.when(z < nz - 1)
+    def _():
+        down(z).wait_recv()
+        o_ref[...] += down_in[z].astype(F32)
+
+    for row in range(nz):
+        across(row).wait_send()
+
+        @pl.when(row > z)
+        def _():
+            up(row).wait_send()
+
+        @pl.when(row < z)
+        def _():
+            down(row).wait_send()
+
+
+def scatter_rows(parts, nz):
+    _, rows, width = parts.shape
+    return pl.pallas_call(
+        functools.partial(scatter_kernel, nz),
+        out_shape=jax.ShapeDtypeStruct((rows, width), F32),
+        in_specs=[pl.BlockSpec(memory_space=pltpu.VMEM)],
+        out_specs=pl.BlockSpec(memory_space=pltpu.VMEM),
+        scratch_shapes=[
+            pltpu.VMEM((nz, rows, width), BF),
+            pltpu.VMEM((nz, rows, width), BF),
+            pltpu.VMEM((nz, rows, width), BF),
+            pltpu.VMEM((nz, rows, width), BF),
+            pltpu.SemaphoreType.DMA((nz,)),
+            pltpu.SemaphoreType.DMA((nz,)),
+            pltpu.SemaphoreType.DMA((nz,)),
+            pltpu.SemaphoreType.DMA((nz,)),
+            pltpu.SemaphoreType.DMA((nz,)),
+            pltpu.SemaphoreType.DMA((nz,)),
+        ],
+        compiler_params=pltpu.CompilerParams(collective_id=2, has_side_effects=True, vmem_limit_bytes=60 << 20),
+        name="scatter_rows",
+    )(parts)
+
+
+def weights_kernel(nctx, nfs, rows, w_ref, g_ref, o_ref, go_ref, own_sem, p_send, p_recv, y_send, y_recv, c_send, c_recv,
+                   gown_sem, gp_send, gp_recv, gy_send, gy_recv, gc_send, gc_recv):
+    ctx, fsdp = lax.axis_index("ctx"), lax.axis_index("fsdp")
+    y, core = fsdp // NCORE, fsdp % NCORE
+    y_mate = (1 - y) * NCORE + core
+    c_mate = y * NCORE + 1 - core
+    barrier = pltpu.get_barrier_semaphore()
+    for step in range(1, nctx):
+        pl.semaphore_signal(barrier, inc=1, device_id={"ctx": (ctx + step) % nctx, "fsdp": fsdp}, device_id_type=pl.DeviceIdType.MESH)
+    for mate in (y_mate, c_mate):
+        pl.semaphore_signal(barrier, inc=1, device_id={"ctx": ctx, "fsdp": mate}, device_id_type=pl.DeviceIdType.MESH)
+    pl.semaphore_wait(barrier, nctx + 1)
+
+    def place(s, f):
+        return o_ref.at[:, pl.ds(pl.multiple_of((s * nfs + f) * rows, rows), rows), :]
+
+    def gplace(s, f):
+        return go_ref.at[s * nfs + f]
+
+    def direct(step):
+        to = (ctx + step) % nctx
+        return (remote(w_ref.at[to], place(ctx, fsdp), p_send.at[step], p_recv.at[step], to, fsdp),
+                remote(g_ref, gplace(ctx, fsdp), gp_send.at[step], gp_recv.at[step], to, fsdp))
+
+    def direct_in(step):
+        frm = (ctx + nctx - step) % nctx
+        return (remote(w_ref.at[ctx], place(frm, fsdp), p_send.at[step], p_recv.at[step], frm, fsdp),
+                remote(g_ref, gplace(frm, fsdp), gp_send.at[step], gp_recv.at[step], frm, fsdp))
+
+    def to_y(step, own=False):
+        frm = (ctx + nctx - step) % nctx
+        return (remote(w_ref.at[ctx] if own else place(frm, fsdp), place(frm, fsdp), y_send.at[step], y_recv.at[step], ctx, y_mate),
+                remote(g_ref if own else gplace(frm, fsdp), gplace(frm, fsdp), gy_send.at[step], gy_recv.at[step], ctx, y_mate))
+
+    def from_y(step):
+        frm = (ctx + nctx - step) % nctx
+        return (remote(w_ref.at[ctx], place(frm, y_mate), y_send.at[step], y_recv.at[step], ctx, y_mate),
+                remote(g_ref, gplace(frm, y_mate), gy_send.at[step], gy_recv.at[step], ctx, y_mate))
+
+    def to_c(step, f, k, own=False):
+        frm = (ctx + nctx - step) % nctx
+        return (remote(w_ref.at[ctx] if own else place(frm, f), place(frm, f), c_send.at[k, step], c_recv.at[k, step], ctx, c_mate),
+                remote(g_ref if own else gplace(frm, f), gplace(frm, f), gc_send.at[k, step], gc_recv.at[k, step], ctx, c_mate))
+
+    def from_c(step, k):
+        frm = (ctx + nctx - step) % nctx
+        f = (c_mate, (1 - y) * NCORE + 1 - core)[k]
+        return (remote(w_ref.at[ctx], place(frm, f), c_send.at[k, step], c_recv.at[k, step], ctx, c_mate),
+                remote(g_ref, gplace(frm, f), gc_send.at[k, step], gc_recv.at[k, step], ctx, c_mate))
+
+    def start(pair):
+        for copy in pair:
+            copy.start()
+
+    own = (pltpu.make_async_copy(w_ref.at[ctx], place(ctx, fsdp), own_sem),
+           pltpu.make_async_copy(g_ref, gplace(ctx, fsdp), gown_sem))
+    for step in range(1, nctx):
+        start(direct(step))
+    start(to_y(0, own=True))
+    start(to_c(0, fsdp, 0, own=True))
+    start(own)
+    for step in range(1, nctx):
+        for copy in direct_in(step):
+            copy.wait_recv()
+        start(to_y(step))
+        start(to_c(step, fsdp, 0))
+    for step in range(nctx):
+        for copy in from_y(step):
+            copy.wait_recv()
+        start(to_c(step, y_mate, 1))
+    for copy in own:
+        copy.wait()
+    for step in range(nctx):
+        for k in range(2):
+            for copy in from_c(step, k):
+                copy.wait_recv()
+            for copy in to_c(step, fsdp, k):
+                copy.wait_send()
+        for copy in to_y(step):
+            copy.wait_send()
+        if step:
+            for copy in direct(step):
+                copy.wait_send()
+
+
+def spread_weights(send, gains, nfs):
+    nctx, mats, rows, width = send.shape
+    return pl.pallas_call(
+        functools.partial(weights_kernel, nctx, nfs, rows),
+        out_shape=(jax.ShapeDtypeStruct((mats, nctx * nfs * rows, width), send.dtype),
+                   jax.ShapeDtypeStruct((nctx * nfs,) + gains.shape, gains.dtype)),
+        in_specs=[pl.BlockSpec(memory_space=pltpu.VMEM), pl.BlockSpec(memory_space=pltpu.VMEM)],
+        out_specs=(pl.BlockSpec(memory_space=pl.ANY), pl.BlockSpec(memory_space=pl.ANY)),
+        scratch_shapes=[
+            pltpu.SemaphoreType.DMA,
+            pltpu.SemaphoreType.DMA((nctx,)), pltpu.SemaphoreType.DMA((nctx,)),
+            pltpu.SemaphoreType.DMA((nctx,)), pltpu.SemaphoreType.DMA((nctx,)),
+            pltpu.SemaphoreType.DMA((2, nctx)), pltpu.SemaphoreType.DMA((2, nctx)),
+        ] * 2,
+        compiler_params=pltpu.CompilerParams(collective_id=3, has_side_effects=True, vmem_limit_bytes=40 << 20),
+        name="spread_weights",
+    )(send, gains)
+
+
+def grads_kernel(nctx, nfs, rows, g_ref, e_ref, o_ref, eo_ref, cin, yin, half, full, e_cin, e_half, e_yin, e_full,
+                 own_sem, c_send, c_recv, y_send, y_recv, p_send, p_recv, eown_sem, ec_sem, ey_sem, ep_send, ep_recv):
+    ctx, fsdp = lax.axis_index("ctx"), lax.axis_index("fsdp")
+    y, core = fsdp // NCORE, fsdp % NCORE
+    y_mate = (1 - y) * NCORE + core
+    c_mate = y * NCORE + 1 - core
+    mats = g_ref.shape[0]
+    barrier = pltpu.get_barrier_semaphore()
+    for step in range(1, nctx):
+        pl.semaphore_signal(barrier, inc=1, device_id={"ctx": (ctx + step) % nctx, "fsdp": fsdp}, device_id_type=pl.DeviceIdType.MESH)
+    for mate in (y_mate, c_mate):
+        pl.semaphore_signal(barrier, inc=1, device_id={"ctx": ctx, "fsdp": mate}, device_id_type=pl.DeviceIdType.MESH)
+    pl.semaphore_wait(barrier, nctx + 1)
+
+    def span(s, f):
+        return pl.ds(pl.multiple_of((s * nfs + f) * rows, rows), rows)
+
+    def to_c(step, k):
+        s = (ctx + step) % nctx
+        f = (1 - y if k == 0 else y) * NCORE + 1 - core
+        return remote(g_ref.at[:, span(s, f), :], cin.at[k, step], c_send.at[k, step], c_recv.at[k, step], ctx, c_mate)
+
+    def to_y(step):
+        return remote(half.at[step], yin.at[step], y_send.at[step], y_recv.at[step], ctx, y_mate)
+
+    def out(step):
+        s = (ctx + step) % nctx
+        return remote(full.at[step], o_ref.at[ctx], p_send.at[step], p_recv.at[step], s, fsdp)
+
+    def out_in(step):
+        s = (ctx + nctx - step) % nctx
+        return remote(full.at[step], o_ref.at[s], p_send.at[step], p_recv.at[step], s, fsdp)
+
+    e_to_c = remote(e_ref.at[1 - core], e_cin, ec_sem.at[0], ec_sem.at[1], ctx, c_mate)
+    e_to_y = remote(e_half.at[1 - y], e_yin, ey_sem.at[0], ey_sem.at[1], ctx, y_mate)
+
+    def e_out(step):
+        s = (ctx + step) % nctx
+        return remote(e_full.at[s], eo_ref.at[ctx], ep_send.at[step], ep_recv.at[step], s, fsdp)
+
+    def e_out_in(step):
+        s = (ctx + nctx - step) % nctx
+        return remote(e_full.at[s], eo_ref.at[s], ep_send.at[step], ep_recv.at[step], s, fsdp)
+
+    e_to_c.start()
+    for step in range(nctx):
+        to_c((step + 1) % nctx, 0).start()
+    for step in range(nctx):
+        to_c((step + 1) % nctx, 1).start()
+    e_to_c.wait_recv()
+    e_half[...] = e_ref[core] + e_cin[...]
+    e_to_y.start()
+    e_own = pltpu.make_async_copy(e_full.at[ctx], eo_ref.at[ctx], eown_sem)
+    own = pltpu.make_async_copy(full.at[0], o_ref.at[ctx], own_sem)
+
+    def first(i, _):
+        step = (i + 1) % nctx
+        s = (ctx + step) % nctx
+        to_c(step, 0).wait_recv()
+
+        def one(m, _):
+            half[step, m] = (g_ref[m, span(s, y_mate), :].astype(F32) + cin[0, step, m].astype(F32)).astype(BF)
+            return 0
+
+        lax.fori_loop(0, mats, one, 0)
+        to_y(step).start()
+        return 0
+
+    lax.fori_loop(0, nctx, first, 0)
+    e_to_y.wait_recv()
+    e_full[...] = e_half[y] + e_yin[...]
+    e_own.start()
+    for step in range(1, nctx):
+        e_out(step).start()
+
+    def second(i, _):
+        step = (i + 1) % nctx
+        s = (ctx + step) % nctx
+        to_c(step, 1).wait_recv()
+        to_y(step).wait_recv()
+
+        def one(m, _):
+            full[step, m] = (g_ref[m, span(s, fsdp), :].astype(F32) + cin[1, step, m].astype(F32) + yin[step, m].astype(F32)).astype(BF)
+            return 0
+
+        lax.fori_loop(0, mats, one, 0)
+
+        @pl.when(step > 0)
+        def _():
+            out(step).start()
+
+        return 0
+
+    lax.fori_loop(0, nctx, second, 0)
+    own.start()
+    for step in range(nctx):
+        for k in range(2):
+            to_c(step, k).wait_send()
+        to_y(step).wait_send()
+        if step:
+            out(step).wait_send()
+            out_in(step).wait_recv()
+            e_out(step).wait_send()
+            e_out_in(step).wait_recv()
+    e_to_c.wait_send()
+    e_to_y.wait_send()
+    e_own.wait()
+    own.wait()
+
+
+def collect_grads(grads, extra, nctx, nfs):
+    mats, total, width = grads.shape
+    rows = total // (nctx * nfs)
+    blk = (mats, rows, width)
+    return pl.pallas_call(
+        functools.partial(grads_kernel, nctx, nfs, rows),
+        out_shape=(jax.ShapeDtypeStruct((nctx,) + blk, BF), jax.ShapeDtypeStruct((nctx, 8, 128), F32)),
+        in_specs=[pl.BlockSpec(memory_space=pltpu.VMEM), pl.BlockSpec(memory_space=pltpu.VMEM)],
+        out_specs=(pl.BlockSpec(memory_space=pl.ANY), pl.BlockSpec(memory_space=pl.ANY)),
+        scratch_shapes=[
+            pltpu.VMEM((2, nctx) + blk, BF),
+            pltpu.VMEM((nctx,) + blk, BF),
+            pltpu.VMEM((nctx,) + blk, BF),
+            pltpu.VMEM((nctx,) + blk, BF),
+            pltpu.VMEM((2, nctx, 8, 128), F32),
+            pltpu.VMEM((2, nctx, 8, 128), F32),
+            pltpu.VMEM((nctx, 8, 128), F32),
+            pltpu.VMEM((nctx, 8, 128), F32),
+            pltpu.SemaphoreType.DMA,
+            pltpu.SemaphoreType.DMA((2, nctx)), pltpu.SemaphoreType.DMA((2, nctx)),
+            pltpu.SemaphoreType.DMA((nctx,)), pltpu.SemaphoreType.DMA((nctx,)),
+            pltpu.SemaphoreType.DMA((nctx,)), pltpu.SemaphoreType.DMA((nctx,)),
+            pltpu.SemaphoreType.DMA,
+            pltpu.SemaphoreType.DMA((2,)), pltpu.SemaphoreType.DMA((2,)),
+            pltpu.SemaphoreType.DMA((nctx,)), pltpu.SemaphoreType.DMA((nctx,)),
+        ],
+        compiler_params=pltpu.CompilerParams(collective_id=4, has_side_effects=True, vmem_limit_bytes=60 << 20),
+        name="collect_grads",
+    )(grads, extra)
+
+
+def rope_tables(places):
+    half_dim = HEAD_DIM // 2
+    freq_steps = jnp.arange(half_dim, dtype=jnp.float32)
+    inverse = jnp.exp(freq_steps * (-2.0 * math.log(10000.0) / HEAD_DIM))
+    angles = places[:, None] * inverse[None, :]
+    return jnp.cos(angles), jnp.sin(angles)
+
+
+def turn(values, cos_part, sin_part):
+    half_dim = HEAD_DIM // 2
+    first_half = values[..., :half_dim]
+    second_half = values[..., half_dim:]
+    cos_part, sin_part = cos_part[:, None, :], sin_part[:, None, :]
+    return jnp.concatenate(
+        [first_half * cos_part - second_half * sin_part, second_half * cos_part + first_half * sin_part],
+        axis=-1,
+    )
+
+
+def dot(left, right, dims):
+    return lax.dot_general(left, right, (dims, ((), ())), preferred_element_type=jnp.float32)
+
+
+NN = ((1,), (0,))
+NT = ((1,), (1,))
+TN = ((0,), (0,))
+
+
+def pack_weights(master_set, layer, nctx):
+    query_weight, key_weight, value_weight, out_weight, attn_gain, moe_gain, gate_weight, up_weight, down_weight = master_set
+    rows = query_weight.shape[1]
+
+    def columns(master):
+        low = master[layer].astype(BF).reshape(rows, nctx, -1)
+        return low.transpose(1, 0, 2)
+
+    attn = jnp.concatenate(
+        [columns(query_weight), columns(key_weight), columns(value_weight), columns(out_weight)], axis=-1
+    )
+
+    def experts(master):
+        low = master[layer].astype(BF)
+        return low.reshape(nctx, -1, rows, low.shape[-1])
+
+    send = jnp.concatenate(
+        [attn[:, None], experts(gate_weight), experts(up_weight), experts(down_weight)], axis=1
+    )
+    gains = jnp.stack([attn_gain[layer], moe_gain[layer]]).astype(BF).astype(F32)
+    gains = jnp.pad(gains, ((0, 6), (0, 128 - rows)))
+    return send, gains
+
+
+def norm_back(values, gain, grad):
+    scale = lax.rsqrt(jnp.mean(values * values, axis=-1, keepdims=True) + EPSILON)
+    unit = values * scale
+    grad_gain = jnp.sum(grad * unit, axis=0)
+    pulled = grad * gain
+    return scale * (pulled - unit * jnp.mean(pulled * unit, axis=-1, keepdims=True)), grad_gain
+
+
+def fast_body(nctx, nfs, *args):
+    (tokens, cotangent, lengths, tile_order, routes, gates), master_set = args[:6], args[6:]
+    nz = nctx // NX
+    rows_here, model_width = tokens.shape[1], tokens.shape[2]
+    group_rows = rows_here * nctx
+    ctx = lax.axis_index("ctx")
+    seg_all, pos_all = layout(lengths[0], tile_order[0], group_rows)
+    visible = (seg_all[:, None] == seg_all[None, :]) & (pos_all[None, :] <= pos_all[:, None])
+    cos_part, sin_part = rope_tables(pos_all.astype(jnp.float32))
+    score_scale = HEAD_DIM ** (-0.5)
+    q_width = 3 * HEAD_DIM
+    kv_at, v_at, o_at = q_width, q_width + HEAD_DIM, q_width + 2 * HEAD_DIM
+
+    expert_ids = jnp.arange(EXPERTS, dtype=jnp.int32)
+    table = jnp.sum(
+        jnp.where(routes[:, 0, :, :, None] == expert_ids, gates[:, 0, :, :, None], 0.0), axis=-2
+    )
+    table_all = lax.all_gather(
+        table.transpose(1, 0, 2).reshape(rows_here, LAYERS * EXPERTS), "ctx", axis=0, tiled=True
+    ).reshape(group_rows, LAYERS, EXPERTS // 2, 2)
+    table_mine = lax.dynamic_index_in_dim(table_all, ctx, 2, keepdims=False)
+
+    fetched = []
+    for layer in range(LAYERS):
+        send, gains = pack_weights(master_set, layer, nctx)
+        mats, gain_all = spread_weights(send, gains, nfs)
+        rows = send.shape[2]
+        fetched.append((mats, gain_all[:, 0, :rows].reshape(-1), gain_all[:, 1, :rows].reshape(-1)))
+
+    hidden = tokens[0].astype(jnp.float32)
+    records = []
+    for layer in range(LAYERS):
+        mats, attn_gain, moe_gain = fetched[layer]
+        attn = mats[0]
+        normed = rms_norm(hidden, attn_gain).astype(BF)
+        normed_all = gather_rows(normed, nz).reshape(group_rows, model_width)
+        proj = dot(normed_all, attn[:, :o_at], NN)
+        turned = turn(proj[:, :v_at].reshape(group_rows, 4, HEAD_DIM), cos_part, sin_part).astype(BF)
+        queries, keys = turned[:, :3], turned[:, 3]
+        values = proj[:, v_at:].astype(BF)
+        raw = jnp.einsum("qhd,kd->hqk", queries, keys, preferred_element_type=jnp.float32) * score_scale
+        raw = jnp.where(visible[None], raw, NEGATIVE)
+        peak = jnp.max(raw, axis=-1, keepdims=True)
+        powers = jnp.exp(raw - peak)
+        probs = powers / jnp.sum(powers, axis=-1, keepdims=True)
+        attended = jnp.einsum("hqk,kd->qhd", probs.astype(BF), values, preferred_element_type=jnp.float32)
+        attended = attended.reshape(group_rows, q_width).astype(BF)
+        part = dot(attended, attn[:, o_at:], NT).astype(BF)
+        middle = hidden + scatter_rows(part.reshape(nctx, rows_here, model_width), nz)
+
+        moe_in = rms_norm(middle, moe_gain).astype(BF)
+        moe_all = gather_rows(moe_in, nz).reshape(group_rows, model_width)
+        acts = []
+        total = 0.0
+        for e in range(2):
+            gate_act = dot(moe_all, mats[1 + e], NN)
+            up_act = dot(moe_all, mats[3 + e], NN)
+            inner = (table_mine[:, layer, e][:, None] * (jax.nn.silu(gate_act) * up_act)).astype(BF)
+            acts.append((gate_act, up_act, inner))
+            total = total + dot(inner, mats[5 + e], NT)
+        moved = scatter_rows(total.astype(BF).reshape(nctx, rows_here, model_width), nz)
+        records.append((hidden, normed_all, queries, keys, values, probs, attended, middle, moe_all, acts))
+        hidden = middle + moved
+
+    output = hidden.astype(BF)
+    grad = cotangent[0].astype(jnp.float32)
+    collected = [None] * LAYERS
+    for layer in reversed(range(LAYERS)):
+        mats, attn_gain, moe_gain = fetched[layer]
+        attn = mats[0]
+        hidden, normed_all, queries, keys, values, probs, attended, middle, moe_all, acts = records[layer]
+        grad_all = gather_rows(grad.astype(BF), nz).reshape(group_rows, model_width)
+        grad_gate, grad_up, grad_down = [], [], []
+        total = 0.0
+        for e in range(2):
+            gate_act, up_act, inner = acts[e]
+            grad_down.append(dot(grad_all, inner, TN).astype(BF))
+            grad_inner = table_mine[:, layer, e][:, None] * dot(grad_all, mats[5 + e], NN)
+            sigmoid = jax.nn.sigmoid(gate_act)
+            d_gate = (grad_inner * up_act * sigmoid * (1.0 + gate_act * (1.0 - sigmoid))).astype(BF)
+            d_up = (grad_inner * gate_act * sigmoid).astype(BF)
+            grad_gate.append(dot(moe_all, d_gate, TN).astype(BF))
+            grad_up.append(dot(moe_all, d_up, TN).astype(BF))
+            total = total + dot(d_gate, mats[1 + e], NT) + dot(d_up, mats[3 + e], NT)
+        grad_moe_in = scatter_rows(total.astype(BF).reshape(nctx, rows_here, model_width), nz)
+        through, grad_moe_gain = norm_back(middle, moe_gain, grad_moe_in)
+        grad_middle = grad + through
+
+        middle_all = gather_rows(grad_middle.astype(BF), nz).reshape(group_rows, model_width)
+        grad_out = dot(middle_all, attended, TN).astype(BF)
+        grad_att = dot(middle_all, attn[:, o_at:], NN).astype(BF).reshape(group_rows, 3, HEAD_DIM)
+        dp = jnp.einsum("qhd,kd->hqk", grad_att, values, preferred_element_type=jnp.float32)
+        delta = jnp.sum(probs * dp, axis=-1, keepdims=True)
+        d_scores = (probs * (dp - delta)).astype(BF)
+        dq = jnp.einsum("hqk,kd->qhd", d_scores, keys, preferred_element_type=jnp.float32) * score_scale
+        dk = jnp.einsum("hqk,qhd->kd", d_scores, queries, preferred_element_type=jnp.float32) * score_scale
+        dv = jnp.einsum("hqk,qhd->kd", probs.astype(BF), grad_att, preferred_element_type=jnp.float32)
+        back = turn(jnp.concatenate([dq, dk[:, None]], axis=1), cos_part, -sin_part)
+        d_proj = jnp.concatenate([back.reshape(group_rows, v_at), dv], axis=1).astype(BF)
+        grad_proj = dot(normed_all, d_proj, TN).astype(BF)
+        part = dot(d_proj, attn[:, :o_at], NT).astype(BF)
+        grad_normed = scatter_rows(part.reshape(nctx, rows_here, model_width), nz)
+        through, grad_attn_gain = norm_back(hidden, attn_gain, grad_normed)
+        grad = grad_middle + through
+
+        grads = jnp.stack([jnp.concatenate([grad_proj, grad_out], axis=1)] + grad_gate + grad_up + grad_down)
+        rows = model_width // (nctx * nfs)
+        extra = jnp.stack([grad_attn_gain, grad_moe_gain]).reshape(2, nctx, nfs // NCORE, NCORE, rows)
+        extra = jnp.pad(extra.transpose(3, 2, 1, 0, 4), ((0, 0), (0, 0), (0, 0), (0, 6), (0, 128 - rows)))
+        collected[layer] = collect_grads(grads, extra, nctx, nfs)
+
+    def attn_part(low, high):
+        return jnp.stack(
+            [
+                c[0][:, 0, :, low:high].transpose(1, 0, 2).reshape(c[0].shape[2], -1).astype(F32)
+                for c in collected
+            ]
+        )
+
+    def expert_part(first):
+        return jnp.stack(
+            [
+                c[0][:, first : first + 2].reshape((EXPERTS,) + c[0].shape[2:]).astype(F32)
+                for c in collected
+            ]
+        )
+
+    def gain_part(kind):
+        return jnp.stack([jnp.sum(c[1][:, kind, :rows], axis=0) for c in collected])
+
+    return (
+        output[None],
+        grad[None],
+        attn_part(0, kv_at),
+        attn_part(kv_at, v_at),
+        attn_part(v_at, o_at),
+        attn_part(o_at, o_at + q_width),
+        gain_part(0),
+        gain_part(1),
+        expert_part(1),
+        expert_part(3),
+        expert_part(5),
+    )
+
+
 def solution(mesh):
     placed = (
         P("fsdp", "ctx", None),
@@ -677,8 +1365,10 @@
         P(None, None, ("ctx", "fsdp"), None),
         P(None, None, ("ctx", "fsdp"), None),
     )
+    nctx, nfs = mesh.shape["ctx"], mesh.shape["fsdp"]
+    chosen = partial(fast_body, nctx, nfs) if (nctx, nfs) == (8, 4) else body
     return jax.shard_map(
-        body,
+        chosen,
         mesh=mesh,
         in_specs=placed,
         out_specs=(

time: 4450 us -> 1310 us (0.29)
  waiting for transfers between devices: 2670 us -> 0 us
  Pallas kernels: 0 us -> 939 us
  blocking collectives: 636 us -> 28.9 us
  local copies, waits for them, and re-layouts: 491 us -> 40 us
  other arithmetic: 201 us -> 64.2 us
  starting transfers between devices: 91.7 us -> 0 us
  matrix products: 313 us -> 232 us
    all_to_all x14 -> x0, waiting for transfers between devices: 995 us -> none  [the longest x4 602 us: send_back(): lax.all_to_all(parts.astype(jnp.bfloat16), 'ctx', split_axis=1, concat_ax...]
    pallas_call x0 -> x20, Pallas kernels: none -> 939 us  [the longest x8 299 us: scatter_rows(): pl.pallas_call(functools.partial(scatter_kernel, nz), out_shape=jax.Shape...]
    reduce_scatter x14 -> x0, waiting for transfers between devices: 899 us -> none  [the longest x2 280 us: layer_backward(): lax.psum_scatter(grad_out_full, ('ctx', 'fsdp'), scatter_dimension=0, til...]
    all_gather x18 -> x0, waiting for transfers between devices: 661 us -> none  [the longest x2 285 us: fetch_layer(): lax.all_gather(query_weight[layer_index].astype(jnp.bfloat16), ('ctx', 'f...]
    all_to_all x6 -> x0, blocking collectives: 551 us -> none  [the longest x1 172 us: send_out(): return lax.all_to_all(slots, 'ctx', split_axis=0, concat_axis=1, tiled=True)]
    convert_element_type x19 -> x32, local copies, waits for them, and re-layouts: 180 us -> 12.9 us  [the longest x20 8.68 us: attn_part(): c[0][:, 0, :, low:high].transpose(1, 0, 2).reshape(c[0].shape[2], -1)]
    unnamed x40 -> x0, waiting for transfers between devices: 114 us -> none
    dot_general x78 -> x58, matrix products: 313 us -> 215 us  [the longest x48 170 us: dot(): lax.dot_general(left, right, (dims, ((), ())), preferred_element_type=jnp...]
  transfers between devices with their start and end apart: 50 -> 0, of which waited for: 35 -> 0; matrix products, arithmetic and copies ran while one was open for 16% -> 0% of each run, Pallas kernels for 0% -> 0%
where the time goes in v1:
time: 1310 us
  Pallas kernels  939 us (72%)
  matrix products  232 us (18%)
  other arithmetic  64.2 us (5%)
  local copies, waits for them, and re-layouts  40 us (3%)
  blocking collectives  28.9 us (2%)
    pallas_call x8, Pallas kernels, scatter_rows(): pl.pallas_call(functools.partial(scatter_kernel, nz), out_shape=jax.Shape...  299 us
    pallas_call x8, Pallas kernels, gather_rows(): pl.pallas_call(functools.partial(gather_kernel, nz), out_shape=jax.ShapeD...  266 us
    pallas_call x2, Pallas kernels, collect_grads(): pl.pallas_call(functools.partial(grads_kernel, nctx, nfs, rows), out_shap...  203 us
    pallas_call x2, Pallas kernels, spread_weights(): pl.pallas_call(functools.partial(weights_kernel, nctx, nfs, rows), out_sh...  171 us
    dot_general x48, matrix products, dot(): lax.dot_general(left, right, (dims, ((), ())), preferred_element_type=jnp...  170 us
    all_gather x1, blocking collectives, fast_body(): lax.all_gather(table.transpose(1, 0, 2).reshape(rows_here, LAYERS * EXPER...  28.9 us

profile of v1, /device:TPU:11, one launch (start us, length us, event | category | flops | bytes accessed | tf_op | source)
XLA Modules:
  0.0 1306.9 jit_solution(3830811407983091060)
XLA Ops:
  12.9 83.3 %spread_weights.3 = (bf16[7,1536,512]{2,1,0:T(8,128)(2,1)S(1)}, f32[32,8,128]{2,1,0:T(8,128)S(1)}) custom-call(bf16[8,7,48,512]{3,2,1,0:T(8,128)(2,1)S(1)} %pad_maximum_fusion.1.w_ref, f32[8,128]{1,0:T(8,128)S(1)} %get-tuple-element.130.g_ref), custom_call_target="tpu_custom_call" | custom-call | tf_op jit(solution)/shard_map/spread_weights/pallas_call | solution.py:987
  96.3 4.1 copy-done
  101.7 45.6 %gather_rows.12 = bf16[8,128,1536]{2,1,0:T(8,128)(2,1)} custom-call(bf16[128,1536]{1,0:T(8,128)(2,1)} %bitcast.486), custom_call_target="tpu_custom_call" | custom-call | tf_op jit(solution)/shard_map/gather_rows/pallas_call | solution.py:773
  147.3 5.5 fusion.60
  152.8 28.9 %all_gather.3 = f32[1024,32]{0,1:T(8,128)S(1)} all-gather(f32[128,32]{0,1:T(8,128)S(1)} %bitcast.537), channel_id=1, replica_groups=mesh['ctx'=8,'fsdp'=4] {'ctx'}, dimensions={0}, use_global_device_ids=true | all-gather | bytes 147456 | tf_op jit(solution)/shard_map/all_gather | solution.py:1222
  183.8 87.6 %spread_weights.2 = (bf16[7,1536,512]{2,1,0:T(8,128)(2,1)S(1)}, f32[32,8,128]{2,1,0:T(8,128)S(1)}) custom-call(bf16[8,7,48,512]{3,2,1,0:T(8,128)(2,1)S(1)} %pad_maximum_fusion.w_ref, f32[8,128]{1,0:T(8,128)S(1)} %get-tuple-element.129.g_ref), custom_call_target="tpu_custom_call" | custom-call | tf_op jit(solution)/shard_map/spread_weights/pallas_call | solution.py:987
  271.3 4.1 copy-done.1
  276.7 43.3 %gather_rows.8 = bf16[8,128,1536]{2,1,0:T(8,128)(2,1)} custom-call(bf16[128,1536]{1,0:T(8,128)(2,1)} %fusion.166.x_ref), custom_call_target="tpu_custom_call" | custom-call | tf_op jit(solution)/shard_map/gather_rows/pallas_call | solution.py:773
  327.6 8.5 fusion.238
  336.2 5.9 fusion.134
  345.1 45.4 %scatter_rows.8 = f32[128,1536]{1,0:T(8,128)} custom-call(bf16[8,128,1536]{2,1,0:T(8,128)(2,1)} %bitcast.482), custom_call_target="tpu_custom_call" | custom-call | tf_op jit(solution)/shard_map/scatter_rows/pallas_call | solution.py:878
  392.9 32.9 %gather_rows.9 = bf16[8,128,1536]{2,1,0:T(8,128)(2,1)} custom-call(bf16[128,1536]{1,0:T(8,128)(2,1)} %multiply_convert_fusion.10.x_ref), custom_call_target="tpu_custom_call" | custom-call | tf_op jit(solution)/shard_map/gather_rows/pallas_call | solution.py:773
  425.8 4.3 fusion.102
  430.2 5.5 multiply_convert_fusion.7
  439.3 3.4 multiply_convert_fusion.6
  442.7 3.5 add_convert_fusion.3
  446.3 37.3 %scatter_rows.9 = f32[128,1536]{1,0:T(8,128)} custom-call(bf16[8,128,1536]{2,1,0:T(8,128)(2,1)} %bitcast.481), custom_call_target="tpu_custom_call" | custom-call | tf_op jit(solution)/shard_map/scatter_rows/pallas_call | solution.py:878
  486.7 31.0 %gather_rows.10 = bf16[8,128,1536]{2,1,0:T(8,128)(2,1)} custom-call(bf16[128,1536]{1,0:T(8,128)(2,1)} %multiply_convert_fusion.9.x_ref), custom_call_target="tpu_custom_call" | custom-call | tf_op jit(solution)/shard_map/gather_rows/pallas_call | solution.py:773
  517.7 3.1 fusion.161
  521.9 8.6 fusion.239
  530.5 5.9 fusion.137
  539.4 40.4 %scatter_rows.10 = f32[128,1536]{1,0:T(8,128)} custom-call(bf16[8,128,1536]{2,1,0:T(8,128)(2,1)} %bitcast.483), custom_call_target="tpu_custom_call" | custom-call | tf_op jit(solution)/shard_map/scatter_rows/pallas_call | solution.py:878
  582.2 27.7 %gather_rows.11 = bf16[8,128,1536]{2,1,0:T(8,128)(2,1)} custom-call(bf16[128,1536]{1,0:T(8,128)(2,1)} %multiply_convert_fusion.8.x_ref), custom_call_target="tpu_custom_call" | custom-call | tf_op jit(solution)/shard_map/gather_rows/pallas_call | solution.py:773
  609.9 4.3 fusion.64
  614.2 5.4 fusion.52
  625.9 3.8 fusion.57
  629.7 4.5 fusion.78
  634.2 4.5 fusion.74
  638.6 8.6 add_convert_fusion.1
  647.2 41.5 %scatter_rows.12 = f32[128,1536]{1,0:T(8,128)} custom-call(bf16[8,128,1536]{2,1,0:T(8,128)(2,1)} %bitcast.479), custom_call_target="tpu_custom_call" | custom-call | tf_op jit(solution)/shard_map/scatter_rows/pallas_call | solution.py:878
  692.9 29.0 %gather_rows.13 = bf16[8,128,1536]{2,1,0:T(8,128)(2,1)} custom-call(bf16[128,1536]{1,0:T(8,128)(2,1)} %fusion.221.x_ref), custom_call_target="tpu_custom_call" | custom-call | tf_op jit(solution)/shard_map/gather_rows/pallas_call | solution.py:773
  721.9 3.4 convolution_convert_fusion.21
  725.4 6.7 fusion.154
  732.4 6.6 fusion.5
  739.0 6.7 fusion.7
  749.2 3.5 convolution_convert_fusion.3
  752.7 33.1 %scatter_rows.13 = f32[128,1536]{1,0:T(8,128)} custom-call(bf16[8,128,1536]{2,1,0:T(8,128)(2,1)} %bitcast.521), custom_call_target="tpu_custom_call" | custom-call | tf_op jit(solution)/shard_map/scatter_rows/pallas_call | solution.py:878
  787.9 3.3 fusion.72
  791.2 4.9 add_convert_fusion.2
  796.2 28.4 %scatter_rows.11 = f32[128,1536]{1,0:T(8,128)} custom-call(bf16[8,128,1536]{2,1,0:T(8,128)(2,1)} %bitcast.480), custom_call_target="tpu_custom_call" | custom-call | tf_op jit(solution)/shard_map/scatter_rows/pallas_call | solution.py:878
  824.6 3.6 fusion.223
  828.2 28.9 %gather_rows.14 = bf16[8,128,1536]{2,1,0:T(8,128)(2,1)} custom-call(bf16[128,1536]{1,0:T(8,128)(2,1)} %get-tuple-element.45.x_ref), custom_call_target="tpu_custom_call" | custom-call | tf_op jit(solution)/shard_map/gather_rows/pallas_call | solution.py:773
  857.1 6.2 multiply_convert_fusion
  869.7 4.4 fusion.100
  874.1 4.5 fusion.96
  878.6 8.6 add_convert_fusion
  887.2 37.4 %scatter_rows.14 = f32[128,1536]{1,0:T(8,128)} custom-call(bf16[8,128,1536]{2,1,0:T(8,128)(2,1)} %bitcast.478), custom_call_target="tpu_custom_call" | custom-call | tf_op jit(solution)/shard_map/scatter_rows/pallas_call | solution.py:878
  929.1 27.8 %gather_rows.15 = bf16[8,128,1536]{2,1,0:T(8,128)(2,1)} custom-call(bf16[128,1536]{1,0:T(8,128)(2,1)} %get-tuple-element.43.x_ref), custom_call_target="tpu_custom_call" | custom-call | tf_op jit(solution)/shard_map/gather_rows/pallas_call | solution.py:773
  956.9 3.3 convolution_convert_fusion.20
  960.3 7.4 fusion.157
  967.7 5.9 fusion.2
  973.6 3.4 fusion.4
  980.6 3.5 convolution_convert_fusion.2
  984.2 35.6 %scatter_rows.15 = f32[128,1536]{1,0:T(8,128)} custom-call(bf16[8,128,1536]{2,1,0:T(8,128)(2,1)} %bitcast.522), custom_call_target="tpu_custom_call" | custom-call | tf_op jit(solution)/shard_map/scatter_rows/pallas_call | solution.py:878
  1025.5 3.3 convolution_convert_fusion.16
  1032.0 4.3 fusion.37
  1042.3 3.1 fusion.43
  1045.4 3.0 fusion.45
  1048.4 3.0 fusion.47.g_ref
  1052.4 114.6 %collect_grads.3 = (bf16[8,7,48,512]{3,2,1,0:T(8,128)(2,1)}, f32[8,8,128]{2,1,0:T(8,128)}) custom-call(bf16[7,1536,512]{2,1,0:T(8,128)(2,1)} %fusion.47.g_ref, f32[2,2,8,8,128]{4,3,2,1,0:T(8,128)} %pad.23.e_ref), custom_call_target="tpu_custom_call" | custom-call | tf_op jit(solution)/shard_map/collect_grads/pallas_call | solution.py:1118
  1174.3 3.3 convolution_convert_fusion.17
  1180.8 4.3 fusion.25
  1191.1 3.1 fusion.31
  1201.2 88.0 %collect_grads.2 = (bf16[8,7,48,512]{3,2,1,0:T(8,128)(2,1)}, f32[8,8,128]{2,1,0:T(8,128)}) custom-call(bf16[7,1536,512]{2,1,0:T(8,128)(2,1)} %fusion.35.g_ref, f32[2,2,8,8,128]{4,3,2,1,0:T(8,128)} %pad.22.e_ref), custom_call_target="tpu_custom_call" | custom-call | tf_op jit(solution)/shard_map/collect_grads/pallas_call | solution.py:1118
  (433 shorter events, 129.6 us)
Async XLA Ops:
  147.3 5.5 copy-start.75
  147.3 5.5 copy-start.76
  147.3 35.1 %copy-start.59 = (bf16[1,48,1536]{2,1,0:T(8,128)(2,1)S(1)}, bf16[1,48,1536]{2,1,0:T(8,128)(2,1)}, u32[]{:S(2)}) copy-start(bf16[1,48,1536]{2,1,0:T(8,128)(2,1)} %get-tuple-element.97) | copy-start | bytes 442372
  183.4 92.3 %copy-start.7 = (bf16[1,128,1536]{2,1,0:T(8,128)(2,1)S(1)}, bf16[1,128,1536]{2,1,0:T(8,128)(2,1)}, u32[]{:S(2)}) copy-start(bf16[1,128,1536]{2,1,0:T(8,128)(2,1)} %param.15) | copy-start | bytes 1179652
  275.6 44.4 %copy-start.64 = (f32[1536]{0:T(1024)}, f32[1536]{0:T(1024)S(1)}, u32[]{:S(2)}) copy-start(f32[1536]{0:T(1024)S(1)} %mul.577) | copy-start | bytes 18436
  275.8 45.9 %copy-start.81 = (f32[128]{0:T(128)}, f32[128]{0:T(128)S(1)}, u32[]{:S(2)}) copy-start(f32[128]{0:T(128)S(1)} %add_rsqrt_fusion.3) | copy-start | bytes 1540
  322.4 19.7 %copy-start.9 = (bf16[1536,512]{1,0:T(8,128)(2,1)}, bf16[1536,512]{1,0:T(8,128)(2,1)S(1)}, u32[]{:S(2)}) copy-start(bf16[1536,512]{1,0:T(8,128)(2,1)S(1)} %slice_bitcast_fusion.1) | copy-start | bytes 4718596
  327.4 421.5 %copy-start.15 = (f32[1024,32]{0,1:T(8,128)}, f32[1024,32]{0,1:T(8,128)S(1)}, u32[]{:S(2)}) copy-start(f32[1024,32]{0,1:T(8,128)S(1)} %get-tuple-element.108) | copy-start | bytes 393220
  327.6 8.6 copy-start.31
  327.6 8.6 copy-start.33
  327.6 8.6 copy-start.60
  336.2 5.9 copy-start.73
  342.1 48.4 %copy-start.39 = (bf16[64,3,1024]{2,0,1:T(8,128)(2,1)}, bf16[64,3,1024]{2,0,1:T(8,128)(2,1)S(1)}, u32[]{:S(2)}) copy-start(bf16[64,3,1024]{2,0,1:T(8,128)(2,1)S(1)} %fusion.134) | copy-start | bytes 1179652
  391.9 91.7 %copy-start.2 = (f32[128,1536]{1,0:T(8,128)}, f32[128,1536]{1,0:T(8,128)S(1)}, u32[]{:S(2)}) copy-start(f32[128,1536]{1,0:T(8,128)S(1)} %get-tuple-element.52) | copy-start | bytes 2359300
  392.0 38.1 %copy-start.66 = (f32[1536]{0:T(1024)}, f32[1536]{0:T(1024)S(1)}, u32[]{:S(2)}) copy-start(f32[1536]{0:T(1024)S(1)} %mul.599) | copy-start | bytes 18436
  392.0 38.1 %copy-start.79 = (f32[128]{0:T(128)}, f32[128]{0:T(128)S(1)}, u32[]{:S(2)}) copy-start(f32[128]{0:T(128)S(1)} %add_rsqrt_fusion.2) | copy-start | bytes 1540
  425.8 9.8 slice-start.3
  430.1 5.5 copy-start.112
  483.6 34.1 %copy-start.12 = (bf16[1536,512]{1,0:T(8,128)(2,1)S(1)}, bf16[1536,512]{1,0:T(8,128)(2,1)}, u32[]{:S(2)}) copy-start(bf16[1536,512]{1,0:T(8,128)(2,1)} %slice_bitcast_fusion) | copy-start | bytes 4718596
  485.8 35.1 %copy-start.83 = (f32[128]{0:T(128)}, f32[128]{0:T(128)S(1)}, u32[]{:S(2)}) copy-start(f32[128]{0:T(128)S(1)} %add_rsqrt_fusion.1) | copy-start | bytes 1540
  521.9 8.6 copy-start.35
  521.9 8.6 copy-start.37
  539.4 41.7 %copy-start.68 = (f32[32,48]{1,0:T(8,128)S(1)}, f32[32,48]{1,0:T(8,128)}, u32[]{:S(2)}) copy-start(f32[32,48]{1,0:T(8,128)} %get-tuple-element.35) | copy-start | bytes 18436
  581.2 109.5 %copy-start.4 = (f32[128,1536]{1,0:T(8,128)}, f32[128,1536]{1,0:T(8,128)S(1)}, u32[]{:S(2)}) copy-start(f32[128,1536]{1,0:T(8,128)S(1)} %get-tuple-element.48) | copy-start | bytes 2359300
  581.3 109.4 %copy-start.77 = (f32[128]{0:T(128)}, f32[128]{0:T(128)S(1)}, u32[]{:S(2)}) copy-start(f32[128]{0:T(128)S(1)} %add_rsqrt_fusion) | copy-start | bytes 1540
  609.9 9.7 slice-start
  619.6 19.0 %copy-start.49 = (bf16[1024,512]{1,0:T(8,128)(2,1)}, bf16[1024,512]{1,0:T(8,128)(2,1)S(1)}, u32[]{:S(2)}) copy-start(bf16[1024,512]{1,0:T(8,128)(2,1)S(1)} %get-tuple-element.59) | copy-start | bytes 3145732
  647.2 43.5 %copy-start.13 = (bf16[1,128,1536]{2,1,0:T(8,128)(2,1)S(1)}, bf16[1,128,1536]{2,1,0:T(8,128)(2,1)}, u32[]{:S(2)}) copy-start(bf16[1,128,1536]{2,1,0:T(8,128)(2,1)} %param.16) | copy-start | bytes 1179652
  690.7 34.7 %copy-start.91 = (f32[128]{0:T(128)}, f32[128]{0:T(128)S(1)}, u32[]{:S(2)}) copy-start(f32[128]{0:T(128)S(1)} %broadcast_multiply_fusion.3) | copy-start | bytes 1540
  721.9 10.2 slice-start.12
  725.4 6.8 slice-start.13
  725.4 7.0 slice-start.14
  732.1 17.1 %copy-start.115 = (bf16[1024,64]{0,1:T(8,128)(2,1)}, bf16[1024,64]{0,1:T(8,128)(2,1)S(1)}, u32[]{:S(2)}) copy-start(bf16[1024,64]{0,1:T(8,128)(2,1)S(1)} %fusion.154) | copy-start | bytes 393220
  739.0 6.7 copy-start.36
  739.0 6.7 copy-start.38
  752.7 33.1 %copy-start.84 = (f32[128]{0:T(128)S(1)}, f32[128]{0:T(128)}, u32[]{:S(2)}) copy-start(f32[128]{0:T(128)} %copy-done.83) | copy-start | bytes 1540
  752.7 35.1 %copy-start.101 = (bf16[1024,512]{1,0:T(8,128)(2,1)S(1)}, bf16[1024,512]{1,0:T(8,128)(2,1)}, u32[]{:S(2)}) copy-start(bf16[1024,512]{1,0:T(8,128)(2,1)} %get-tuple-element.64) | copy-start | bytes 3145732
  796.2 28.4 %copy-start.14 = (bf16[1,128,1536]{2,1,0:T(8,128)(2,1)S(1)}, bf16[1,128,1536]{2,1,0:T(8,128)(2,1)}, u32[]{:S(2)}) copy-start(bf16[1,128,1536]{2,1,0:T(8,128)(2,1)} %param.16) | copy-start | bytes 1179652
  796.2 28.4 %copy-start.78 = (f32[128]{0:T(128)S(1)}, f32[128]{0:T(128)}, u32[]{:S(2)}) copy-start(f32[128]{0:T(128)} %copy-done.77) | copy-start | bytes 1540
  796.2 28.4 %copy-start.92 = (f32[128]{0:T(128)S(1)}, f32[128]{0:T(128)}, u32[]{:S(2)}) copy-start(f32[128]{0:T(128)} %copy-done.91) | copy-start | bytes 1540
  824.6 38.7 %slice-start.6 = ((s8[11010048]{0:T(1024)(128)(4,1)}), s8[2621440]{0:T(1024)(128)(4,1)S(1)}, s32[]{:S(2)}) async-start(s8[11010048]{0:T(1024)(128)(4,1)} %bitcast.468), calls=%async_computation.6 | async-start | bytes 5242880
  828.2 28.9 %copy-start.88 = (f32[1024,1,1]{0,2,1:T(1,128)S(1)}, f32[1024,1,1]{0,2,1:T(1,128)}, u32[]{:S(2)}) copy-start(f32[1024,1,1]{0,2,1:T(1,128)} %get-tuple-element.104) | copy-start | bytes 12292
  857.1 6.2 slice-start.7
  857.1 6.2 slice-start.8
  863.3 15.3 %copy-start.51 = (bf16[1024,512]{1,0:T(8,128)(2,1)}, bf16[1024,512]{1,0:T(8,128)(2,1)S(1)}, u32[]{:S(2)}) copy-start(bf16[1024,512]{1,0:T(8,128)(2,1)S(1)} %get-tuple-element.55) | copy-start | bytes 3145732
  887.2 37.4 %copy-start.3 = (f32[128,1536]{1,0:T(8,128)S(1)}, f32[128,1536]{1,0:T(8,128)}, u32[]{:S(2)}) copy-start(f32[128,1536]{1,0:T(8,128)} %copy-done.2) | copy-start | bytes 2359300
  887.2 37.4 %copy-start.67 = (f32[1536]{0:T(1024)S(1)}, f32[1536]{0:T(1024)}, u32[]{:S(2)}) copy-start(f32[1536]{0:T(1024)} %copy-done.66) | copy-start | bytes 18436
  887.2 37.4 %copy-start.80 = (f32[128]{0:T(128)S(1)}, f32[128]{0:T(128)}, u32[]{:S(2)}) copy-start(f32[128]{0:T(128)} %copy-done.79) | copy-start | bytes 1540
  887.2 39.5 %copy-start.30 = (f32[128,1536]{1,0:T(8,128)S(1)}, f32[128,1536]{1,0:T(8,128)}, u32[]{:S(2)}) copy-start(f32[128,1536]{1,0:T(8,128)} %get-tuple-element.46) | copy-start | bytes 2359300
  926.6 30.3 %copy-start.10 = (bf16[1536,512]{1,0:T(8,128)(2,1)S(1)}, bf16[1536,512]{1,0:T(8,128)(2,1)}, u32[]{:S(2)}) copy-start(bf16[1536,512]{1,0:T(8,128)(2,1)} %copy-done.9) | copy-start | bytes 4718596
  929.1 31.1 %copy-start.74 = (f32[3,1024]{1,0:T(4,128)S(1)}, f32[3,1024]{1,0:T(4,128)}, u32[]{:S(2)}) copy-start(f32[3,1024]{1,0:T(4,128)} %copy-done.73) | copy-start | bytes 36868
  960.2 13.3 %slice-start.9 = ((s8[12582912]{0:T(1024)(128)(4,1)}), s8[4194304]{0:T(1024)(128)(4,1)S(1)}, s32[]{:S(2)}) async-start(s8[12582912]{0:T(1024)(128)(4,1)} %bitcast.470), calls=%async_computation.9 | async-start | bytes 8388608
  960.2 13.3 %slice-start.10 = ((s8[12582912]{0:T(1024)(128)(4,1)}), s8[4194304]{0:T(1024)(128)(4,1)S(1)}, s32[]{:S(2)}) async-start(s8[12582912]{0:T(1024)(128)(4,1)} %bitcast.470), calls=%async_computation.10 | async-start | bytes 8388608
  967.7 5.9 slice-start.11
  984.2 35.7 %copy-start.8 = (bf16[1,128,1536]{2,1,0:T(8,128)(2,1)S(1)}, bf16[1,128,1536]{2,1,0:T(8,128)(2,1)}, u32[]{:S(2)}) copy-start(bf16[1,128,1536]{2,1,0:T(8,128)(2,1)} %param.15) | copy-start | bytes 1179652
  984.2 35.7 %copy-start.65 = (f32[1536]{0:T(1024)S(1)}, f32[1536]{0:T(1024)}, u32[]{:S(2)}) copy-start(f32[1536]{0:T(1024)} %copy-done.64) | copy-start | bytes 18436
  984.2 35.7 %copy-start.82 = (f32[128]{0:T(128)S(1)}, f32[128]{0:T(128)}, u32[]{:S(2)}) copy-start(f32[128]{0:T(128)} %copy-done.81) | copy-start | bytes 1540
  984.2 40.3 %copy-start.5 = (bf16[8,128,1536]{2,1,0:T(8,128)(2,1)S(1)}, bf16[8,128,1536]{2,1,0:T(8,128)(2,1)}, u32[]{:S(2)}) copy-start(bf16[8,128,1536]{2,1,0:T(8,128)(2,1)} %gather_rows.13) | copy-start | bytes 9437188
  984.2 40.3 %copy-start.42 = (bf16[64,3,1024]{2,0,1:T(8,128)(2,1)S(1)}, bf16[64,3,1024]{2,0,1:T(8,128)(2,1)}, u32[]{:S(2)}) copy-start(bf16[64,3,1024]{2,0,1:T(8,128)(2,1)} %copy-done.41) | copy-start | bytes 1179652
  1052.4 118.9 %copy-start.6 = (bf16[8,128,1536]{2,1,0:T(8,128)(2,1)S(1)}, bf16[8,128,1536]{2,1,0:T(8,128)(2,1)}, u32[]{:S(2)}) copy-start(bf16[8,128,1536]{2,1,0:T(8,128)(2,1)} %gather_rows.15) | copy-start | bytes 9437188
  1052.4 118.9 %copy-start.40 = (bf16[64,3,1024]{2,0,1:T(8,128)(2,1)S(1)}, bf16[64,3,1024]{2,0,1:T(8,128)(2,1)}, u32[]{:S(2)}) copy-start(bf16[64,3,1024]{2,0,1:T(8,128)(2,1)} %copy-done.39) | copy-start | bytes 1179652
  1201.2 90.1 %copy-start.58 = (bf16[1,48,1536]{2,1,0:T(8,128)(2,1)S(1)}, bf16[1,48,1536]{2,1,0:T(8,128)(2,1)}, u32[]{:S(2)}) copy-start(bf16[1,48,1536]{2,1,0:T(8,128)(2,1)} %convert_element_type.570) | copy-start | bytes 442372
  1201.2 91.9 %copy-start.17 = (bf16[8,7,48,512]{3,2,1,0:T(8,128)(2,1)S(1)}, bf16[8,7,48,512]{3,2,1,0:T(8,128)(2,1)}, u32[]{:S(2)}) copy-start(bf16[8,7,48,512]{3,2,1,0:T(8,128)(2,1)} %get-tuple-element.24) | copy-start | bytes 8257540
  1289.2 7.1 copy-start.55
  (69 other events, 211.9 us)

commit v2 on v0

--- a/solution.py
+++ b/solution.py
@@ -1,9 +1,12 @@
 from functools import partial
+import functools
 import math
 
 import jax
 import jax.numpy as jnp
 from jax import lax
+from jax.experimental import pallas as pl
+from jax.experimental.pallas import tpu as pltpu
 from jax.sharding import PartitionSpec as P
 
 HEAD_DIM = 64
@@ -659,6 +662,1133 @@
     )
 
 
+BF = jnp.bfloat16
+F32 = jnp.float32
+NX = 2
+NCORE = 2
+ANY = pl.BlockSpec(memory_space=pl.ANY)
+VM = pl.BlockSpec(memory_space=pltpu.VMEM)
+DMA = pltpu.SemaphoreType.DMA
+
+NN = ((1,), (0,))
+NT = ((1,), (1,))
+TN = ((0,), (0,))
+
+
+def dot(left, right, dims):
+    return lax.dot_general(left, right, (dims, ((), ())), preferred_element_type=jnp.float32)
+
+
+def remote(src, dst, send_sem, recv_sem, ctx, fsdp):
+    return pltpu.make_async_remote_copy(
+        src_ref=src,
+        dst_ref=dst,
+        send_sem=send_sem,
+        recv_sem=recv_sem,
+        device_id={"ctx": ctx, "fsdp": fsdp},
+        device_id_type=pl.DeviceIdType.MESH,
+    )
+
+
+def greet(barrier, ctx, fsdp):
+    pl.semaphore_signal(
+        barrier, inc=1, device_id={"ctx": ctx, "fsdp": fsdp}, device_id_type=pl.DeviceIdType.MESH
+    )
+
+
+class Line:
+    def __init__(self, nz):
+        self.nz = nz
+        self.ctx, self.fsdp = lax.axis_index("ctx"), lax.axis_index("fsdp")
+        self.z, self.x = self.ctx // NX, self.ctx % NX
+        self.mate = self.z * NX + 1 - self.x
+        self.above = (self.z + 1) * NX + self.x
+        self.below = (self.z - 1) * NX + self.x
+
+    def greet(self):
+        barrier = pltpu.get_barrier_semaphore()
+        greet(barrier, self.mate, self.fsdp)
+
+        @pl.when(self.z > 0)
+        def _():
+            greet(barrier, self.below, self.fsdp)
+
+        @pl.when(self.z < self.nz - 1)
+        def _():
+            greet(barrier, self.above, self.fsdp)
+
+        ends = jnp.where(self.z > 0, 1, 0) + jnp.where(self.z < self.nz - 1, 1, 0)
+        pl.semaphore_wait(barrier, 1 + ends)
+
+    def near(self, i):
+        z, nz = self.z, self.nz
+        mid1 = jnp.where(i == 0, 1, jnp.where(i == 1, 0, i))
+        mid2 = jnp.where(i == 0, 2, jnp.where(i == 1, 1, jnp.where(i == 2, 3, 0)))
+        return jnp.where(z == 0, i, jnp.where(z == nz - 1, nz - 1 - i, jnp.where(z == 1, mid1, mid2)))
+
+    def far(self, i):
+        z, nz = self.z, self.nz
+        mid1 = jnp.where(i == 0, 3, jnp.where(i == 1, 0, jnp.where(i == 2, 2, 1)))
+        mid2 = jnp.where(i == 0, 0, jnp.where(i == 1, 3, jnp.where(i == 2, 1, 2)))
+        return jnp.where(z == 0, nz - 1 - i, jnp.where(z == nz - 1, i, jnp.where(z == 1, mid1, mid2)))
+
+
+class Gather:
+    @staticmethod
+    def scratch(nz):
+        return [DMA((6, nz))]
+
+    def __init__(self, line, own_ref, all_ref, sems):
+        self.line, self.own, self.all, self.sems = line, own_ref, all_ref, sems
+
+    def block(self, row):
+        return self.all.at[row * NX + self.line.x]
+
+    def up(self, t, src=None):
+        line = self.line
+        block = self.block(line.z - t)
+        return remote(block if src is None else src, block, self.sems.at[0, t], self.sems.at[1, t], line.above, line.fsdp)
+
+    def down(self, t, src=None):
+        line = self.line
+        block = self.block(line.z + t)
+        return remote(block if src is None else src, block, self.sems.at[2, t], self.sems.at[3, t], line.below, line.fsdp)
+
+    def across(self, row, src=None):
+        line = self.line
+        block = self.block(row)
+        return remote(block if src is None else src, block, self.sems.at[4, row], self.sems.at[5, row], line.mate, line.fsdp)
+
+    def start(self):
+        line = self.line
+
+        @pl.when(line.z < line.nz - 1)
+        def _():
+            self.up(0, self.own).start()
+
+        @pl.when(line.z > 0)
+        def _():
+            self.down(0, self.own).start()
+
+        self.across(line.z, self.own).start()
+
+    def forward(self, t):
+        line = self.line
+
+        @pl.when(line.z - 1 - t >= 0)
+        def _():
+            remote(self.own, self.block(line.z - 1 - t), self.sems.at[0, t], self.sems.at[1, t], line.above, line.fsdp).wait_recv()
+
+            @pl.when(line.z < line.nz - 1)
+            def _():
+                self.up(t + 1).start()
+
+            self.across(line.z - 1 - t).start()
+
+        @pl.when(line.z + 1 + t < line.nz)
+        def _():
+            remote(self.own, self.block(line.z + 1 + t), self.sems.at[2, t], self.sems.at[3, t], line.below, line.fsdp).wait_recv()
+
+            @pl.when(line.z > 0)
+            def _():
+                self.down(t + 1).start()
+
+            self.across(line.z + 1 + t).start()
+
+    def wait_pair(self, row):
+        line = self.line
+        remote(self.own, self.all.at[row * NX + 1 - line.x], self.sems.at[4, row], self.sems.at[5, row], line.mate, line.fsdp).wait_recv()
+
+    def finish(self):
+        line = self.line
+        for t in range(line.nz - 1):
+
+            @pl.when((line.z - t >= 0) & (line.z < line.nz - 1))
+            def _():
+                self.up(t).wait_send()
+
+            @pl.when((line.z + t < line.nz) & (line.z > 0))
+            def _():
+                self.down(t).wait_send()
+
+        for row in range(line.nz):
+            self.across(row).wait_send()
+
+
+class Scatter:
+    @staticmethod
+    def scratch(nz, rows, width):
+        return [pltpu.VMEM((4, nz, rows, width), BF), DMA((6, nz))]
+
+    def __init__(self, line, part_ref, out_ref, work, sems):
+        self.line, self.part, self.out, self.sems = line, part_ref, out_ref, sems
+        self.xin, self.acc, self.upin, self.downin = (work.at[i] for i in range(4))
+
+    def across(self, row):
+        line = self.line
+        return remote(self.part.at[row * NX + 1 - line.x], self.xin.at[row], self.sems.at[0, row], self.sems.at[1, row], line.mate, line.fsdp)
+
+    def up(self, row):
+        line = self.line
+        return remote(self.acc.at[row], self.upin.at[row], self.sems.at[2, row], self.sems.at[3, row], line.above, line.fsdp)
+
+    def down(self, row):
+        line = self.line
+        return remote(self.acc.at[row], self.downin.at[row], self.sems.at[4, row], self.sems.at[5, row], line.below, line.fsdp)
+
+    def add(self, i):
+        line = self.line
+        row = line.far(i)
+        self.across(row).wait_recv()
+        mine = self.part[row * NX + line.x].astype(F32) + self.xin[row].astype(F32)
+
+        @pl.when(row > line.z)
+        def _():
+            @pl.when(line.z == 0)
+            def _():
+                self.acc[row] = mine.astype(BF)
+
+            @pl.when(line.z > 0)
+            def _():
+                self.up(row).wait_recv()
+                self.acc[row] = (mine + self.upin[row].astype(F32)).astype(BF)
+
+            self.up(row).start()
+
+        @pl.when(row < line.z)
+        def _():
+            @pl.when(line.z == line.nz - 1)
+            def _():
+                self.acc[row] = mine.astype(BF)
+
+            @pl.when(line.z < line.nz - 1)
+            def _():
+                self.down(row).wait_recv()
+                self.acc[row] = (mine + self.downin[row].astype(F32)).astype(BF)
+
+            self.down(row).start()
+
+        @pl.when(row == line.z)
+        def _():
+            self.out[...] = mine
+
+    def finish(self):
+        line = self.line
+
+        @pl.when(line.z > 0)
+        def _():
+            self.up(line.z).wait_recv()
+            self.out[...] += self.upin[line.z].astype(F32)
+
+        @pl.when(line.z < line.nz - 1)
+        def _():
+            self.down(line.z).wait_recv()
+            self.out[...] += self.downin[line.z].astype(F32)
+
+        for row in range(line.nz):
+            self.across(row).wait_send()
+
+            @pl.when(row > line.z)
+            def _():
+                self.up(row).wait_send()
+
+            @pl.when(row < line.z)
+            def _():
+                self.down(row).wait_send()
+
+
+def params(collective, vmem_mib):
+    return pltpu.CompilerParams(collective_id=collective, has_side_effects=True, vmem_limit_bytes=vmem_mib << 20)
+
+
+def gather_kernel(nz, x_ref, o_ref, own_sem, sems):
+    line = Line(nz)
+    line.greet()
+    ring = Gather(line, x_ref, o_ref, sems)
+    ring.start()
+    own = pltpu.make_async_copy(x_ref, o_ref.at[line.ctx], own_sem)
+    own.start()
+    for t in range(nz - 1):
+        ring.forward(t)
+    for row in range(nz):
+        ring.wait_pair(row)
+    ring.finish()
+    own.wait()
+
+
+def gather_rows(block, nz):
+    rows, width = block.shape
+    return pl.pallas_call(
+        functools.partial(gather_kernel, nz),
+        out_shape=jax.ShapeDtypeStruct((nz * NX, rows, width), block.dtype),
+        in_specs=[VM],
+        out_specs=ANY,
+        scratch_shapes=[DMA] + Gather.scratch(nz),
+        compiler_params=params(1, 16),
+        name="gather_rows",
+    )(block)
+
+
+def scatter_kernel(nz, p_ref, o_ref, work, sems):
+    line = Line(nz)
+    line.greet()
+    ring = Scatter(line, p_ref, o_ref, work, sems)
+    for i in range(nz):
+        ring.across(line.far(i)).start()
+    for i in range(nz):
+        ring.add(i)
+    ring.finish()
+
+
+def scatter_rows(parts, nz):
+    _, rows, width = parts.shape
+    return pl.pallas_call(
+        functools.partial(scatter_kernel, nz),
+        out_shape=jax.ShapeDtypeStruct((rows, width), F32),
+        in_specs=[VM],
+        out_specs=VM,
+        scratch_shapes=Scatter.scratch(nz, rows, width),
+        compiler_params=params(2, 32),
+        name="scatter_rows",
+    )(parts)
+
+
+def experts_kernel(nz, layer, x_ref, share_ref, mats_ref, o_ref, all_out, gate_out, up_out,
+                   mats, blocks, part, gate, up, load_sem, save_sem, gsems, work, ssems):
+    line = Line(nz)
+    rows, width = x_ref.shape
+    load = pltpu.make_async_copy(mats_ref.at[layer, pl.ds(1, 6)], mats, load_sem)
+    load.start()
+    line.greet()
+    ring = Gather(line, x_ref, blocks, gsems)
+    ring.start()
+    blocks[line.ctx] = x_ref[...]
+    load.wait()
+
+    def saves(row):
+        pair = pl.ds(row * NX, NX)
+        return (
+            pltpu.make_async_copy(blocks.at[pair], all_out.at[pair], save_sem.at[0, row]),
+            pltpu.make_async_copy(gate.at[pair], gate_out.at[pair], save_sem.at[1, row]),
+            pltpu.make_async_copy(up.at[pair], up_out.at[pair], save_sem.at[2, row]),
+        )
+
+    def step(i, carry):
+        @pl.when(i < nz - 1)
+        def _():
+            ring.forward(i)
+
+        row = line.near(i)
+        ring.wait_pair(row)
+        pair = pl.ds(row * NX, NX)
+        block = blocks[pair].reshape(NX * rows, width)
+        share = share_ref[pair].reshape(NX * rows, 2)
+        total = None
+        for e in range(2):
+            gate_act = dot(block, mats[e], NN)
+            up_act = dot(block, mats[2 + e], NN)
+            units = gate_act.shape[1]
+            gate[pair, :, pl.ds(e * units, units)] = gate_act.astype(BF).reshape(NX, rows, units)
+            up[pair, :, pl.ds(e * units, units)] = up_act.astype(BF).reshape(NX, rows, units)
+            inner = gate_act / (1.0 + jnp.exp(-gate_act)) * up_act * share[:, e : e + 1]
+            term = dot(inner.astype(BF), mats[4 + e], NT)
+            total = term if total is None else total + term
+        part[pair] = total.astype(BF).reshape(NX, rows, width)
+        for save in saves(row):
+            save.start()
+        return carry
+
+    lax.fori_loop(0, nz, step, 0)
+    sums = Scatter(line, part, o_ref, work, ssems)
+    for i in range(nz):
+        sums.across(line.far(i)).start()
+    ring.finish()
+    for i in range(nz):
+        sums.add(i)
+    sums.finish()
+    for row in range(nz):
+        for save in saves(row):
+            save.wait()
+
+
+def experts_forward(block, share, mats, layer, nz):
+    rows, width = block.shape
+    units = mats.shape[3]
+    group = nz * NX
+    acts = jax.ShapeDtypeStruct((group, rows, 2 * units), BF)
+    return pl.pallas_call(
+        functools.partial(experts_kernel, nz, layer),
+        out_shape=(
+            jax.ShapeDtypeStruct((rows, width), F32),
+            jax.ShapeDtypeStruct((group, rows, width), BF),
+            acts,
+            acts,
+        ),
+        in_specs=[VM, VM, ANY],
+        out_specs=(VM, ANY, ANY, ANY),
+        scratch_shapes=[
+            pltpu.VMEM((6, width, units), BF),
+            pltpu.VMEM((group, rows, width), BF),
+            pltpu.VMEM((group, rows, width), BF),
+            pltpu.VMEM((group, rows, 2 * units), BF),
+            pltpu.VMEM((group, rows, 2 * units), BF),
+            DMA,
+            DMA((3, nz)),
+        ]
+        + Gather.scratch(nz)
+        + Scatter.scratch(nz, rows, width),
+        compiler_params=params(5 + 2 * layer, 60),
+        name="experts_forward",
+    )(block, share, mats)
+
+
+def experts_back_kernel(nz, layer, x_ref, share_ref, mats_ref, gate_ref, up_ref, o_ref, all_out, dgate_out, dup_out, inner_out,
+                        mats, blocks, part, gate, up, inners, load_sem, save_sem, gsems, work, ssems):
+    line = Line(nz)
+    rows, width = x_ref.shape
+    loads = (
+        pltpu.make_async_copy(mats_ref.at[layer, pl.ds(1, 6)], mats, load_sem.at[0]),
+        pltpu.make_async_copy(gate_ref, gate, load_sem.at[1]),
+        pltpu.make_async_copy(up_ref, up, load_sem.at[2]),
+    )
+    for load in loads:
+        load.start()
+    line.greet()
+    ring = Gather(line, x_ref, blocks, gsems)
+    ring.start()
+    blocks[line.ctx] = x_ref[...]
+    for load in loads:
+        load.wait()
+
+    def saves(row):
+        pair = pl.ds(row * NX, NX)
+        return (
+            pltpu.make_async_copy(blocks.at[pair], all_out.at[pair], save_sem.at[0, row]),
+            pltpu.make_async_copy(gate.at[pair], dgate_out.at[pair], save_sem.at[1, row]),
+            pltpu.make_async_copy(up.at[pair], dup_out.at[pair], save_sem.at[2, row]),
+            pltpu.make_async_copy(inners.at[pair], inner_out.at[pair], save_sem.at[3, row]),
+        )
+
+    def step(i, carry):
+        @pl.when(i < nz - 1)
+        def _():
+            ring.forward(i)
+
+        row = line.near(i)
+        ring.wait_pair(row)
+        pair = pl.ds(row * NX, NX)
+        block = blocks[pair].reshape(NX * rows, width)
+        share = share_ref[pair].reshape(NX * rows, 2)
+        total = None
+        units = mats.shape[2]
+        for e in range(2):
+            part_of = pl.ds(e * units, units)
+            gate_act = gate[pair, :, part_of].reshape(NX * rows, units).astype(F32)
+            up_act = up[pair, :, part_of].reshape(NX * rows, units).astype(F32)
+            grad_inner = dot(block, mats[4 + e], NN) * share[:, e : e + 1]
+            sigmoid = 1.0 / (1.0 + jnp.exp(-gate_act))
+            silu = gate_act * sigmoid
+            d_gate = (grad_inner * up_act * (sigmoid + silu * (1.0 - sigmoid))).astype(BF)
+            d_up = (grad_inner * silu).astype(BF)
+            inners[pair, :, part_of] = (silu * up_act * share[:, e : e + 1]).astype(BF).reshape(NX, rows, units)
+            gate[pair, :, part_of] = d_gate.reshape(NX, rows, units)
+            up[pair, :, part_of] = d_up.reshape(NX, rows, units)
+            term = dot(d_gate, mats[e], NT) + dot(d_up, mats[2 + e], NT)
+            total = term if total is None else total + term
+        part[pair] = total.astype(BF).reshape(NX, rows, width)
+        for save in saves(row):
+            save.start()
+        return carry
+
+    lax.fori_loop(0, nz, step, 0)
+    sums = Scatter(line, part, o_ref, work, ssems)
+    for i in range(nz):
+        sums.across(line.far(i)).start()
+    ring.finish()
+    for i in range(nz):
+        sums.add(i)
+    sums.finish()
+    for row in range(nz):
+        for save in saves(row):
+            save.wait()
+
+
+def experts_backward(block, share, mats, layer, gate_act, up_act, nz):
+    rows, width = block.shape
+    units = mats.shape[3]
+    group = nz * NX
+    acts = jax.ShapeDtypeStruct((group, rows, 2 * units), BF)
+    held = pltpu.VMEM((group, rows, 2 * units), BF)
+    return pl.pallas_call(
+        functools.partial(experts_back_kernel, nz, layer),
+        out_shape=(
+            jax.ShapeDtypeStruct((rows, width), F32),
+            jax.ShapeDtypeStruct((group, rows, width), BF),
+            acts,
+            acts,
+            acts,
+        ),
+        in_specs=[VM, VM, ANY, ANY, ANY],
+        out_specs=(VM, ANY, ANY, ANY, ANY),
+        scratch_shapes=[
+            pltpu.VMEM((6, width, units), BF),
+            pltpu.VMEM((group, rows, width), BF),
+            pltpu.VMEM((group, rows, width), BF),
+            held,
+            held,
+            held,
+            DMA((3,)),
+            DMA((4, nz)),
+        ]
+        + Gather.scratch(nz)
+        + Scatter.scratch(nz, rows, width),
+        compiler_params=params(6 + 2 * layer, 60),
+        name="experts_backward",
+    )(block, share, mats, gate_act, up_act)
+
+
+def far_of(nz, z, i):
+    mid1 = jnp.where(i == 0, 3, jnp.where(i == 1, 0, jnp.where(i == 2, 2, 1)))
+    mid2 = jnp.where(i == 0, 0, jnp.where(i == 1, 3, jnp.where(i == 2, 1, 2)))
+    return jnp.where(z == 0, nz - 1 - i, jnp.where(z == nz - 1, i, jnp.where(z == 1, mid1, mid2)))
+
+
+class Exchange:
+    @staticmethod
+    def scratch(nz, blk, lead=()):
+        return [
+            pltpu.VMEM(lead + (2, 2, 2) + blk, BF),
+            pltpu.VMEM(lead + (nz,) + blk, BF),
+            DMA(lead + (2, nz, nz, 2)),
+            DMA(lead + (2, nz)),
+        ]
+
+    def __init__(self, line, src_at, dst_at, passing, for_mate, zs, xs, lead=()):
+        self.line, self.src_at, self.dst_at, self.lead = line, src_at, dst_at, lead
+        self.passing, self.for_mate, self.zs, self.xs = passing, for_mate, zs, xs
+
+    def held(self, way, src, dest, side, at):
+        last = self.line.nz - 1
+        slot = (dest - at - 1) + src if way == 0 else (at - dest - 1) + last - src
+        return self.passing.at[self.lead + (way, slot, side)]
+
+    def zsem(self, kind, src, dest, side):
+        return self.zs.at[self.lead + (kind, src, dest, side)]
+
+    def hop(self, way, src, dest, side, ref):
+        line = self.line
+        to = line.z + 1 if way == 0 else line.z - 1
+        sems = self.zsem(0, src, dest, side), self.zsem(1, src, dest, side)
+        target = to * NX + line.x
+
+        @pl.when(dest == to)
+        def _():
+            land = self.dst_at(src * NX + line.x) if side == 0 else self.for_mate.at[self.lead + (src,)]
+            remote(ref, land, *sems, target, line.fsdp).start()
+
+        @pl.when(dest != to)
+        def _():
+            remote(ref, self.held(way, src, dest, side, to), *sems, target, line.fsdp).start()
+
+    def to_mate(self, src, ref=None):
+        line = self.line
+        ref = self.for_mate.at[self.lead + (src,)] if ref is None else ref
+        return remote(ref, self.dst_at(src * NX + line.x), self.xs.at[self.lead + (0, src)], self.xs.at[self.lead + (1, src)], line.mate, line.fsdp)
+
+    def send(self, dest):
+        line = self.line
+        for side, column in ((0, line.x), (1, 1 - line.x)):
+            ref = self.src_at(dest * NX + column)
+
+            @pl.when(dest > line.z)
+            def _():
+                self.hop(0, line.z, dest, side, ref)
+
+            @pl.when(dest < line.z)
+            def _():
+                self.hop(1, line.z, dest, side, ref)
+
+        @pl.when(dest == line.z)
+        def _():
+            self.to_mate(line.z, self.src_at(line.mate)).start()
+
+    def events(self, i):
+        line = self.line
+        found = []
+        for k in range(1, line.nz):
+            j = i - k
+            for way in range(2):
+                src = line.z - k if way == 0 else line.z + k
+                dest = far_of(line.nz, src, j)
+                here = (dest >= line.z) if way == 0 else (dest <= line.z)
+                found.append((way, src, dest, (src >= 0) & (src < line.nz) & (j >= 0) & (j < line.nz - 1) & here))
+        return found
+
+    def handle(self, way, src, dest, arrived):
+        line = self.line
+        for side in range(2):
+            wait = self.held(way, 0 if way == 0 else line.nz - 1, line.z + 1 if way == 0 else line.z - 1, side, line.z)
+            remote(wait, wait, self.zsem(0, src, dest, side), self.zsem(1, src, dest, side), line.mate, line.fsdp).wait_recv()
+
+            @pl.when(dest != line.z)
+            def _():
+                self.hop(way, src, dest, side, self.held(way, src, dest, side, line.z))
+
+        @pl.when(dest == line.z)
+        def _():
+            self.to_mate(src).start()
+            arrived(src * NX + line.x)
+
+    def mate_arrived(self, src):
+        line = self.line
+        wait = self.for_mate.at[self.lead + (src,)]
+        remote(wait, wait, self.xs.at[self.lead + (0, src)], self.xs.at[self.lead + (1, src)], line.mate, line.fsdp).wait_recv()
+
+    def finish(self):
+        line = self.line
+        wait = self.for_mate.at[self.lead + (0,)]
+        for src in range(line.nz):
+            for dest in range(line.nz):
+                if src != dest:
+                    passes = (line.z >= src) & (line.z < dest) if src < dest else (line.z <= src) & (line.z > dest)
+
+                    @pl.when(passes)
+                    def _():
+                        for side in range(2):
+                            remote(wait, wait, self.zsem(0, src, dest, side), self.zsem(1, src, dest, side), line.mate, line.fsdp).wait_send()
+
+            self.to_mate(src).wait_send()
+
+
+LAG = 3
+
+
+def weights_kernel(nctx, nfs, rows, w_ref, g_ref, o_ref, go_ref, passing, for_mate, zs, xs, own_sem, y_sem, c_sem, gown_sem, gp_sem, gy_sem, gc_sem):
+    nz = nctx // NX
+    line = Line(nz)
+    ctx, fsdp = line.ctx, line.fsdp
+    layers = w_ref.shape[0]
+    y, core = fsdp // NCORE, fsdp % NCORE
+    y_mate = (1 - y) * NCORE + core
+    c_mate = y * NCORE + 1 - core
+    y_c_mate = (1 - y) * NCORE + 1 - core
+    barrier = pltpu.get_barrier_semaphore()
+    for step in range(1, nctx):
+        greet(barrier, (ctx + step) % nctx, fsdp)
+    for other in (y_mate, c_mate):
+        greet(barrier, ctx, other)
+    pl.semaphore_wait(barrier, nctx + 1)
+
+    def place(layer, s, f):
+        return o_ref.at[layer, :, pl.ds(pl.multiple_of((s * nfs + f) * rows, rows), rows), :]
+
+    def swap(layer):
+        return Exchange(
+            line,
+            lambda to: w_ref.at[layer, to],
+            lambda frm: place(layer, frm, fsdp),
+            passing, for_mate, zs, xs,
+            (layer,),
+        )
+
+    def over_y(layer, frm, f, ref=None):
+        return remote(place(layer, frm, f) if ref is None else ref, place(layer, frm, f), y_sem.at[0, layer, frm], y_sem.at[1, layer, frm], ctx, y_mate)
+
+    def over_c(layer, frm, f, k, ref=None):
+        return remote(place(layer, frm, f) if ref is None else ref, place(layer, frm, f), c_sem.at[0, k, layer, frm], c_sem.at[1, k, layer, frm], ctx, c_mate)
+
+    def own(layer):
+        return pltpu.make_async_copy(w_ref.at[layer, ctx], place(layer, ctx, fsdp), own_sem.at[layer])
+
+    def begin(layer):
+        exchange = swap(layer)
+        for i in range(nz - 1):
+            exchange.send(line.far(i))
+        exchange.send(line.z)
+        over_y(layer, ctx, fsdp, w_ref.at[layer, ctx]).start()
+        over_c(layer, ctx, fsdp, 0, w_ref.at[layer, ctx]).start()
+        own(layer).start()
+
+    def arrived(layer, frm):
+        over_y(layer, frm, fsdp).start()
+        over_c(layer, frm, fsdp, 0).start()
+
+    def from_y(layer, frm):
+        over_y(layer, frm, y_mate).wait_recv()
+        over_c(layer, frm, y_mate, 1).start()
+
+    def take(layer, i):
+        exchange = swap(layer)
+        for way, src, dest, real in exchange.events(i):
+
+            @pl.when(real)
+            def _():
+                exchange.handle(way, src, dest, lambda frm: arrived(layer, frm))
+
+        def mine(late, then):
+            @pl.when(i == late)
+            def _():
+                then(line.z)
+
+            for way, src, dest, real in exchange.events(i - late):
+
+                @pl.when(real & (dest == line.z))
+                def _():
+                    then(src)
+
+        def mates(src):
+            exchange.mate_arrived(src)
+            arrived(layer, src * NX + 1 - line.x)
+
+        mine(1, mates)
+        mine(2, lambda src: from_y(layer, src * NX + line.x))
+        mine(3, lambda src: from_y(layer, src * NX + 1 - line.x))
+
+    def small(to):
+        return remote(g_ref.at[to], go_ref.at[ctx * nfs + fsdp], gp_sem.at[0, to], gp_sem.at[1, ctx], to, fsdp)
+
+    def small_in(frm):
+        return remote(g_ref.at[ctx], go_ref.at[frm * nfs + fsdp], gp_sem.at[0, frm], gp_sem.at[1, frm], frm, fsdp)
+
+    def small_y(frm, f):
+        return remote(go_ref.at[frm * nfs + f], go_ref.at[frm * nfs + f], gy_sem.at[0, frm], gy_sem.at[1, frm], ctx, y_mate)
+
+    def small_c(frm, f, k):
+        return remote(go_ref.at[frm * nfs + f], go_ref.at[frm * nfs + f], gc_sem.at[0, k, frm], gc_sem.at[1, k, frm], ctx, c_mate)
+
+    small_own = pltpu.make_async_copy(g_ref.at[ctx], go_ref.at[ctx * nfs + fsdp], gown_sem)
+    small_own.start()
+    for step in range(1, nctx):
+        small((ctx + step) % nctx).start()
+    steps = 2 * nz - 3 + 3
+
+    def step(i, carry):
+        for layer in range(layers):
+            at = i - LAG * layer
+
+            @pl.when(at == 0)
+            def _():
+                begin(layer)
+
+        def each(layer, carry):
+            at = i - LAG * layer
+
+            @pl.when((at > 0) & (at <= steps))
+            def _():
+                take(layer, at)
+
+            return carry
+
+        lax.fori_loop(0, layers, each, 0)
+        return carry
+
+    lax.fori_loop(0, steps + 1 + LAG * (layers - 1), step, 0)
+    small_own.wait()
+    for k in range(nctx):
+        if k:
+            small_in((ctx + k) % nctx).wait_recv()
+        small_y((ctx + k) % nctx, fsdp).start()
+        small_c((ctx + k) % nctx, fsdp, 0).start()
+    for k in range(nctx):
+        small_y((ctx + k) % nctx, y_mate).wait_recv()
+        small_c((ctx + k) % nctx, y_mate, 1).start()
+    for frm in range(nctx):
+        small_c(frm, c_mate, 0).wait_recv()
+        small_c(frm, y_c_mate, 1).wait_recv()
+        small_c(frm, fsdp, 0).wait_send()
+        small_c(frm, y_mate, 1).wait_send()
+        small_y(frm, fsdp).wait_send()
+    for step_ in range(1, nctx):
+        small((ctx + step_) % nctx).wait_send()
+
+    def close(layer, carry):
+        own(layer).wait()
+        for frm in range(nctx):
+            over_c(layer, frm, c_mate, 0).wait_recv()
+            over_c(layer, frm, y_c_mate, 1).wait_recv()
+            over_c(layer, frm, fsdp, 0).wait_send()
+            over_c(layer, frm, y_mate, 1).wait_send()
+            over_y(layer, frm, fsdp).wait_send()
+        swap(layer).finish()
+        return carry
+
+    lax.fori_loop(0, layers, close, 0)
+
+
+def spread_weights(send, small, nfs):
+    layers, nctx, mats, rows, width = send.shape
+    return pl.pallas_call(
+        functools.partial(weights_kernel, nctx, nfs, rows),
+        out_shape=(
+            jax.ShapeDtypeStruct((layers, mats, nctx * nfs * rows, width), send.dtype),
+            jax.ShapeDtypeStruct((nctx * nfs,) + small.shape[1:], small.dtype),
+        ),
+        in_specs=[VM, VM],
+        out_specs=(ANY, ANY),
+        scratch_shapes=Exchange.scratch(nctx // NX, (mats, rows, width), (layers,))
+        + [
+            DMA((layers,)),
+            DMA((2, layers, nctx)),
+            DMA((2, 2, layers, nctx)),
+            DMA,
+            DMA((2, nctx)),
+            DMA((2, nctx)),
+            DMA((2, 2, nctx)),
+        ],
+        compiler_params=params(3, 40),
+        name="spread_weights",
+    )(send, small)
+
+
+def grads_kernel(nctx, nfs, rows, normed_ref, dproj_ref, middle_ref, attended_ref, moe_ref, dgate_ref, dup_ref, grad_ref, inner_ref, e_ref,
+                 o_ref, eo_ref, mine, cin, yin, half, full, e_cin, e_half, e_yin, e_full,
+                 own_sem, c_sem, y_sem, p_sem, eown_sem, ec_sem, ey_sem, ep_sem):
+    nz = nctx // NX
+    line = Line(nz)
+    ctx, fsdp = line.ctx, line.fsdp
+    y, core = fsdp // NCORE, fsdp % NCORE
+    y_mate = (1 - y) * NCORE + core
+    c_mate = y * NCORE + 1 - core
+    mats = mine.shape[0]
+    proj = dproj_ref.shape[1]
+    units = dgate_ref.shape[1] // 2
+    slab = NX * nfs * rows
+    barrier = pltpu.get_barrier_semaphore()
+    for step in range(1, nctx):
+        greet(barrier, (ctx + step) % nctx, fsdp)
+    for other in (y_mate, c_mate):
+        greet(barrier, ctx, other)
+    pl.semaphore_wait(barrier, nctx + 1)
+
+    def span(s, f):
+        return pl.ds(pl.multiple_of((s * nfs + f) * rows, rows), rows)
+
+    def to_c(s, k):
+        f = (1 - y if k == 0 else y) * NCORE + 1 - core
+        return remote(mine.at[:, span(s, f), :], cin.at[k, s], c_sem.at[0, k, s], c_sem.at[1, k, s], ctx, c_mate)
+
+    def to_y(s):
+        return remote(half.at[s], yin.at[s], y_sem.at[0, s], y_sem.at[1, s], ctx, y_mate)
+
+    def out(s):
+        return remote(full.at[s], o_ref.at[ctx], p_sem.at[0, s], p_sem.at[1, ctx], s, fsdp)
+
+    def out_in(s):
+        return remote(full.at[s], o_ref.at[s], p_sem.at[0, s], p_sem.at[1, s], s, fsdp)
+
+    e_to_c = remote(e_ref.at[1 - core], e_cin, ec_sem.at[0], ec_sem.at[1], ctx, c_mate)
+    e_to_y = remote(e_half.at[1 - y], e_yin, ey_sem.at[0], ey_sem.at[1], ctx, y_mate)
+
+    def e_out(s):
+        return remote(e_full.at[s], eo_ref.at[ctx], ep_sem.at[0, s], ep_sem.at[1, ctx], s, fsdp)
+
+    def e_out_in(s):
+        return remote(e_full.at[s], eo_ref.at[s], ep_sem.at[0, s], ep_sem.at[1, s], s, fsdp)
+
+    e_to_c.start()
+    own = pltpu.make_async_copy(full.at[ctx], o_ref.at[ctx], own_sem)
+    e_own = pltpu.make_async_copy(e_full.at[ctx], eo_ref.at[ctx], eown_sem)
+
+    turn_of = line.far
+
+    def compute(row):
+        lanes = pl.ds(pl.multiple_of(row * slab, 128), slab)
+        tall = pl.ds(pl.multiple_of(row * slab, 16), slab)
+        mine[0, tall, pl.ds(0, proj)] = dot(normed_ref[:, lanes], dproj_ref[...], TN).astype(BF)
+        mine[0, tall, pl.ds(proj, mine.shape[2] - proj)] = dot(middle_ref[:, lanes], attended_ref[...], TN).astype(BF)
+        moe = moe_ref[:, lanes]
+        for e in range(2):
+            part_of = pl.ds(e * units, units)
+            mine[1 + e, tall, :] = dot(moe, dgate_ref[:, part_of], TN).astype(BF)
+            mine[3 + e, tall, :] = dot(moe, dup_ref[:, part_of], TN).astype(BF)
+            mine[5 + e, tall, :] = dot(grad_ref[:, lanes], inner_ref[:, part_of], TN).astype(BF)
+
+    def first(s):
+        to_c(s, 0).wait_recv()
+
+        def one(m, _):
+            half[s, m] = (mine[m, span(s, y_mate), :].astype(F32) + cin[0, s, m].astype(F32)).astype(BF)
+            return 0
+
+        lax.fori_loop(0, mats, one, 0)
+        to_y(s).start()
+
+    def second(s):
+        to_c(s, 1).wait_recv()
+        to_y(s).wait_recv()
+
+        def one(m, _):
+            full[s, m] = (mine[m, span(s, fsdp), :].astype(F32) + cin[1, s, m].astype(F32) + yin[s, m].astype(F32)).astype(BF)
+            return 0
+
+        lax.fori_loop(0, mats, one, 0)
+
+        @pl.when(s != ctx)
+        def _():
+            out(s).start()
+
+    def step(i, carry):
+        @pl.when(i < nz)
+        def _():
+            row = turn_of(i)
+            compute(row)
+            for k in range(2):
+                for side in range(NX):
+                    to_c(row * NX + side, k).start()
+
+        @pl.when((i >= 1) & (i < nz + 1))
+        def _():
+            for side in range(NX):
+                first(turn_of(i - 1) * NX + side)
+
+        @pl.when((i >= 2) & (i < nz + 2))
+        def _():
+            row = turn_of(i - 2)
+            for side in range(NX):
+                second(row * NX + side)
+
+        return carry
+
+    lax.fori_loop(0, nz + 2, step, 0)
+    own.start()
+    e_to_c.wait_recv()
+    e_half[...] = e_ref[core] + e_cin[...]
+    e_to_y.start()
+    e_to_y.wait_recv()
+    e_full[...] = e_half[y] + e_yin[...]
+    e_own.start()
+    for step_ in range(1, nctx):
+        e_out((ctx + step_) % nctx).start()
+    for s in range(nctx):
+        for k in range(2):
+            to_c(s, k).wait_send()
+        to_y(s).wait_send()
+
+        @pl.when(s != ctx)
+        def _():
+            out(s).wait_send()
+            out_in(s).wait_recv()
+            e_out(s).wait_send()
+            e_out_in(s).wait_recv()
+
+    e_to_c.wait_send()
+    e_to_y.wait_send()
+    e_own.wait()
+    own.wait()
+
+
+def collect_grads(nctx, nfs, normed, dproj, middle, attended, moe, dgate, dup, grad, inner, extra):
+    width = normed.shape[1]
+    rows = width // (nctx * nfs)
+    mats, cols = 7, dproj.shape[1] + attended.shape[1]
+    blk = (mats, rows, cols)
+    tile = extra.shape[3:]
+    return pl.pallas_call(
+        functools.partial(grads_kernel, nctx, nfs, rows),
+        out_shape=(jax.ShapeDtypeStruct((nctx,) + blk, BF), jax.ShapeDtypeStruct((nctx,) + tile, F32)),
+        in_specs=[VM] * 10,
+        out_specs=(ANY, ANY),
+        scratch_shapes=[
+            pltpu.VMEM((mats, width, cols), BF),
+            pltpu.VMEM((2, nctx) + blk, BF),
+            pltpu.VMEM((nctx,) + blk, BF),
+            pltpu.VMEM((nctx,) + blk, BF),
+            pltpu.VMEM((nctx,) + blk, BF),
+            pltpu.VMEM((2, nctx) + tile, F32),
+            pltpu.VMEM((2, nctx) + tile, F32),
+            pltpu.VMEM((nctx,) + tile, F32),
+            pltpu.VMEM((nctx,) + tile, F32),
+            DMA,
+            DMA((2, 2, nctx)),
+            DMA((2, nctx)),
+            DMA((2, nctx)),
+            DMA,
+            DMA((2,)),
+            DMA((2,)),
+            DMA((2, nctx)),
+        ],
+        compiler_params=params(4, 63),
+        name="collect_grads",
+    )(normed, dproj, middle, attended, moe, dgate, dup, grad, inner, extra)
+
+
+def rope_tables(places):
+    half_dim = HEAD_DIM // 2
+    freq_steps = jnp.arange(half_dim, dtype=jnp.float32)
+    inverse = jnp.exp(freq_steps * (-2.0 * math.log(10000.0) / HEAD_DIM))
+    angles = places[:, None] * inverse[None, :]
+    return jnp.cos(angles), jnp.sin(angles)
+
+
+def turn(values, cos_part, sin_part):
+    half_dim = HEAD_DIM // 2
+    first_half = values[..., :half_dim]
+    second_half = values[..., half_dim:]
+    cos_part, sin_part = cos_part[:, None, :], sin_part[:, None, :]
+    return jnp.concatenate(
+        [first_half * cos_part - second_half * sin_part, second_half * cos_part + first_half * sin_part],
+        axis=-1,
+    )
+
+
+def pack_weights(master_set, layer, nctx):
+    query_weight, key_weight, value_weight, out_weight, attn_gain, moe_gain, gate_weight, up_weight, down_weight = master_set
+    rows = query_weight.shape[1]
+
+    def columns(master):
+        low = master[layer].astype(BF).reshape(rows, nctx, -1)
+        return low.transpose(1, 0, 2)
+
+    attn = jnp.concatenate(
+        [columns(query_weight), columns(key_weight), columns(value_weight), columns(out_weight)], axis=-1
+    )
+
+    def experts(master):
+        low = master[layer].astype(BF)
+        return low.reshape(nctx, -1, rows, low.shape[-1])
+
+    send = jnp.concatenate(
+        [attn[:, None], experts(gate_weight), experts(up_weight), experts(down_weight)], axis=1
+    )
+    gains = jnp.stack([attn_gain[layer], moe_gain[layer]]).astype(BF).astype(F32)
+    return send, jnp.pad(gains, ((0, 0), (0, 128 - rows)))
+
+
+def norm_back(values, gain, grad):
+    scale = lax.rsqrt(jnp.mean(values * values, axis=-1, keepdims=True) + EPSILON)
+    unit = values * scale
+    grad_gain = jnp.sum(grad * unit, axis=0)
+    pulled = grad * gain
+    return scale * (pulled - unit * jnp.mean(pulled * unit, axis=-1, keepdims=True)), grad_gain
+
+
+def fast_body(nctx, nfs, *args):
+    (tokens, cotangent, lengths, tile_order, routes, gates), master_set = args[:6], args[6:]
+    nz = nctx // NX
+    rows_here, model_width = tokens.shape[1], tokens.shape[2]
+    group_rows = rows_here * nctx
+    ctx = lax.axis_index("ctx")
+    seg_all, pos_all = layout(lengths[0], tile_order[0], group_rows)
+    visible = (seg_all[:, None] == seg_all[None, :]) & (pos_all[None, :] <= pos_all[:, None])
+    cos_part, sin_part = rope_tables(pos_all.astype(jnp.float32))
+    score_scale = HEAD_DIM ** (-0.5)
+    q_width = 3 * HEAD_DIM
+    kv_at, v_at, o_at = q_width, q_width + HEAD_DIM, q_width + 2 * HEAD_DIM
+
+    expert_ids = jnp.arange(EXPERTS, dtype=jnp.int32)
+    table = jnp.sum(
+        jnp.where(routes[:, 0, :, :, None] == expert_ids, gates[:, 0, :, :, None], 0.0), axis=-2
+    )
+    packed = [pack_weights(master_set, layer, nctx) for layer in range(LAYERS)]
+    rows = packed[0][0].shape[2]
+    gains = jnp.broadcast_to(jnp.concatenate([gain for _, gain in packed])[None], (nctx, 2 * LAYERS, 128))
+    shares = table.transpose(2, 0, 1).reshape(nctx, 2, LAYERS, rows_here).transpose(0, 2, 1, 3)
+    shares = shares.reshape(nctx, 2 * LAYERS, rows_here)
+    pad = jnp.zeros((nctx, 8 - 2 * LAYERS, 128), F32)
+    small = jnp.concatenate([gains, pad, shares, pad], axis=1)
+    mats_all, small_all = spread_weights(jnp.stack([send for send, _ in packed]), small, nfs)
+    shares = lax.dynamic_index_in_dim(
+        small_all.reshape(nctx, nfs, 16, 128), lax.axis_index("fsdp"), 1, keepdims=False
+    )
+    fetched = [
+        (
+            mats_all[layer, 0],
+            small_all[:, 2 * layer, :rows].reshape(-1),
+            small_all[:, 2 * layer + 1, :rows].reshape(-1),
+            shares[:, 8 + 2 * layer : 10 + 2 * layer].transpose(0, 2, 1),
+        )
+        for layer in range(LAYERS)
+    ]
+
+    hidden = tokens[0].astype(jnp.float32)
+    records = []
+    for layer in range(LAYERS):
+        attn, attn_gain, moe_gain, share = fetched[layer]
+        normed = rms_norm(hidden, attn_gain).astype(BF)
+        normed_all = gather_rows(normed, nz).reshape(group_rows, model_width)
+        proj = dot(normed_all, attn[:, :o_at], NN)
+        turned = turn(proj[:, :v_at].reshape(group_rows, 4, HEAD_DIM), cos_part, sin_part).astype(BF)
+        queries, keys = turned[:, :3], turned[:, 3]
+        values = proj[:, v_at:].astype(BF)
+        raw = jnp.einsum("qhd,kd->hqk", queries, keys, preferred_element_type=jnp.float32) * score_scale
+        raw = jnp.where(visible[None], raw, NEGATIVE)
+        peak = jnp.max(raw, axis=-1, keepdims=True)
+        powers = jnp.exp(raw - peak)
+        probs = powers / jnp.sum(powers, axis=-1, keepdims=True)
+        attended = jnp.einsum("hqk,kd->qhd", probs.astype(BF), values, preferred_element_type=jnp.float32)
+        attended = attended.reshape(group_rows, q_width).astype(BF)
+        part = dot(attended, attn[:, o_at:], NT).astype(BF)
+        middle = hidden + scatter_rows(part.reshape(nctx, rows_here, model_width), nz)
+
+        moe_in = rms_norm(middle, moe_gain).astype(BF)
+        moved, moe_all, gate_act, up_act = experts_forward(moe_in, share, mats_all, layer, nz)
+        records.append((hidden, normed_all, queries, keys, values, probs, attended, middle, moe_all, gate_act, up_act))
+        hidden = middle + moved
+
+    output = hidden.astype(BF)
+    grad = cotangent[0].astype(jnp.float32)
+    collected = [None] * LAYERS
+    for layer in reversed(range(LAYERS)):
+        attn, attn_gain, moe_gain, share = fetched[layer]
+        hidden, normed_all, queries, keys, values, probs, attended, middle, moe_all, gate_act, up_act = records[layer]
+        grad_moe_in, grad_all, d_gate, d_up, inner = experts_backward(grad.astype(BF), share, mats_all, layer, gate_act, up_act, nz)
+        through, grad_moe_gain = norm_back(middle, moe_gain, grad_moe_in)
+        grad_middle = grad + through
+
+        middle_all = gather_rows(grad_middle.astype(BF), nz).reshape(group_rows, model_width)
+        grad_att = dot(middle_all, attn[:, o_at:], NN).astype(BF).reshape(group_rows, 3, HEAD_DIM)
+        dp = jnp.einsum("qhd,kd->hqk", grad_att, values, preferred_element_type=jnp.float32)
+        delta = jnp.sum(probs * dp, axis=-1, keepdims=True)
+        d_scores = (probs * (dp - delta)).astype(BF)
+        dq = jnp.einsum("hqk,kd->qhd", d_scores, keys, preferred_element_type=jnp.float32) * score_scale
+        dk = jnp.einsum("hqk,qhd->kd", d_scores, queries, preferred_element_type=jnp.float32) * score_scale
+        dv = jnp.einsum("hqk,qhd->kd", probs.astype(BF), grad_att, preferred_element_type=jnp.float32)
+        back = turn(jnp.concatenate([dq, dk[:, None]], axis=1), cos_part, -sin_part)
+        d_proj = jnp.concatenate([back.reshape(group_rows, v_at), dv], axis=1).astype(BF)
+        part = dot(d_proj, attn[:, :o_at], NT).astype(BF)
+        grad_normed = scatter_rows(part.reshape(nctx, rows_here, model_width), nz)
+        through, grad_attn_gain = norm_back(hidden, attn_gain, grad_normed)
+        grad = grad_middle + through
+
+        extra = jnp.stack([grad_attn_gain, grad_moe_gain]).reshape(2, nctx, nfs // NCORE, NCORE, rows)
+        extra = jnp.pad(extra.transpose(3, 2, 1, 0, 4), ((0, 0), (0, 0), (0, 0), (0, 6), (0, 128 - rows)))
+        flat = [part.reshape(group_rows, -1) for part in (moe_all, d_gate, d_up, grad_all, inner)]
+        collected[layer] = collect_grads(nctx, nfs, normed_all, d_proj, middle_all, attended, *flat, extra)
+
+    def attn_part(low, high):
+        return jnp.stack(
+            [
+                c[0][:, 0, :, low:high].transpose(1, 0, 2).reshape(c[0].shape[2], -1).astype(F32)
+                for c in collected
+            ]
+        )
+
+    def expert_part(first):
+        return jnp.stack(
+            [
+                c[0][:, first : first + 2].reshape((EXPERTS,) + c[0].shape[2:]).astype(F32)
+                for c in collected
+            ]
+        )
+
+    def gain_part(kind):
+        return jnp.stack([jnp.sum(c[1][:, kind, :rows], axis=0) for c in collected])
+
+    return (
+        output[None],
+        grad[None],
+        attn_part(0, kv_at),
+        attn_part(kv_at, v_at),
+        attn_part(v_at, o_at),
+        attn_part(o_at, o_at + q_width),
+        gain_part(0),
+        gain_part(1),
+        expert_part(1),
+        expert_part(3),
+        expert_part(5),
+    )
+
+
 def solution(mesh):
     placed = (
         P("fsdp", "ctx", None),
@@ -677,8 +1807,10 @@
         P(None, None, ("ctx", "fsdp"), None),
         P(None, None, ("ctx", "fsdp"), None),
     )
+    nctx, nfs = mesh.shape["ctx"], mesh.shape["fsdp"]
+    chosen = partial(fast_body, nctx, nfs) if (nctx, nfs) == (8, 4) else body
     return jax.shard_map(
-        body,
+        chosen,
         mesh=mesh,
         in_specs=placed,
         out_specs=(

time: 4450 us -> 1120 us (0.25)
  waiting for transfers between devices: 2670 us -> 0 us
  Pallas kernels: 0 us -> 925 us
  blocking collectives: 636 us -> 0 us
  local copies, waits for them, and re-layouts: 491 us -> 46.3 us
  matrix products: 313 us -> 83.6 us
  other arithmetic: 201 us -> 58.7 us
  starting transfers between devices: 91.7 us -> 0 us
    all_to_all x14 -> x0, waiting for transfers between devices: 995 us -> none  [the longest x4 602 us: send_back(): lax.all_to_all(parts.astype(jnp.bfloat16), 'ctx', split_axis=1, concat_ax...]
    pallas_call x0 -> x15, Pallas kernels: none -> 925 us  [the longest x2 212 us: collect_grads(): pl.pallas_call(functools.partial(grads_kernel, nctx, nfs, rows), out_shap...]
    reduce_scatter x14 -> x0, waiting for transfers between devices: 899 us -> none  [the longest x2 280 us: layer_backward(): lax.psum_scatter(grad_out_full, ('ctx', 'fsdp'), scatter_dimension=0, til...]
    all_gather x18 -> x0, waiting for transfers between devices: 661 us -> none  [the longest x2 285 us: fetch_layer(): lax.all_gather(query_weight[layer_index].astype(jnp.bfloat16), ('ctx', 'f...]
    all_to_all x6 -> x0, blocking collectives: 551 us -> none  [the longest x1 172 us: send_out(): return lax.all_to_all(slots, 'ctx', split_axis=0, concat_axis=1, tiled=True)]
    dot_general x78 -> x18, matrix products: 313 us -> 63.9 us  [the longest x2 17.4 us: fast_body(): jnp.einsum('qhd,kd->hqk', grad_att, values, preferred_element_type=jnp.fl...]
    convert_element_type x19 -> x30, local copies, waits for them, and re-layouts: 180 us -> 16.6 us  [the longest x8 7.31 us: columns(): low = master[layer].astype(BF).reshape(rows, nctx, -1)]
    unnamed x40 -> x0, waiting for transfers between devices: 114 us -> none
  transfers between devices with their start and end apart: 50 -> 0, of which waited for: 35 -> 0; matrix products, arithmetic and copies ran while one was open for 16% -> 0% of each run, Pallas kernels for 0% -> 0%
where the time goes in v2:
time: 1120 us
  Pallas kernels  925 us (83%)
  matrix products  83.6 us (7%)
  other arithmetic  58.7 us (5%)
  local copies, waits for them, and re-layouts  46.3 us (4%)
    pallas_call x2, Pallas kernels, collect_grads(): pl.pallas_call(functools.partial(grads_kernel, nctx, nfs, rows), out_shap...  212 us
    pallas_call x1, Pallas kernels, spread_weights(): pl.pallas_call(functools.partial(weights_kernel, nctx, nfs, rows), out_sh...  161 us
    pallas_call x2, Pallas kernels, experts_backward(): pl.pallas_call(functools.partial(experts_back_kernel, nz, layer), out_sha...  150 us
    pallas_call x2, Pallas kernels, experts_forward(): pl.pallas_call(functools.partial(experts_kernel, nz, layer), out_shape=(j...  138 us
    pallas_call x4, Pallas kernels, scatter_rows(): pl.pallas_call(functools.partial(scatter_kernel, nz), out_shape=jax.Shape...  137 us
    pallas_call x4, Pallas kernels, gather_rows(): pl.pallas_call(functools.partial(gather_kernel, nz), out_shape=jax.ShapeD...  127 us

profile of v2, /device:TPU:11, one launch (start us, length us, event | category | flops | bytes accessed | tf_op | source)
XLA Modules:
  0.0 1116.6 jit_solution(13027644699045027649)
XLA Ops:
  0.7 2.3 convert.129
  4.2 1.2 fusion.114
  6.7 1.3 fusion.113
  11.7 1.8 maximum_bitcast_fusion.1
  13.5 1.8 convert_element_type.383
  15.3 1.8 convert_element_type.380
  17.0 1.8 copy_bitcast_fusion.2
  18.9 1.6 convert_element_type.382
  20.4 1.6 convert_element_type.381
  23.0 1.2 maximum_bitcast_fusion.2
  24.2 1.6 maximum_bitcast_fusion
  26.7 161.5 %spread_weights.1 = (bf16[2,7,1536,512]{3,2,1,0:T(8,128)(2,1)}, f32[32,16,128]{2,1,0:T(8,128)S(1)}) custom-call(bf16[2,8,7,48,512]{4,3,2,1,0:T(8,128)(2,1)S(1)} %pad_maximum_fusion.w_ref, f32[8,16,128]{2,1,0:T(8,128)S(1)} %pad_maximum_fusion.9.g_ref), custom_call_target="tpu_custom_call" | custom-call | tf_op jit(solution)/shard_map/spread_weights/pallas_call | solution.py:1420
  188.2 3.3 slice_bitcast_fusion
  191.7 1.3 slice_bitcast_fusion.2
  194.1 37.6 %gather_rows.4 = bf16[8,128,1536]{2,1,0:T(8,128)(2,1)S(1)} custom-call(bf16[128,1536]{1,0:T(8,128)(2,1)S(1)} %fusion.62.x_ref), custom_call_target="tpu_custom_call" | custom-call | tf_op jit(solution)/shard_map/gather_rows/pallas_call | solution.py:921
  231.7 2.3 fusion.60
  234.5 2.0 compare_and_fusion
  236.5 1.3 slice.296
  239.3 8.5 fusion.122
  247.8 5.9 fusion.30
  253.7 1.3 convolution_convert_fusion.1
  255.1 34.8 %scatter_rows.4 = f32[128,1536]{1,0:T(8,128)S(1)} custom-call(bf16[8,128,1536]{2,1,0:T(8,128)(2,1)S(1)} %bitcast.267), custom_call_target="tpu_custom_call" | custom-call | tf_op jit(solution)/shard_map/scatter_rows/pallas_call | solution.py:945
  291.1 67.6 %experts_forward.2 = (f32[128,1536]{1,0:T(8,128)}, bf16[8,128,1536]{2,1,0:T(8,128)(2,1)}, bf16[8,128,1024]{2,1,0:T(8,128)(2,1)}, bf16[8,128,1024]{2,1,0:T(8,128)(2,1)}) custom-call(bf16[128,1536]{1,0:T(8,128)(2,1)} %multiply_convert_fusion.2.x_ref, f32[8,128,2]{2,1,0:T(8,128)} %get-tuple-element.119.share_ref, ...), custom_call_target="tpu_custom_call" | custom-call | tf_op jit(solution)/shard_map/experts_forward/pallas_call | solution.py:1019
  358.7 1.4 multiply_reduce_fusion.7
  360.3 36.7 %gather_rows.5 = bf16[8,128,1536]{2,1,0:T(8,128)(2,1)S(1)} custom-call(bf16[128,1536]{1,0:T(8,128)(2,1)S(1)} %multiply_convert_fusion.1.x_ref), custom_call_target="tpu_custom_call" | custom-call | tf_op jit(solution)/shard_map/gather_rows/pallas_call | solution.py:921
  397.1 1.2 fusion.57
  401.2 11.2 %fusion.123 = (f32[3,1024]{1,0:T(4,128)}, f32[3,1024,1024]{1,2,0:T(8,128)}) fusion(pred[1024,1024]{0,1:T(8,128)(4,1)} %compare_and_fusion, bf16[1024,64,1]{0,1,2:T(8,128)(2,1)} %maximum_bitcast_fusion.4, bf16[1024,4,32]{0,2,1:T(8,128)(2,1)} %copy-done.22, bf16[1024,4,32]{0,2,1:T(8,128)(2,1)S(1)} %get-tuple-element.113), kind=kOutput, calls=%fused_computation.239 | convolution fusion | flops 416023552 | bytes 14299136 | tf_op jit(solution)/shard_map/sub | solution.py:1716
  412.4 5.8 fusion.33
  418.2 1.3 convolution_convert_fusion
  419.5 36.7 %scatter_rows.5 = f32[128,1536]{1,0:T(8,128)S(1)} custom-call(bf16[8,128,1536]{2,1,0:T(8,128)(2,1)S(1)} %bitcast.268), custom_call_target="tpu_custom_call" | custom-call | tf_op jit(solution)/shard_map/scatter_rows/pallas_call | solution.py:945
  457.4 70.9 %experts_forward.3 = (f32[128,1536]{1,0:T(8,128)}, bf16[8,128,1536]{2,1,0:T(8,128)(2,1)}, bf16[8,128,1024]{2,1,0:T(8,128)(2,1)}, bf16[8,128,1024]{2,1,0:T(8,128)(2,1)}) custom-call(bf16[128,1536]{1,0:T(8,128)(2,1)} %multiply_convert_fusion.x_ref, f32[8,128,2]{2,1,0:T(8,128)} %get-tuple-element.118.share_ref, bf16[2,7,1536,512]{3,2,1,0:T(8,128)(2,1)} %get-tuple-element.36.mats_ref), custom_call_target="tpu_custom_call" | custom-call | tf_op jit(solution)/shard_map/experts_forward/pallas_call | solution.py:1019
  528.2 75.1 %experts_backward.2 = (f32[128,1536]{1,0:T(8,128)}, bf16[8,128,1536]{2,1,0:T(8,128)(2,1)}, bf16[8,128,1024]{2,1,0:T(8,128)(2,1)}, bf16[8,128,1024]{2,1,0:T(8,128)(2,1)}, bf16[8,128,1024]{2,1,0:T(8,128)(2,1)}) custom-call(bf16[128,1536]{1,0:T(8,128)(2,1)} %bitcast.277, f32[8,128,2]{2,1,0:T(8,128)} %get-tuple-element.118.share_ref, ...), custom_call_target="tpu_custom_call" | custom-call | tf_op jit(solution)/shard_map/experts_backward/pallas_call | solution.py:1122
  603.4 2.0 multiply_reduce_fusion
  605.4 1.5 fusion.106.x_ref
  607.0 26.0 %gather_rows.6 = bf16[8,128,1536]{2,1,0:T(8,128)(2,1)S(1)} custom-call(bf16[128,1536]{1,0:T(8,128)(2,1)S(1)} %fusion.106.x_ref), custom_call_target="tpu_custom_call" | custom-call | tf_op jit(solution)/shard_map/gather_rows/pallas_call | solution.py:921
  633.0 1.7 copy-done.2
  634.7 1.4 convolution_convert_fusion.5
  636.8 6.6 fusion.50
  644.3 11.7 %fusion.5 = (f32[3,1024]{1,0:T(4,128)S(1)}, f32[1024,1024,3]{1,0,2:T(8,128)}) fusion(f32[3,1024,1024]{1,2,0:T(8,128)} %get-tuple-element.138, f32[3,1024]{1,0:T(4,128)S(1)} %copy-done.53, bf16[1024,3,64]{0,2,1:T(8,128)(2,1)} %bitcast.318, f32[1024,320]{0,1:T(8,128)} %copy-done.34), kind=kOutput, calls=%fused_computation.9 | convolution fusion | flops 412087296 | bytes 25714688 | tf_op jit(solution)/shard_map/qhd,kd->hqk/dot_general | solution.py:1740
  656.0 6.7 fusion.7
  662.8 2.0 fusion.49
  667.0 2.0 copy.132
  669.1 3.3 convolution_convert_fusion.3
  672.5 34.2 %scatter_rows.6 = f32[128,1536]{1,0:T(8,128)S(1)} custom-call(bf16[8,128,1536]{2,1,0:T(8,128)(2,1)S(1)} %bitcast.269), custom_call_target="tpu_custom_call" | custom-call | tf_op jit(solution)/shard_map/scatter_rows/pallas_call | solution.py:945
  707.1 1.6 fusion.108
  708.7 74.5 %experts_backward.3 = (f32[128,1536]{1,0:T(8,128)}, bf16[8,128,1536]{2,1,0:T(8,128)(2,1)}, bf16[8,128,1024]{2,1,0:T(8,128)(2,1)}, bf16[8,128,1024]{2,1,0:T(8,128)(2,1)}, bf16[8,128,1024]{2,1,0:T(8,128)(2,1)}) custom-call(bf16[128,1536]{1,0:T(8,128)(2,1)} %get-tuple-element.77.x_ref, f32[8,128,2]{2,1,0:T(8,128)} %get-tuple-element.119.share_ref, ...), custom_call_target="tpu_custom_call" | custom-call | tf_op jit(solution)/shard_map/experts_backward/pallas_call | solution.py:1122
  783.2 2.0 multiply_reduce_fusion.2
  785.2 2.4 fusion.107
  787.6 26.5 %gather_rows.7 = bf16[8,128,1536]{2,1,0:T(8,128)(2,1)S(1)} custom-call(bf16[128,1536]{1,0:T(8,128)(2,1)S(1)} %get-tuple-element.75.x_ref), custom_call_target="tpu_custom_call" | custom-call | tf_op jit(solution)/shard_map/gather_rows/pallas_call | solution.py:921
  814.1 1.6 copy-done.3
  815.7 1.4 convolution_convert_fusion.4
  817.1 6.6 fusion.53
  824.6 5.7 fusion.2
  830.3 6.6 fusion.4
  837.0 2.0 fusion.47
  840.6 2.8 convolution_convert_fusion.2
  843.5 31.5 %scatter_rows.7 = f32[128,1536]{1,0:T(8,128)S(1)} custom-call(bf16[8,128,1536]{2,1,0:T(8,128)(2,1)S(1)} %bitcast.270), custom_call_target="tpu_custom_call" | custom-call | tf_op jit(solution)/shard_map/scatter_rows/pallas_call | solution.py:945
  880.0 120.7 %collect_grads.3 = (bf16[8,7,48,512]{3,2,1,0:T(8,128)(2,1)}, f32[8,8,128]{2,1,0:T(8,128)}) custom-call(bf16[1024,1536]{1,0:T(8,128)(2,1)} %bitcast.262, bf16[1024,320]{1,0:T(8,128)(2,1)} %pad_maximum_fusion.1.dproj_ref, bf16[1024,1536]{1,0:T(8,128)(2,1)} %bitcast.264, bf16[1024,192]{1,0:T(8,128)(2,1)} %copy.145.attended_ref, bf16[1024,1536]{1,0:T(8,128)(2,1)} %bitcast.279, ...), custom_call_target="tpu_custom_call" | custom-call | tf_op jit(solution)/shard_map/collect_grads/pallas_call | solution.py:1586
  1005.8 91.1 %collect_grads.2 = (bf16[8,7,48,512]{3,2,1,0:T(8,128)(2,1)}, f32[8,8,128]{2,1,0:T(8,128)}) custom-call(bf16[1024,1536]{1,0:T(8,128)(2,1)} %bitcast.260, bf16[1024,320]{1,0:T(8,128)(2,1)} %pad_maximum_fusion.2.dproj_ref, bf16[1024,1536]{1,0:T(8,128)(2,1)} %bitcast.266, bf16[1024,192]{1,0:T(8,128)(2,1)} %copy.141.attended_ref, bf16[1024,1536]{1,0:T(8,128)(2,1)} %bitcast.278, ...), custom_call_target="tpu_custom_call" | custom-call | tf_op jit(solution)/shard_map/collect_grads/pallas_call | solution.py:1586
  1098.3 1.9 maximum_convert_fusion.3
  1103.3 1.5 maximum_convert_fusion.5
  1110.6 1.9 maximum_convert_fusion
  1112.5 1.9 maximum_convert_fusion.1
  1114.3 1.9 maximum_convert_fusion.2
  (271 shorter events, 43.0 us)
Async XLA Ops:
  0.6 3.3 copy-start.14
  3.9 2.5 copy-start.15
  6.7 2.2 copy-start.37
  6.7 3.2 copy-start.41
  7.9 2.7 copy-start.42
  188.1 5.6 copy-start.4
  191.4 62.3 %copy-start.7 = (bf16[1536,512]{1,0:T(8,128)(2,1)}, bf16[1536,512]{1,0:T(8,128)(2,1)S(1)}, u32[]{:S(2)}) copy-start(bf16[1536,512]{1,0:T(8,128)(2,1)S(1)} %get-tuple-element.88) | copy-start | bytes 4718596
  193.7 40.3 %copy-start.43 = (f32[1536]{0:T(1024)}, f32[1536]{0:T(1024)S(1)}, u32[]{:S(2)}) copy-start(f32[1536]{0:T(1024)S(1)} %mul.406) | copy-start | bytes 18436
  193.9 40.1 %copy-start.60 = (f32[128]{0:T(128)}, f32[128]{0:T(128)S(1)}, u32[]{:S(2)}) copy-start(f32[128]{0:T(128)S(1)} %add_rsqrt_fusion.3) | copy-start | bytes 1540
  231.7 2.4 copy-start
  231.7 2.4 copy-start.69
  231.7 2.6 copy-start.66
  239.1 8.7 copy-start.30
  239.2 8.6 copy-start.18
  239.2 8.6 copy-start.20
  239.2 8.6 copy-start.38
  247.8 5.9 copy-start.51
  253.7 36.2 %copy-start.25 = (bf16[64,3,1024]{2,0,1:T(8,128)(2,1)}, bf16[64,3,1024]{2,0,1:T(8,128)(2,1)S(1)}, u32[]{:S(2)}) copy-start(bf16[64,3,1024]{2,0,1:T(8,128)(2,1)S(1)} %fusion.30) | copy-start | bytes 1179652
  290.2 68.5 %copy-start.58 = (f32[128]{0:T(128)}, f32[128]{0:T(128)S(1)}, u32[]{:S(2)}) copy-start(f32[128]{0:T(128)S(1)} %add_rsqrt_fusion.2) | copy-start | bytes 1540
  358.7 38.4 %copy-start.9 = (bf16[1536,512]{1,0:T(8,128)(2,1)S(1)}, bf16[1536,512]{1,0:T(8,128)(2,1)}, u32[]{:S(2)}) copy-start(bf16[1536,512]{1,0:T(8,128)(2,1)} %get-tuple-element.87) | copy-start | bytes 4718596
  360.2 38.2 %copy-start.45 = (f32[1536]{0:T(1024)}, f32[1536]{0:T(1024)S(1)}, u32[]{:S(2)}) copy-start(f32[1536]{0:T(1024)S(1)} %mul.432) | copy-start | bytes 18436
  360.2 38.2 %copy-start.62 = (f32[128]{0:T(128)}, f32[128]{0:T(128)S(1)}, u32[]{:S(2)}) copy-start(f32[128]{0:T(128)S(1)} %add_rsqrt_fusion.1) | copy-start | bytes 1540
  397.1 1.7 copy-start.1
  397.1 1.8 copy-start.31
  419.5 36.9 %copy-start.47 = (f32[32,48]{1,0:T(8,128)S(1)}, f32[32,48]{1,0:T(8,128)}, u32[]{:S(2)}) copy-start(f32[32,48]{1,0:T(8,128)} %get-tuple-element.67) | copy-start | bytes 18436
  456.5 148.9 %copy-start.56 = (f32[128]{0:T(128)}, f32[128]{0:T(128)S(1)}, u32[]{:S(2)}) copy-start(f32[128]{0:T(128)S(1)} %add_rsqrt_fusion) | copy-start | bytes 1540
  528.2 77.2 %copy-start.11 = (bf16[1,128,1536]{2,1,0:T(8,128)(2,1)S(1)}, bf16[1,128,1536]{2,1,0:T(8,128)(2,1)}, u32[]{:S(2)}) copy-start(bf16[1,128,1536]{2,1,0:T(8,128)(2,1)} %param.16) | copy-start | bytes 1179652
  605.4 29.3 %copy-start.10 = (bf16[1536,512]{1,0:T(8,128)(2,1)S(1)}, bf16[1536,512]{1,0:T(8,128)(2,1)}, u32[]{:S(2)}) copy-start(bf16[1536,512]{1,0:T(8,128)(2,1)} %get-tuple-element.87) | copy-start | bytes 4718596
  605.4 30.7 %copy-start.64 = (f32[128]{0:T(128)}, f32[128]{0:T(128)S(1)}, u32[]{:S(2)}) copy-start(f32[128]{0:T(128)S(1)} %broadcast_multiply_fusion.3) | copy-start | bytes 1540
  606.9 29.9 %copy-start.53 = (f32[3,1024]{1,0:T(4,128)S(1)}, f32[3,1024]{1,0:T(4,128)}, u32[]{:S(2)}) copy-start(f32[3,1024]{1,0:T(4,128)} %get-tuple-element.137) | copy-start | bytes 36868
  633.0 1.7 copy-start.2
  644.3 11.7 %slice-start = ((s8[12582912]{0:T(1024)(128)(4,1)}), s8[4194304]{0:T(1024)(128)(4,1)S(1)}, s32[]{:S(2)}) async-start(s8[12582912]{0:T(1024)(128)(4,1)} %bitcast.272), calls=%async_computation | async-start | bytes 8388608
  644.3 11.7 %slice-start.1 = ((s8[12582912]{0:T(1024)(128)(4,1)}), s8[4194304]{0:T(1024)(128)(4,1)S(1)}, s32[]{:S(2)}) async-start(s8[12582912]{0:T(1024)(128)(4,1)} %bitcast.272), calls=%async_computation.1 | async-start | bytes 8388608
  644.3 11.7 %slice-start.2 = ((s8[12582912]{0:T(1024)(128)(4,1)}), s8[4194304]{0:T(1024)(128)(4,1)S(1)}, s32[]{:S(2)}) async-start(s8[12582912]{0:T(1024)(128)(4,1)} %bitcast.272), calls=%async_computation.2 | async-start | bytes 8388608
  656.0 6.8 copy-start.23
  662.8 2.0 copy-start.40
  672.4 34.3 %copy-start.46 = (f32[1536]{0:T(1024)S(1)}, f32[1536]{0:T(1024)}, u32[]{:S(2)}) copy-start(f32[1536]{0:T(1024)} %copy-done.45) | copy-start | bytes 18436
  672.5 34.3 %copy-start.63 = (f32[128]{0:T(128)S(1)}, f32[128]{0:T(128)}, u32[]{:S(2)}) copy-start(f32[128]{0:T(128)} %copy-done.62) | copy-start | bytes 1540
  672.5 34.6 %copy-start.6 = (f32[128,1536]{1,0:T(8,128)S(1)}, f32[128,1536]{1,0:T(8,128)}, u32[]{:S(2)}) copy-start(f32[128,1536]{1,0:T(8,128)} %get-tuple-element.41) | copy-start | bytes 2359300
  672.5 34.6 %copy-start.35 = (f32[128,1536]{1,0:T(8,128)S(1)}, f32[128,1536]{1,0:T(8,128)}, u32[]{:S(2)}) copy-start(f32[128,1536]{1,0:T(8,128)} %get-tuple-element.38) | copy-start | bytes 2359300
  672.5 34.6 %copy-start.57 = (f32[128]{0:T(128)S(1)}, f32[128]{0:T(128)}, u32[]{:S(2)}) copy-start(f32[128]{0:T(128)} %copy-done.56) | copy-start | bytes 1540
  672.5 34.6 %copy-start.65 = (f32[128]{0:T(128)S(1)}, f32[128]{0:T(128)}, u32[]{:S(2)}) copy-start(f32[128]{0:T(128)} %copy-done.64) | copy-start | bytes 1540
  708.7 74.5 %copy-start.59 = (f32[128]{0:T(128)S(1)}, f32[128]{0:T(128)}, u32[]{:S(2)}) copy-start(f32[128]{0:T(128)} %copy-done.58) | copy-start | bytes 1540
  708.7 76.5 %copy-start.17 = (f32[128,1536]{1,0:T(8,128)S(1)}, f32[128,1536]{1,0:T(8,128)}, u32[]{:S(2)}) copy-start(f32[128,1536]{1,0:T(8,128)} %get-tuple-element.78) | copy-start | bytes 2359300
  785.2 30.5 %copy-start.8 = (bf16[1536,512]{1,0:T(8,128)(2,1)S(1)}, bf16[1536,512]{1,0:T(8,128)(2,1)}, u32[]{:S(2)}) copy-start(bf16[1536,512]{1,0:T(8,128)(2,1)} %copy-done.7) | copy-start | bytes 4718596
  787.6 29.5 %copy-start.52 = (f32[3,1024]{1,0:T(4,128)S(1)}, f32[3,1024]{1,0:T(4,128)}, u32[]{:S(2)}) copy-start(f32[3,1024]{1,0:T(4,128)} %copy-done.51) | copy-start | bytes 36868
  814.1 1.6 copy-start.3
  830.3 6.7 copy-start.19
  830.3 6.7 copy-start.21
  837.0 2.0 copy-start.39
  843.4 31.6 %copy-start.5 = (bf16[1,128,1536]{2,1,0:T(8,128)(2,1)S(1)}, bf16[1,128,1536]{2,1,0:T(8,128)(2,1)}, u32[]{:S(2)}) copy-start(bf16[1,128,1536]{2,1,0:T(8,128)(2,1)} %param.15) | copy-start | bytes 1179652
  843.4 31.6 %copy-start.44 = (f32[1536]{0:T(1024)S(1)}, f32[1536]{0:T(1024)}, u32[]{:S(2)}) copy-start(f32[1536]{0:T(1024)} %copy-done.43) | copy-start | bytes 18436
  843.4 31.6 %copy-start.61 = (f32[128]{0:T(128)S(1)}, f32[128]{0:T(128)}, u32[]{:S(2)}) copy-start(f32[128]{0:T(128)} %copy-done.60) | copy-start | bytes 1540
  843.4 32.5 %copy-start.16 = (f32[128,1536]{1,0:T(8,128)S(1)}, f32[128,1536]{1,0:T(8,128)}, u32[]{:S(2)}) copy-start(f32[128,1536]{1,0:T(8,128)} %get-tuple-element.76) | copy-start | bytes 2359300
  843.5 33.6 %copy-start.24 = (bf16[1024,256]{1,0:T(8,128)(2,1)S(1)}, bf16[1024,256]{1,0:T(8,128)(2,1)}, u32[]{:S(2)}) copy-start(bf16[1024,256]{1,0:T(8,128)(2,1)} %copy.132) | copy-start | bytes 1572868
  843.5 33.6 %copy-start.32 = (bf16[1024,64]{1,0:T(8,128)(2,1)S(1)}, bf16[1024,64]{1,0:T(8,128)(2,1)}, u32[]{:S(2)}) copy-start(bf16[1024,64]{1,0:T(8,128)(2,1)} %copy.133) | copy-start | bytes 393220
  875.1 3.0 copy-start.28
  875.1 4.0 copy-start.48
  880.0 122.8 %copy-start.33 = (bf16[1024,64]{1,0:T(8,128)(2,1)S(1)}, bf16[1024,64]{1,0:T(8,128)(2,1)}, u32[]{:S(2)}) copy-start(bf16[1024,64]{1,0:T(8,128)(2,1)} %copy.138) | copy-start | bytes 393220
  1000.7 3.1 copy-start.26
  1000.7 4.1 copy-start.49
  1000.8 4.2 copy-start.50
  1098.1 12.0 %copy-start.12 = (bf16[8,7,48,512]{3,2,1,0:T(8,128)(2,1)S(1)}, bf16[8,7,48,512]{3,2,1,0:T(8,128)(2,1)}, u32[]{:S(2)}) copy-start(bf16[8,7,48,512]{3,2,1,0:T(8,128)(2,1)} %get-tuple-element.56) | copy-start | bytes 8257540
  1106.3 4.1 copy-start.13
  (10 other events, 9.5 us)

commit v3 on v2

--- a/solution.py
+++ b/solution.py
@@ -1450,7 +1450,7 @@
     y_mate = (1 - y) * NCORE + core
     c_mate = y * NCORE + 1 - core
     mats = mine.shape[0]
-    proj = dproj_ref.shape[1]
+    proj = mine.shape[2] - attended_ref.shape[1]
     units = dgate_ref.shape[1] // 2
     slab = NX * nfs * rows
     barrier = pltpu.get_barrier_semaphore()
@@ -1494,7 +1494,7 @@
     def compute(row):
         lanes = pl.ds(pl.multiple_of(row * slab, 128), slab)
         tall = pl.ds(pl.multiple_of(row * slab, 16), slab)
-        mine[0, tall, pl.ds(0, proj)] = dot(normed_ref[:, lanes], dproj_ref[...], TN).astype(BF)
+        mine[0, tall, pl.ds(0, proj)] = dot(normed_ref[:, lanes], dproj_ref[...], TN)[:, :proj].astype(BF)
         mine[0, tall, pl.ds(proj, mine.shape[2] - proj)] = dot(middle_ref[:, lanes], attended_ref[...], TN).astype(BF)
         moe = moe_ref[:, lanes]
         for e in range(2):
@@ -1580,7 +1580,7 @@
 def collect_grads(nctx, nfs, normed, dproj, middle, attended, moe, dgate, dup, grad, inner, extra):
     width = normed.shape[1]
     rows = width // (nctx * nfs)
-    mats, cols = 7, dproj.shape[1] + attended.shape[1]
+    mats, cols = 7, dgate.shape[1] // 2
     blk = (mats, rows, cols)
     tile = extra.shape[3:]
     return pl.pallas_call(
@@ -1612,6 +1612,273 @@
     )(normed, dproj, middle, attended, moe, dgate, dup, grad, inner, extra)
 
 
+def spin(values, cos_part, sin_part):
+    lane = lax.broadcasted_iota(jnp.int32, values.shape, 1) % HEAD_DIM
+    half_dim = HEAD_DIM // 2
+    swapped = jnp.where(
+        lane < half_dim,
+        pltpu.roll(values, values.shape[1] - half_dim, 1),
+        pltpu.roll(values, half_dim, 1),
+    )
+    return values * cos_part + swapped * sin_part
+
+
+def attention_kernel(nz, layer, x_ref, mats_ref, cos_ref, sin_ref, key_at_ref, query_at_ref,
+                     o_ref, all_out, q_ref, k_ref, v_ref, peak_ref, share_ref, att_ref,
+                     attn, out_w, blocks, part, v_turned, probs, load_sem, save_sem, gsems, work, ssems):
+    line = Line(nz)
+    rows, width = x_ref.shape
+    pair_rows = NX * rows
+    heads = q_ref.shape[1] // rows
+    o_at = (heads + 2) * HEAD_DIM
+    wide = -(-o_at // 128) * 128
+    load = pltpu.make_async_copy(mats_ref.at[layer, 0], attn, load_sem)
+    load.start()
+    line.greet()
+    ring = Gather(line, x_ref, blocks, gsems)
+    ring.start()
+    blocks[line.ctx] = x_ref[...]
+    load.wait()
+    out_w[...] = attn[:, o_at:]
+
+    def save(row):
+        pair = pl.ds(row * NX, NX)
+        return pltpu.make_async_copy(blocks.at[pair], all_out.at[pair], save_sem.at[row])
+
+    def project(i, carry):
+        @pl.when(i < nz - 1)
+        def _():
+            ring.forward(i)
+
+        row = line.near(i)
+        ring.wait_pair(row)
+        pair = pl.ds(row * NX, NX)
+        tall = pl.ds(pl.multiple_of(row * pair_rows, pair_rows), pair_rows)
+        block = blocks[pair].reshape(pair_rows, width)
+        save(row).start()
+        proj = dot(block, attn[:, :wide], NN)
+        cos_part, sin_part = cos_ref[tall, :], sin_ref[tall, :]
+        first = spin(proj[:, :128], cos_part, sin_part)
+        second = spin(proj[:, 128:256], cos_part, sin_part)
+        values = proj[:, 256 : 256 + HEAD_DIM]
+        for side in range(NX):
+            at = slice(side * rows, (side + 1) * rows)
+            q_ref[row * NX + side, 0:rows, :] = first[at, :HEAD_DIM].astype(BF)
+            q_ref[row * NX + side, rows : 2 * rows, :] = first[at, HEAD_DIM:].astype(BF)
+            q_ref[row * NX + side, 2 * rows : 3 * rows, :] = second[at, :HEAD_DIM].astype(BF)
+        k_ref[tall, :] = second[:, HEAD_DIM:].astype(BF)
+        v_ref[tall, :] = values.astype(BF)
+        v_turned[:, tall] = values.T.astype(BF)
+        return carry
+
+    lax.fori_loop(0, nz, project, 0)
+    ring.finish()
+    sums = Scatter(line, part, o_ref, work, ssems)
+
+    def attend(at):
+        scores = dot(k_ref[...], q_ref[at], NT)
+        key_at = key_at_ref[...]
+        visible = (key_at >= query_at_ref[at, 0:1, :]) & (key_at <= query_at_ref[at, 1:2, :])
+        for head in range(heads):
+            lanes = slice(head * rows, (head + 1) * rows)
+            raw = jnp.where(visible, scores[:, lanes] * HEAD_DIM**-0.5, NEGATIVE)
+            peak = jnp.max(raw, axis=0, keepdims=True)
+            powers = jnp.exp(raw - peak)
+            peak_ref[at, :, lanes] = peak
+            share_ref[at, :, lanes] = 1.0 / jnp.sum(powers, axis=0, keepdims=True)
+            probs[:, lanes] = powers.astype(BF)
+        turned = dot(v_turned[...], probs[...], NN) * share_ref[at]
+        stacked = turned.T.astype(BF)
+        for head in range(heads):
+            att_ref[at, :, head * HEAD_DIM : (head + 1) * HEAD_DIM] = stacked[head * rows : (head + 1) * rows]
+        part[at] = dot(att_ref[at], out_w[...], NT).astype(BF)
+
+    def step(i, carry):
+        row = line.far(i)
+        attend(row * NX + 1 - line.x)
+        sums.across(row).start()
+        attend(row * NX + line.x)
+
+        @pl.when(i > 0)
+        def _():
+            sums.add(i - 1)
+
+        return carry
+
+    lax.fori_loop(0, nz, step, 0)
+    sums.add(nz - 1)
+    sums.finish()
+    for row in range(nz):
+        save(row).wait()
+
+
+def attention_rows(block, mats, layer, cos_part, sin_part, key_at, query_at, nz):
+    rows, width = block.shape
+    group = nz * NX
+    group_rows = group * rows
+    heads = 3
+    return pl.pallas_call(
+        functools.partial(attention_kernel, nz, layer),
+        out_shape=(
+            jax.ShapeDtypeStruct((rows, width), F32),
+            jax.ShapeDtypeStruct((group, rows, width), BF),
+            jax.ShapeDtypeStruct((group, heads * rows, HEAD_DIM), BF),
+            jax.ShapeDtypeStruct((group_rows, HEAD_DIM), BF),
+            jax.ShapeDtypeStruct((group_rows, HEAD_DIM), BF),
+            jax.ShapeDtypeStruct((group, 1, heads * rows), F32),
+            jax.ShapeDtypeStruct((group, 1, heads * rows), F32),
+            jax.ShapeDtypeStruct((group, rows, heads * HEAD_DIM), BF),
+        ),
+        in_specs=[VM, ANY, VM, VM, VM, VM],
+        out_specs=(VM, ANY, VM, VM, VM, VM, VM, VM),
+        scratch_shapes=[
+            pltpu.VMEM(mats.shape[2:], BF),
+            pltpu.VMEM((width, heads * HEAD_DIM), BF),
+            pltpu.VMEM((group, rows, width), BF),
+            pltpu.VMEM((group, rows, width), BF),
+            pltpu.VMEM((HEAD_DIM, group_rows), BF),
+            pltpu.VMEM((group_rows, heads * rows), BF),
+            DMA,
+            DMA((nz,)),
+        ]
+        + Gather.scratch(nz)
+        + Scatter.scratch(nz, rows, width),
+        compiler_params=params(9 + 2 * layer, 60),
+        name="attention_forward",
+    )(block, mats, cos_part, sin_part, key_at, query_at)
+
+
+def attention_back_kernel(nz, layer, x_ref, mats_ref, cos_ref, sin_ref, key_at_ref, query_at_ref, q_ref, k_ref, v_ref, peak_ref, share_ref,
+                          o_ref, all_out, dproj_ref,
+                          attn, out_w, blocks, part, k_turned, probs, slopes, dq, dk, dv, load_sem, save_sem, gsems, work, ssems):
+    line = Line(nz)
+    rows, width = x_ref.shape
+    pair_rows = NX * rows
+    heads = q_ref.shape[1] // rows
+    o_at = (heads + 2) * HEAD_DIM
+    wide = dproj_ref.shape[2]
+    scale = HEAD_DIM**-0.5
+    load = pltpu.make_async_copy(mats_ref.at[layer, 0], attn, load_sem)
+    load.start()
+    line.greet()
+    ring = Gather(line, x_ref, blocks, gsems)
+    ring.start()
+    blocks[line.ctx] = x_ref[...]
+    k_turned[...] = k_ref[...].astype(F32).T.astype(BF)
+    dk[...] = jnp.zeros(dk.shape, F32)
+    dv[...] = jnp.zeros(dv.shape, F32)
+    load.wait()
+    out_w[...] = attn[:, o_at:]
+
+    def save(row):
+        pair = pl.ds(row * NX, NX)
+        return pltpu.make_async_copy(blocks.at[pair], all_out.at[pair], save_sem.at[row])
+
+    def back(at):
+        d_att = dot(blocks[at], out_w[...], NN)
+        d_heads = jnp.concatenate(
+            [d_att[:, head * HEAD_DIM : (head + 1) * HEAD_DIM] for head in range(heads)], axis=0
+        ).astype(BF)
+        scores = dot(k_ref[...], q_ref[at], NT)
+        d_probs = dot(v_ref[...], d_heads, NT)
+        key_at = key_at_ref[...]
+        visible = (key_at >= query_at_ref[at, 0:1, :]) & (key_at <= query_at_ref[at, 1:2, :])
+        for head in range(heads):
+            lanes = slice(head * rows, (head + 1) * rows)
+            raw = jnp.where(visible, scores[:, lanes] * scale, NEGATIVE)
+            prob = jnp.exp(raw - peak_ref[at, :, lanes]) * share_ref[at, :, lanes]
+            grad = d_probs[:, lanes]
+            delta = jnp.sum(prob * grad, axis=0, keepdims=True)
+            probs[:, lanes] = prob.astype(BF)
+            slopes[:, lanes] = (prob * (grad - delta)).astype(BF)
+        dv[...] += dot(probs[...], d_heads, NN)
+        dk[...] += dot(slopes[...], q_ref[at], NN)
+        stacked = dot(k_turned[...], slopes[...], NN).T * scale
+        for head in range(heads):
+            dq[at, :, head * HEAD_DIM : (head + 1) * HEAD_DIM] = stacked[head * rows : (head + 1) * rows]
+
+    def take(i, carry):
+        @pl.when(i < nz - 1)
+        def _():
+            ring.forward(i)
+
+        row = line.near(i)
+        back(row * NX + line.x)
+        ring.wait_pair(row)
+        save(row).start()
+        back(row * NX + 1 - line.x)
+        return carry
+
+    lax.fori_loop(0, nz, take, 0)
+    ring.finish()
+    sums = Scatter(line, part, o_ref, work, ssems)
+
+    def project(at):
+        tall = pl.ds(pl.multiple_of(at * rows, rows), rows)
+        cos_part, sin_part = cos_ref[tall, :], -sin_ref[tall, :]
+        block_dq = dq[at]
+        second = jnp.concatenate([block_dq[:, 128:], dk[tall, :] * scale], axis=1)
+        dproj_ref[at, :, 0:128] = spin(block_dq[:, :128], cos_part, sin_part).astype(BF)
+        dproj_ref[at, :, 128:256] = spin(second, cos_part, sin_part).astype(BF)
+        last = jnp.concatenate([dv[tall, :], jnp.zeros((rows, wide - 256 - HEAD_DIM), F32)], axis=1)
+        dproj_ref[at, :, 256:wide] = last.astype(BF)
+        part[at] = dot(dproj_ref[at], attn[:, :wide], NT).astype(BF)
+
+    def step(i, carry):
+        row = line.far(i)
+        project(row * NX + 1 - line.x)
+        sums.across(row).start()
+        project(row * NX + line.x)
+
+        @pl.when(i > 0)
+        def _():
+            sums.add(i - 1)
+
+        return carry
+
+    lax.fori_loop(0, nz, step, 0)
+    sums.add(nz - 1)
+    sums.finish()
+    for row in range(nz):
+        save(row).wait()
+
+
+def attention_rows_back(block, mats, layer, cos_part, sin_part, key_at, query_at, queries, keys, values, peaks, shares, nz):
+    rows, width = block.shape
+    group = nz * NX
+    group_rows = group * rows
+    heads = 3
+    wide = 384
+    return pl.pallas_call(
+        functools.partial(attention_back_kernel, nz, layer),
+        out_shape=(
+            jax.ShapeDtypeStruct((rows, width), F32),
+            jax.ShapeDtypeStruct((group, rows, width), BF),
+            jax.ShapeDtypeStruct((group, rows, wide), BF),
+        ),
+        in_specs=[VM, ANY] + [VM] * 9,
+        out_specs=(VM, ANY, VM),
+        scratch_shapes=[
+            pltpu.VMEM(mats.shape[2:], BF),
+            pltpu.VMEM((width, heads * HEAD_DIM), BF),
+            pltpu.VMEM((group, rows, width), BF),
+            pltpu.VMEM((group, rows, width), BF),
+            pltpu.VMEM((HEAD_DIM, group_rows), BF),
+            pltpu.VMEM((group_rows, heads * rows), BF),
+            pltpu.VMEM((group_rows, heads * rows), BF),
+            pltpu.VMEM((group, rows, heads * HEAD_DIM), F32),
+            pltpu.VMEM((group_rows, HEAD_DIM), F32),
+            pltpu.VMEM((group_rows, HEAD_DIM), F32),
+            DMA,
+            DMA((nz,)),
+        ]
+        + Gather.scratch(nz)
+        + Scatter.scratch(nz, rows, width),
+        compiler_params=params(10 + 2 * layer, 60),
+        name="attention_backward",
+    )(block, mats, cos_part, sin_part, key_at, query_at, queries, keys, values, peaks, shares)
+
+
 def rope_tables(places):
     half_dim = HEAD_DIM // 2
     freq_steps = jnp.arange(half_dim, dtype=jnp.float32)
@@ -1620,17 +1887,6 @@
     return jnp.cos(angles), jnp.sin(angles)
 
 
-def turn(values, cos_part, sin_part):
-    half_dim = HEAD_DIM // 2
-    first_half = values[..., :half_dim]
-    second_half = values[..., half_dim:]
-    cos_part, sin_part = cos_part[:, None, :], sin_part[:, None, :]
-    return jnp.concatenate(
-        [first_half * cos_part - second_half * sin_part, second_half * cos_part + first_half * sin_part],
-        axis=-1,
-    )
-
-
 def pack_weights(master_set, layer, nctx):
     query_weight, key_weight, value_weight, out_weight, attn_gain, moe_gain, gate_weight, up_weight, down_weight = master_set
     rows = query_weight.shape[1]
@@ -1668,10 +1924,16 @@
     rows_here, model_width = tokens.shape[1], tokens.shape[2]
     group_rows = rows_here * nctx
     ctx = lax.axis_index("ctx")
-    seg_all, pos_all = layout(lengths[0], tile_order[0], group_rows)
-    visible = (seg_all[:, None] == seg_all[None, :]) & (pos_all[None, :] <= pos_all[:, None])
-    cos_part, sin_part = rope_tables(pos_all.astype(jnp.float32))
-    score_scale = HEAD_DIM ** (-0.5)
+    _, pos_all = layout(lengths[0], tile_order[0], group_rows)
+    cos_half, sin_half = rope_tables(pos_all.astype(jnp.float32))
+    cos_part = jnp.concatenate([cos_half] * 4, axis=1)
+    sin_part = jnp.concatenate([-sin_half, sin_half] * 2, axis=1)
+    row_ids = jnp.arange(rows_here, dtype=jnp.int32)
+    first_at = (tile_order[0][:, None] * TILE + row_ids[None, :]).reshape(group_rows)
+    key_at = first_at[:, None]
+    query_at = jnp.stack(
+        [(first_at - pos_all).reshape(nctx, rows_here), first_at.reshape(nctx, rows_here)], axis=1
+    )
     q_width = 3 * HEAD_DIM
     kv_at, v_at, o_at = q_width, q_width + HEAD_DIM, q_width + 2 * HEAD_DIM
 
@@ -1692,7 +1954,6 @@
     )
     fetched = [
         (
-            mats_all[layer, 0],
             small_all[:, 2 * layer, :rows].reshape(-1),
             small_all[:, 2 * layer + 1, :rows].reshape(-1),
             shares[:, 8 + 2 * layer : 10 + 2 * layer].transpose(0, 2, 1),
@@ -1703,57 +1964,38 @@
     hidden = tokens[0].astype(jnp.float32)
     records = []
     for layer in range(LAYERS):
-        attn, attn_gain, moe_gain, share = fetched[layer]
+        attn_gain, moe_gain, share = fetched[layer]
         normed = rms_norm(hidden, attn_gain).astype(BF)
-        normed_all = gather_rows(normed, nz).reshape(group_rows, model_width)
-        proj = dot(normed_all, attn[:, :o_at], NN)
-        turned = turn(proj[:, :v_at].reshape(group_rows, 4, HEAD_DIM), cos_part, sin_part).astype(BF)
-        queries, keys = turned[:, :3], turned[:, 3]
-        values = proj[:, v_at:].astype(BF)
-        raw = jnp.einsum("qhd,kd->hqk", queries, keys, preferred_element_type=jnp.float32) * score_scale
-        raw = jnp.where(visible[None], raw, NEGATIVE)
-        peak = jnp.max(raw, axis=-1, keepdims=True)
-        powers = jnp.exp(raw - peak)
-        probs = powers / jnp.sum(powers, axis=-1, keepdims=True)
-        attended = jnp.einsum("hqk,kd->qhd", probs.astype(BF), values, preferred_element_type=jnp.float32)
-        attended = attended.reshape(group_rows, q_width).astype(BF)
-        part = dot(attended, attn[:, o_at:], NT).astype(BF)
-        middle = hidden + scatter_rows(part.reshape(nctx, rows_here, model_width), nz)
+        mixed, normed_all, queries, keys, values, peaks, sums, attended = attention_rows(
+            normed, mats_all, layer, cos_part, sin_part, key_at, query_at, nz
+        )
+        middle = hidden + mixed
 
         moe_in = rms_norm(middle, moe_gain).astype(BF)
         moved, moe_all, gate_act, up_act = experts_forward(moe_in, share, mats_all, layer, nz)
-        records.append((hidden, normed_all, queries, keys, values, probs, attended, middle, moe_all, gate_act, up_act))
+        records.append((hidden, normed_all, queries, keys, values, peaks, sums, attended, middle, moe_all, gate_act, up_act))
         hidden = middle + moved
 
     output = hidden.astype(BF)
     grad = cotangent[0].astype(jnp.float32)
     collected = [None] * LAYERS
     for layer in reversed(range(LAYERS)):
-        attn, attn_gain, moe_gain, share = fetched[layer]
-        hidden, normed_all, queries, keys, values, probs, attended, middle, moe_all, gate_act, up_act = records[layer]
+        attn_gain, moe_gain, share = fetched[layer]
+        hidden, normed_all, queries, keys, values, peaks, sums, attended, middle, moe_all, gate_act, up_act = records[layer]
         grad_moe_in, grad_all, d_gate, d_up, inner = experts_backward(grad.astype(BF), share, mats_all, layer, gate_act, up_act, nz)
         through, grad_moe_gain = norm_back(middle, moe_gain, grad_moe_in)
         grad_middle = grad + through
 
-        middle_all = gather_rows(grad_middle.astype(BF), nz).reshape(group_rows, model_width)
-        grad_att = dot(middle_all, attn[:, o_at:], NN).astype(BF).reshape(group_rows, 3, HEAD_DIM)
-        dp = jnp.einsum("qhd,kd->hqk", grad_att, values, preferred_element_type=jnp.float32)
-        delta = jnp.sum(probs * dp, axis=-1, keepdims=True)
-        d_scores = (probs * (dp - delta)).astype(BF)
-        dq = jnp.einsum("hqk,kd->qhd", d_scores, keys, preferred_element_type=jnp.float32) * score_scale
-        dk = jnp.einsum("hqk,qhd->kd", d_scores, queries, preferred_element_type=jnp.float32) * score_scale
-        dv = jnp.einsum("hqk,qhd->kd", probs.astype(BF), grad_att, preferred_element_type=jnp.float32)
-        back = turn(jnp.concatenate([dq, dk[:, None]], axis=1), cos_part, -sin_part)
-        d_proj = jnp.concatenate([back.reshape(group_rows, v_at), dv], axis=1).astype(BF)
-        part = dot(d_proj, attn[:, :o_at], NT).astype(BF)
-        grad_normed = scatter_rows(part.reshape(nctx, rows_here, model_width), nz)
+        grad_normed, middle_all, d_proj = attention_rows_back(
+            grad_middle.astype(BF), mats_all, layer, cos_part, sin_part, key_at, query_at, queries, keys, values, peaks, sums, nz
+        )
         through, grad_attn_gain = norm_back(hidden, attn_gain, grad_normed)
         grad = grad_middle + through
 
         extra = jnp.stack([grad_attn_gain, grad_moe_gain]).reshape(2, nctx, nfs // NCORE, NCORE, rows)
         extra = jnp.pad(extra.transpose(3, 2, 1, 0, 4), ((0, 0), (0, 0), (0, 0), (0, 6), (0, 128 - rows)))
-        flat = [part.reshape(group_rows, -1) for part in (moe_all, d_gate, d_up, grad_all, inner)]
-        collected[layer] = collect_grads(nctx, nfs, normed_all, d_proj, middle_all, attended, *flat, extra)
+        flat = [part.reshape(group_rows, -1) for part in (normed_all, d_proj, middle_all, attended, moe_all, d_gate, d_up, grad_all, inner)]
+        collected[layer] = collect_grads(nctx, nfs, *flat, extra)
 
     def attn_part(low, high):
         return jnp.stack(

time: 1120 us -> 1060 us (0.946)
  matrix products: 83.6 us -> 0 us
  Pallas kernels: 925 us -> 975 us
  local copies, waits for them, and re-layouts: 46.3 us -> 24.5 us
    dot_general x18 -> x0, matrix products: 63.9 us -> none  [the longest x2 17.4 us: fast_body(): jnp.einsum('qhd,kd->hqk', grad_att, values, preferred_element_type=jnp.fl...]
    pallas_call x8 -> x4, Pallas kernels: 264 us -> 303 us  [the longest x2 153 us: attention_rows_back(): pl.pallas_call(functools.partial(attention_back_kernel, nz, layer), out_s...]
    sub x2 -> x0, matrix products: 19.7 us -> none  [fast_body(): powers = jnp.exp(raw - peak)]
    convert_element_type x3 -> x0, other arithmetic: 13.4 us -> none  [the longest x2 13.4 us: fast_body(): d_scores = (probs * (dp - delta)).astype(BF)]
    pallas_call x2, Pallas kernels: 212 us -> 224 us  [collect_grads(): pl.pallas_call(functools.partial(grads_kernel, nctx, nfs, rows), out_shap...]
where the time goes in v3:
time: 1060 us; the launch traced here: 1050 us
  Pallas kernels  975 us (92%)
  other arithmetic  53.2 us (5%)
  local copies, waits for them, and re-layouts  24.5 us (2%)
    pallas_call x2, Pallas kernels, collect_grads(): pl.pallas_call(functools.partial(grads_kernel, nctx, nfs, rows), out_shap...  224 us
    pallas_call x1, Pallas kernels, spread_weights(): pl.pallas_call(functools.partial(weights_kernel, nctx, nfs, rows), out_sh...  161 us
    pallas_call x2, Pallas kernels, attention_rows_back(): pl.pallas_call(functools.partial(attention_back_kernel, nz, layer), out_s...  153 us
    pallas_call x2, Pallas kernels, attention_rows(): pl.pallas_call(functools.partial(attention_kernel, nz, layer), out_shape=...  150 us
    pallas_call x2, Pallas kernels, experts_backward(): pl.pallas_call(functools.partial(experts_back_kernel, nz, layer), out_sha...  148 us
    pallas_call x2, Pallas kernels, experts_forward(): pl.pallas_call(functools.partial(experts_kernel, nz, layer), out_shape=(j...  138 us

profile of v3, /device:TPU:11, one launch (start us, length us, event | category | flops | bytes accessed | tf_op | source)
XLA Modules:
  0.0 1054.4 jit_solution(3615550426052413480)
XLA Ops:
  0.7 0.9 reduce-window.4
  2.2 0.7 fusion.32
  2.9 0.7 convert.90
  3.6 0.7 convert.91
  4.3 1.2 fusion.11
  5.6 0.7 select_reduce_fusion.1
  7.2 0.7 select_reduce_fusion
  8.0 0.9 convert.84
  9.2 0.9 convert.85
  11.3 0.9 maximum_bitcast_fusion.2
  12.5 0.9 maximum_bitcast_fusion.3
  13.5 1.0 copy.93.key_at_ref
  14.5 1.9 fusion.13
  16.4 1.9 pad_maximum_fusion.1
  18.7 1.8 copy-done.9
  20.8 1.8 copy-done.10
  22.9 0.9 copy-done.12
  25.7 161.5 %spread_weights.1 = (bf16[2,7,1536,512]{3,2,1,0:T(8,128)(2,1)}, f32[32,16,128]{2,1,0:T(8,128)S(1)}) custom-call(bf16[2,8,7,48,512]{4,3,2,1,0:T(8,128)(2,1)S(1)} %pad_maximum_fusion.w_ref, f32[8,16,128]{2,1,0:T(8,128)S(1)} %pad_maximum_fusion.3.g_ref), custom_call_target="tpu_custom_call" | custom-call | tf_op jit(solution)/shard_map/spread_weights/pallas_call | solution.py:1420
  187.7 0.9 fusion.4.x_ref
  188.8 1.3 slice_bitcast_fusion
  190.1 75.8 %attention_forward.2 = (f32[128,1536]{1,0:T(8,128)}, bf16[8,128,1536]{2,1,0:T(8,128)(2,1)}, bf16[8,384,64]{2,1,0:T(8,128)(2,1)}, bf16[1024,64]{1,0:T(8,128)(2,1)...) custom-call(bf16[128,1536]{1,0:T(8,128)(2,1)} %fusion.4.x_ref, ...), custom_call_target="tpu_custom_call" | custom-call | tf_op jit(solution)/shard_map/attention_forward/pallas_call | solution.py:1720
  265.9 1.3 multiply_reduce_fusion.8
  267.2 0.9 multiply_convert_fusion.2.x_ref
  268.1 69.8 %experts_forward.2 = (f32[128,1536]{1,0:T(8,128)}, bf16[8,128,1536]{2,1,0:T(8,128)(2,1)}, bf16[8,128,1024]{2,1,0:T(8,128)(2,1)}, bf16[8,128,1024]{2,1,0:T(8,128)(2,1)}) custom-call(bf16[128,1536]{1,0:T(8,128)(2,1)} %multiply_convert_fusion.2.x_ref, f32[8,128,2]{2,1,0:T(8,128)} %get-tuple-element.151.share_ref, ...), custom_call_target="tpu_custom_call" | custom-call | tf_op jit(solution)/shard_map/experts_forward/pallas_call | solution.py:1019
  337.9 1.3 multiply_reduce_fusion.7
  339.2 0.9 multiply_convert_fusion.1.x_ref
  340.1 74.4 %attention_forward.3 = (f32[128,1536]{1,0:T(8,128)}, bf16[8,128,1536]{2,1,0:T(8,128)(2,1)}, bf16[8,384,64]{2,1,0:T(8,128)(2,1)}, bf16[1024,64]{1,0:T(8,128)(2,1)...) custom-call(bf16[128,1536]{1,0:T(8,128)(2,1)} %multiply_convert_fusion., ...), custom_call_target="tpu_custom_call" | custom-call | tf_op jit(solution)/shard_map/attention_forward/pallas_call | solution.py:1720
  414.5 1.3 multiply_reduce_fusion.6
  415.8 0.9 multiply_convert_fusion.x_ref
  416.7 68.3 %experts_forward.3 = (f32[128,1536]{1,0:T(8,128)}, bf16[8,128,1536]{2,1,0:T(8,128)(2,1)}, bf16[8,128,1024]{2,1,0:T(8,128)(2,1)}, bf16[8,128,1024]{2,1,0:T(8,128)(2,1)}) custom-call(bf16[128,1536]{1,0:T(8,128)(2,1)} %multiply_convert_fusion.x_ref, f32[8,128,2]{2,1,0:T(8,128)} %get-tuple-element.150.share_ref, bf16[2,7,1536,512]{3,2,1,0:T(8,128)(2,1)} %get-tuple-element.58.mats_ref), custom_call_target="tpu_custom_call" | custom-call | tf_op jit(solution)/shard_map/experts_forward/pallas_call | solution.py:1019
  485.0 72.4 %experts_backward.2 = (f32[128,1536]{1,0:T(8,128)}, bf16[8,128,1536]{2,1,0:T(8,128)(2,1)}, bf16[8,128,1024]{2,1,0:T(8,128)(2,1)}, bf16[8,128,1024]{2,1,0:T(8,128)(2,1)}, bf16[8,128,1024]{2,1,0:T(8,128)(2,1)}) custom-call(bf16[128,1536]{1,0:T(8,128)(2,1)} %bitcast.143, f32[8,128,2]{2,1,0:T(8,128)} %get-tuple-element.150.share_ref, ...), custom_call_target="tpu_custom_call" | custom-call | tf_op jit(solution)/shard_map/experts_backward/pallas_call | solution.py:1122
  557.4 1.4 multiply_reduce_fusion
  559.0 2.1 fusion.33.x_ref
  561.1 78.0 %attention_backward.2 = (f32[128,1536]{1,0:T(8,128)}, bf16[8,128,1536]{2,1,0:T(8,128)(2,1)}, bf16[8,128,384]{2,1,0:T(8,128)(2,1)}) custom-call(bf16[128,1536]{1,0:T(8,128)(2,1)} %fusion.33.x_ref, bf16[2,7,1536,512]{3,2,1,0:T(8,128)(2,1)} %get-tuple-element.58.mats_ref, f32[1024,128]{1,0:T(8,128)} %get-tuple-element.181.cos_ref, ...), custom_call_target="tpu_custom_call" | custom-call | tf_op jit(solution)/shard_map/attention_backward/pallas_call | solution.py:1852
  639.1 1.4 multiply_reduce_fusion.1
  640.6 3.0 fusion.35
  643.7 0.7 pad.19.e_ref
  644.4 120.7 %collect_grads.3 = (bf16[8,7,48,512]{3,2,1,0:T(8,128)(2,1)}, f32[8,8,128]{2,1,0:T(8,128)}) custom-call(bf16[1024,1536]{1,0:T(8,128)(2,1)} %bitcast.146, bf16[1024,384]{1,0:T(8,128)(2,1)} %bitcast.170, bf16[1024,1536]{1,0:T(8,128)(2,1)} %bitcast.150, bf16[1024,192]{1,0:T(8,128)(2,1)} %bitcast.173, bf16[1024,1536]{1,0:T(8,128)(2,1)} %bitcast.148, ...), custom_call_target="tpu_custom_call" | custom-call | tf_op jit(solution)/shard_map/collect_grads/pallas_call | solution.py:1586
  765.1 0.9 slice_reduce_fusion.4
  765.9 1.0 slice_bitcast_fusion.6
  767.3 1.2 slice_bitcast_fusion.2
  768.5 3.1 fusion.37
  771.6 0.8 convert_element_type.376
  772.5 0.8 convert_element_type.358
  773.3 75.4 %experts_backward.3 = (f32[128,1536]{1,0:T(8,128)}, bf16[8,128,1536]{2,1,0:T(8,128)(2,1)}, bf16[8,128,1024]{2,1,0:T(8,128)(2,1)}, bf16[8,128,1024]{2,1,0:T(8,128)(2,1)}, bf16[8,128,1024]{2,1,0:T(8,128)(2,1)}) custom-call(bf16[128,1536]{1,0:T(8,128)(2,1)} %get-tuple-element.121.x_ref, f32[8,128,2]{2,1,0:T(8,128)} %get-tuple-element.151.share_ref, ...), custom_call_target="tpu_custom_call" | custom-call | tf_op jit(solution)/shard_map/experts_backward/pallas_call | solution.py:1122
  848.8 1.4 multiply_reduce_fusion.2
  850.2 2.1 fusion.34
  852.3 75.1 %attention_backward.3 = (f32[128,1536]{1,0:T(8,128)}, bf16[8,128,1536]{2,1,0:T(8,128)(2,1)}, bf16[8,128,384]{2,1,0:T(8,128)(2,1)}) custom-call(bf16[128,1536]{1,0:T(8,128)(2,1)} %get-tuple-element.119.x_ref, bf16[2,7,1536,512]{3,2,1,0:T(8,128)(2,1)} %get-tuple-element.58.mats_ref, f32[1024,128]{1,0:T(8,128)} %get-tuple-element.181.cos_ref, ...), custom_call_target="tpu_custom_call" | custom-call | tf_op jit(solution)/shard_map/attention_backward/pallas_call | solution.py:1852
  927.6 1.4 fusion.10
  929.1 2.3 fusion.9
  931.5 0.7 pad.18.e_ref
  932.2 103.5 %collect_grads.2 = (bf16[8,7,48,512]{3,2,1,0:T(8,128)(2,1)}, f32[8,8,128]{2,1,0:T(8,128)}) custom-call(bf16[1024,1536]{1,0:T(8,128)(2,1)} %bitcast.144, bf16[1024,384]{1,0:T(8,128)(2,1)} %bitcast.171, bf16[1024,1536]{1,0:T(8,128)(2,1)} %bitcast.151, bf16[1024,192]{1,0:T(8,128)(2,1)} %bitcast.172, bf16[1024,1536]{1,0:T(8,128)(2,1)} %bitcast.145, ...), custom_call_target="tpu_custom_call" | custom-call | tf_op jit(solution)/shard_map/collect_grads/pallas_call | solution.py:1586
  1035.8 0.9 slice_reduce_fusion.5
  1037.8 1.0 slice_bitcast_fusion.7
  1039.0 0.7 maximum_convert_fusion.6
  1039.8 0.7 maximum_convert_fusion.5
  1040.5 1.1 slice_bitcast_fusion.3
  1041.7 1.8 fusion.36
  1043.6 0.8 convert_element_type.373
  1044.6 1.8 maximum_convert_fusion.3
  1046.4 1.9 maximum_convert_fusion.4
  1048.3 1.9 maximum_convert_fusion.1
  1050.2 1.9 maximum_convert_fusion.2
  1052.1 1.9 maximum_convert_fusion
  (114 shorter events, 9.6 us)
Async XLA Ops:
  0.6 10.3 copy-start.15
  0.7 9.8 copy-start.14
  12.5 5.8 copy-start.8
  18.5 1.9 copy-start.9
  20.7 1.9 copy-start.10
  22.8 1.0 copy-start.12
  23.8 1.0 copy-start.13
  25.7 162.0 %copy-start = (bf16[1,128,1536]{2,1,0:T(8,128)(2,1)S(1)}, bf16[1,128,1536]{2,1,0:T(8,128)(2,1)}, u32[]{:S(2)}) copy-start(bf16[1,128,1536]{2,1,0:T(8,128)(2,1)} %param.15) | copy-start | bytes 1179652
  485.0 73.9 %copy-start.3 = (bf16[1,128,1536]{2,1,0:T(8,128)(2,1)S(1)}, bf16[1,128,1536]{2,1,0:T(8,128)(2,1)}, u32[]{:S(2)}) copy-start(bf16[1,128,1536]{2,1,0:T(8,128)(2,1)} %param.16) | copy-start | bytes 1179652
  561.1 79.5 %copy-start.2 = (f32[128,1536]{1,0:T(8,128)S(1)}, f32[128,1536]{1,0:T(8,128)}, u32[]{:S(2)}) copy-start(f32[128,1536]{1,0:T(8,128)} %get-tuple-element.65) | copy-start | bytes 2359300
  561.1 79.5 %copy-start.4 = (bf16[1,128,1536]{2,1,0:T(8,128)(2,1)S(1)}, bf16[1,128,1536]{2,1,0:T(8,128)(2,1)}, u32[]{:S(2)}) copy-start(bf16[1,128,1536]{2,1,0:T(8,128)(2,1)} %param.16) | copy-start | bytes 1179652
  773.3 76.9 %copy-start.11 = (f32[128,1536]{1,0:T(8,128)S(1)}, f32[128,1536]{1,0:T(8,128)}, u32[]{:S(2)}) copy-start(f32[128,1536]{1,0:T(8,128)} %get-tuple-element.122) | copy-start | bytes 2359300
  852.3 75.3 %copy-start.1 = (bf16[1,128,1536]{2,1,0:T(8,128)(2,1)S(1)}, bf16[1,128,1536]{2,1,0:T(8,128)(2,1)}, u32[]{:S(2)}) copy-start(bf16[1,128,1536]{2,1,0:T(8,128)(2,1)} %param.15) | copy-start | bytes 1179652
  1043.5 4.8 copy-start.7
  1046.4 3.8 copy-start.6
  1050.2 1.9 copy-start.5

commit v4 on v3

--- a/solution.py
+++ b/solution.py
@@ -733,83 +733,133 @@
         return jnp.where(z == 0, nz - 1 - i, jnp.where(z == nz - 1, i, jnp.where(z == 1, mid1, mid2)))
 
 
+EXTRA = 16
+
+
 class Gather:
     @staticmethod
     def scratch(nz):
-        return [DMA((6, nz))]
+        return [DMA((10, nz))]
 
     def __init__(self, line, own_ref, all_ref, sems):
         self.line, self.own, self.all, self.sems = line, own_ref, all_ref, sems
-
-    def block(self, row):
-        return self.all.at[row * NX + self.line.x]
+        self.main = own_ref.shape[0] - EXTRA
+
+    def block(self, row, column=None):
+        column = self.line.x if column is None else column
+        return self.all.at[row * NX + column, pl.ds(0, self.main)]
+
+    def extras(self, row):
+        return self.all.at[pl.ds(row * NX, NX), pl.ds(self.main, EXTRA)]
+
+    def own_main(self):
+        return self.own.at[pl.ds(0, self.main)]
+
+    def move(self, kind, t, src, dst, ctx):
+        return remote(src, dst, self.sems.at[kind, t], self.sems.at[kind + 1, t], ctx, self.line.fsdp)
 
     def up(self, t, src=None):
-        line = self.line
-        block = self.block(line.z - t)
-        return remote(block if src is None else src, block, self.sems.at[0, t], self.sems.at[1, t], line.above, line.fsdp)
+        block = self.block(self.line.z - t)
+        return self.move(0, t, block if src is None else src, block, self.line.above)
 
     def down(self, t, src=None):
-        line = self.line
-        block = self.block(line.z + t)
-        return remote(block if src is None else src, block, self.sems.at[2, t], self.sems.at[3, t], line.below, line.fsdp)
+        block = self.block(self.line.z + t)
+        return self.move(2, t, block if src is None else src, block, self.line.below)
 
     def across(self, row, src=None):
-        line = self.line
         block = self.block(row)
-        return remote(block if src is None else src, block, self.sems.at[4, row], self.sems.at[5, row], line.mate, line.fsdp)
+        return self.move(4, row, block if src is None else src, block, self.line.mate)
+
+    def extra_up(self, t):
+        return self.move(6, t, self.extras(self.line.z - t), self.extras(self.line.z - t), self.line.above)
+
+    def extra_down(self, t):
+        return self.move(8, t, self.extras(self.line.z + t), self.extras(self.line.z + t), self.line.below)
+
+    def extra_across(self, column):
+        own = self.own.at[pl.ds(self.main, EXTRA)]
+        there = self.all.at[self.line.z * NX + column, pl.ds(self.main, EXTRA)]
+        last = self.line.nz - 1
+        return remote(own, there, self.sems.at[6, last], self.sems.at[7, last], self.line.mate, self.line.fsdp)
 
     def start(self):
         line = self.line
+        self.extra_across(line.x).start()
 
         @pl.when(line.z < line.nz - 1)
         def _():
-            self.up(0, self.own).start()
+            self.up(0, self.own_main()).start()
 
         @pl.when(line.z > 0)
         def _():
-            self.down(0, self.own).start()
-
-        self.across(line.z, self.own).start()
+            self.down(0, self.own_main()).start()
+
+        self.across(line.z, self.own_main()).start()
+
+    def start_extras(self):
+        line = self.line
+        self.extra_across(1 - line.x).wait_recv()
+
+        @pl.when(line.z < line.nz - 1)
+        def _():
+            self.extra_up(0).start()
+
+        @pl.when(line.z > 0)
+        def _():
+            self.extra_down(0).start()
 
     def forward(self, t):
         line = self.line
 
         @pl.when(line.z - 1 - t >= 0)
         def _():
-            remote(self.own, self.block(line.z - 1 - t), self.sems.at[0, t], self.sems.at[1, t], line.above, line.fsdp).wait_recv()
+            row = line.z - 1 - t
+            self.move(0, t, self.own_main(), self.block(row), line.above).wait_recv()
 
             @pl.when(line.z < line.nz - 1)
             def _():
                 self.up(t + 1).start()
 
-            self.across(line.z - 1 - t).start()
+            self.across(row).start()
+            self.move(6, t, self.extras(row), self.extras(row), line.above).wait_recv()
+
+            @pl.when(line.z < line.nz - 1)
+            def _():
+                self.extra_up(t + 1).start()
 
         @pl.when(line.z + 1 + t < line.nz)
         def _():
-            remote(self.own, self.block(line.z + 1 + t), self.sems.at[2, t], self.sems.at[3, t], line.below, line.fsdp).wait_recv()
+            row = line.z + 1 + t
+            self.move(2, t, self.own_main(), self.block(row), line.below).wait_recv()
 
             @pl.when(line.z > 0)
             def _():
                 self.down(t + 1).start()
 
-            self.across(line.z + 1 + t).start()
+            self.across(row).start()
+            self.move(8, t, self.extras(row), self.extras(row), line.below).wait_recv()
+
+            @pl.when(line.z > 0)
+            def _():
+                self.extra_down(t + 1).start()
 
     def wait_pair(self, row):
-        line = self.line
-        remote(self.own, self.all.at[row * NX + 1 - line.x], self.sems.at[4, row], self.sems.at[5, row], line.mate, line.fsdp).wait_recv()
+        self.move(4, row, self.own_main(), self.block(row, 1 - self.line.x), self.line.mate).wait_recv()
 
     def finish(self):
         line = self.line
+        self.extra_across(line.x).wait_send()
         for t in range(line.nz - 1):
 
             @pl.when((line.z - t >= 0) & (line.z < line.nz - 1))
             def _():
                 self.up(t).wait_send()
+                self.extra_up(t).wait_send()
 
             @pl.when((line.z + t < line.nz) & (line.z > 0))
             def _():
                 self.down(t).wait_send()
+                self.extra_down(t).wait_send()
 
         for row in range(line.nz):
             self.across(row).wait_send()
@@ -818,29 +868,78 @@
 class Scatter:
     @staticmethod
     def scratch(nz, rows, width):
-        return [pltpu.VMEM((4, nz, rows, width), BF), DMA((6, nz))]
-
-    def __init__(self, line, part_ref, out_ref, work, sems):
-        self.line, self.part, self.out, self.sems = line, part_ref, out_ref, sems
+        return [
+            pltpu.VMEM((4, nz, rows - EXTRA, width), BF),
+            pltpu.VMEM((4, nz, NX, EXTRA, width), BF),
+            DMA((10, nz)),
+            DMA((2,)),
+        ]
+
+    def __init__(self, line, part_ref, out_ref, work, extra, sems, mate_sems):
+        self.line, self.part, self.out, self.sems, self.mate_sems = line, part_ref, out_ref, sems, mate_sems
         self.xin, self.acc, self.upin, self.downin = (work.at[i] for i in range(4))
+        self.eacc, self.eup, self.edown, self.emate = (extra.at[i] for i in range(4))
+        self.main = part_ref.shape[1] - EXTRA
+
+    def move(self, kind, row, src, dst, ctx):
+        return remote(src, dst, self.sems.at[kind, row], self.sems.at[kind + 1, row], ctx, self.line.fsdp)
 
     def across(self, row):
-        line = self.line
-        return remote(self.part.at[row * NX + 1 - line.x], self.xin.at[row], self.sems.at[0, row], self.sems.at[1, row], line.mate, line.fsdp)
+        mates = self.part.at[row * NX + 1 - self.line.x, pl.ds(0, self.main)]
+        return self.move(0, row, mates, self.xin.at[row], self.line.mate)
 
     def up(self, row):
-        line = self.line
-        return remote(self.acc.at[row], self.upin.at[row], self.sems.at[2, row], self.sems.at[3, row], line.above, line.fsdp)
+        return self.move(2, row, self.acc.at[row], self.upin.at[row], self.line.above)
 
     def down(self, row):
-        line = self.line
-        return remote(self.acc.at[row], self.downin.at[row], self.sems.at[4, row], self.sems.at[5, row], line.below, line.fsdp)
+        return self.move(4, row, self.acc.at[row], self.downin.at[row], self.line.below)
+
+    def extra_up(self, row):
+        return self.move(6, row, self.eacc.at[row], self.eup.at[row], self.line.above)
+
+    def extra_down(self, row):
+        return self.move(8, row, self.eacc.at[row], self.edown.at[row], self.line.below)
+
+    def extra_across(self):
+        return remote(
+            self.emate.at[0, 0], self.emate.at[1, 0], self.mate_sems.at[0], self.mate_sems.at[1], self.line.mate, self.line.fsdp
+        )
+
+    def extras(self, row):
+        return self.part[pl.ds(row * NX, NX), pl.ds(self.main, EXTRA), :].astype(F32)
 
     def add(self, i):
         line = self.line
         row = line.far(i)
+
+        @pl.when(row > line.z)
+        def _():
+            @pl.when(line.z == 0)
+            def _():
+                self.eacc[row] = self.extras(row).astype(BF)
+
+            @pl.when(line.z > 0)
+            def _():
+                self.extra_up(row).wait_recv()
+                self.eacc[row] = (self.extras(row) + self.eup[row].astype(F32)).astype(BF)
+
+            self.extra_up(row).start()
+
+        @pl.when(row < line.z)
+        def _():
+            @pl.when(line.z == line.nz - 1)
+            def _():
+                self.eacc[row] = self.extras(row).astype(BF)
+
+            @pl.when(line.z < line.nz - 1)
+            def _():
+                self.extra_down(row).wait_recv()
+                self.eacc[row] = (self.extras(row) + self.edown[row].astype(F32)).astype(BF)
+
+            self.extra_down(row).start()
+
         self.across(row).wait_recv()
-        mine = self.part[row * NX + line.x].astype(F32) + self.xin[row].astype(F32)
+        mine = self.part[row * NX + line.x, 0 : self.main, :].astype(F32) + self.xin[row].astype(F32)
 
         @pl.when(row > line.z)
         def _():
@@ -870,100 +969,89 @@
 
         @pl.when(row == line.z)
         def _():
-            self.out[...] = mine
+            self.out[0 : self.main, :] = mine
+
+    def extra_sum(self, column):
+        at = self.line.z * NX + column
+        return self.part[at, self.main : self.main + EXTRA, :].astype(F32)
 
     def finish(self):
         line = self.line
+        self.out[self.main : self.main + EXTRA, :] = self.extra_sum(line.x)
+        others = self.extra_sum(1 - line.x)
+
+        def more(ref):
+            self.out[self.main : self.main + EXTRA, :] += ref[line.z, line.x].astype(F32)
 
         @pl.when(line.z > 0)
         def _():
+            self.extra_up(line.z).wait_recv()
+            more(self.eup)
+
+        @pl.when(line.z < line.nz - 1)
+        def _():
+            self.extra_down(line.z).wait_recv()
+            more(self.edown)
+
+        @pl.when(line.z == 0)
+        def _():
+            self.emate[0, 0] = (others + self.edown[line.z, 1 - line.x].astype(F32)).astype(BF)
+
+        @pl.when(line.z == line.nz - 1)
+        def _():
+            self.emate[0, 0] = (others + self.eup[line.z, 1 - line.x].astype(F32)).astype(BF)
+
+        @pl.when((line.z > 0) & (line.z < line.nz - 1))
+        def _():
+            self.emate[0, 0] = (
+                others + self.eup[line.z, 1 - line.x].astype(F32) + self.edown[line.z, 1 - line.x].astype(F32)
+            ).astype(BF)
+
+        self.extra_across().start()
+
+        @pl.when(line.z > 0)
+        def _():
             self.up(line.z).wait_recv()
-            self.out[...] += self.upin[line.z].astype(F32)
+            self.out[0 : self.main, :] += self.upin[line.z].astype(F32)
 
         @pl.when(line.z < line.nz - 1)
         def _():
             self.down(line.z).wait_recv()
-            self.out[...] += self.downin[line.z].astype(F32)
-
+            self.out[0 : self.main, :] += self.downin[line.z].astype(F32)
+
+        self.extra_across().wait_recv()
+        self.out[self.main : self.main + EXTRA, :] += self.emate[1, 0].astype(F32)
+        self.extra_across().wait_send()
         for row in range(line.nz):
             self.across(row).wait_send()
 
             @pl.when(row > line.z)
             def _():
                 self.up(row).wait_send()
+                self.extra_up(row).wait_send()
 
             @pl.when(row < line.z)
             def _():
                 self.down(row).wait_send()
+                self.extra_down(row).wait_send()
 
 
 def params(collective, vmem_mib):
     return pltpu.CompilerParams(collective_id=collective, has_side_effects=True, vmem_limit_bytes=vmem_mib << 20)
 
 
-def gather_kernel(nz, x_ref, o_ref, own_sem, sems):
-    line = Line(nz)
-    line.greet()
-    ring = Gather(line, x_ref, o_ref, sems)
-    ring.start()
-    own = pltpu.make_async_copy(x_ref, o_ref.at[line.ctx], own_sem)
-    own.start()
-    for t in range(nz - 1):
-        ring.forward(t)
-    for row in range(nz):
-        ring.wait_pair(row)
-    ring.finish()
-    own.wait()
-
-
-def gather_rows(block, nz):
-    rows, width = block.shape
-    return pl.pallas_call(
-        functools.partial(gather_kernel, nz),
-        out_shape=jax.ShapeDtypeStruct((nz * NX, rows, width), block.dtype),
-        in_specs=[VM],
-        out_specs=ANY,
-        scratch_shapes=[DMA] + Gather.scratch(nz),
-        compiler_params=params(1, 16),
-        name="gather_rows",
-    )(block)
-
-
-def scatter_kernel(nz, p_ref, o_ref, work, sems):
-    line = Line(nz)
-    line.greet()
-    ring = Scatter(line, p_ref, o_ref, work, sems)
-    for i in range(nz):
-        ring.across(line.far(i)).start()
-    for i in range(nz):
-        ring.add(i)
-    ring.finish()
-
-
-def scatter_rows(parts, nz):
-    _, rows, width = parts.shape
-    return pl.pallas_call(
-        functools.partial(scatter_kernel, nz),
-        out_shape=jax.ShapeDtypeStruct((rows, width), F32),
-        in_specs=[VM],
-        out_specs=VM,
-        scratch_shapes=Scatter.scratch(nz, rows, width),
-        compiler_params=params(2, 32),
-        name="scatter_rows",
-    )(parts)
-
-
 def experts_kernel(nz, layer, x_ref, share_ref, mats_ref, o_ref, all_out, gate_out, up_out,
-                   mats, blocks, part, gate, up, load_sem, save_sem, gsems, work, ssems):
+                   mats, blocks, part, gate, up, load_sem, save_sem, gsems, work, ework, ssems, msems):
     line = Line(nz)
     rows, width = x_ref.shape
     load = pltpu.make_async_copy(mats_ref.at[layer, pl.ds(1, 6)], mats, load_sem)
     load.start()
     line.greet()
     ring = Gather(line, x_ref, blocks, gsems)
+    blocks[line.ctx] = x_ref[...]
     ring.start()
-    blocks[line.ctx] = x_ref[...]
     load.wait()
+    ring.start_extras()
 
     def saves(row):
         pair = pl.ds(row * NX, NX)
@@ -999,7 +1087,7 @@
         return carry
 
     lax.fori_loop(0, nz, step, 0)
-    sums = Scatter(line, part, o_ref, work, ssems)
+    sums = Scatter(line, part, o_ref, work, ework, ssems, msems)
     for i in range(nz):
         sums.across(line.far(i)).start()
     ring.finish()
@@ -1043,7 +1131,7 @@
 
 
 def experts_back_kernel(nz, layer, x_ref, share_ref, mats_ref, gate_ref, up_ref, o_ref, all_out, dgate_out, dup_out, inner_out,
-                        mats, blocks, part, gate, up, inners, load_sem, save_sem, gsems, work, ssems):
+                        mats, blocks, part, gate, up, inners, load_sem, save_sem, gsems, work, ework, ssems, msems):
     line = Line(nz)
     rows, width = x_ref.shape
     loads = (
@@ -1055,10 +1143,11 @@
         load.start()
     line.greet()
     ring = Gather(line, x_ref, blocks, gsems)
+    blocks[line.ctx] = x_ref[...]
     ring.start()
-    blocks[line.ctx] = x_ref[...]
     for load in loads:
         load.wait()
+    ring.start_extras()
 
     def saves(row):
         pair = pl.ds(row * NX, NX)
@@ -1101,7 +1190,7 @@
         return carry
 
     lax.fori_loop(0, nz, step, 0)
-    sums = Scatter(line, part, o_ref, work, ssems)
+    sums = Scatter(line, part, o_ref, work, ework, ssems, msems)
     for i in range(nz):
         sums.across(line.far(i)).start()
     ring.finish()
@@ -1440,19 +1529,54 @@
     )(send, small)
 
 
-def grads_kernel(nctx, nfs, rows, normed_ref, dproj_ref, middle_ref, attended_ref, moe_ref, dgate_ref, dup_ref, grad_ref, inner_ref, e_ref,
-                 o_ref, eo_ref, mine, cin, yin, half, full, e_cin, e_half, e_yin, e_full,
-                 own_sem, c_sem, y_sem, p_sem, eown_sem, ec_sem, ey_sem, ep_sem):
+def grads_kernel(nctx, nfs, rows, layers, *refs):
+    count = 9 * layers
+    ins, (e_ref, o_ref, eo_ref), refs = refs[:count], refs[count : count + 3], refs[count + 3 :]
+    tall, dproj, attended, dgate, dup, inner, mine, cin, yin, e_cin, e_half, e_yin, e_full = refs[:13]
+    tall_sem, wide_sem, own_sem, c_sem, y_sem, p_sem, eown_sem, ec_sem, ey_sem, ep_sem = refs[13:]
     nz = nctx // NX
     line = Line(nz)
     ctx, fsdp = line.ctx, line.fsdp
     y, core = fsdp // NCORE, fsdp % NCORE
     y_mate = (1 - y) * NCORE + core
     c_mate = y * NCORE + 1 - core
-    mats = mine.shape[0]
-    proj = mine.shape[2] - attended_ref.shape[1]
-    units = dgate_ref.shape[1] // 2
-    slab = NX * nfs * rows
+    mats, slab = mine.shape[1], mine.shape[2]
+    proj = mine.shape[3] - attended.shape[2]
+    units = dgate.shape[2] // 2
+    items = layers * nz
+
+    def layer_of(i):
+        return layers - 1 - i // nz
+
+    def row_of(i):
+        return line.far(i % nz)
+
+    def wide_loads(layer):
+        _, dproj_in, _, attended_in, _, dgate_in, dup_in, _, inner_in = ins[9 * layer : 9 * layer + 9]
+        pairs = ((dproj_in, dproj), (attended_in, attended), (dgate_in, dgate), (dup_in, dup), (inner_in, inner))
+        return [pltpu.make_async_copy(src, dst.at[layer], wide_sem.at[k, layer]) for k, (src, dst) in enumerate(pairs)]
+
+    def tall_loads(i, layer):
+        normed_in, _, middle_in, _, moe_in, _, _, grad_in, _ = ins[9 * layer : 9 * layer + 9]
+        lanes = pl.ds(pl.multiple_of(row_of(i) * slab, 128), slab)
+        return [
+            pltpu.make_async_copy(src.at[:, lanes], tall.at[i % 2, k], tall_sem.at[i % 2, k])
+            for k, src in enumerate((normed_in, middle_in, moe_in, grad_in))
+        ]
+
+    def load(i):
+        for layer in range(layers):
+
+            @pl.when(layer_of(i) == layer)
+            def _():
+                for copy in tall_loads(i, layer):
+                    copy.start()
+
+    for layer in reversed(range(layers)):
+        for copy in wide_loads(layer):
+            copy.start()
+        if layer == layers - 1:
+            load(0)
     barrier = pltpu.get_barrier_semaphore()
     for step in range(1, nctx):
         greet(barrier, (ctx + step) % nctx, fsdp)
@@ -1460,24 +1584,29 @@
         greet(barrier, ctx, other)
     pl.semaphore_wait(barrier, nctx + 1)
 
-    def span(s, f):
-        return pl.ds(pl.multiple_of((s * nfs + f) * rows, rows), rows)
-
-    def to_c(s, k):
+    def span(side, f):
+        return pl.ds(pl.multiple_of((side * nfs + f) * rows, rows), rows)
+
+    def to_c(i, side, k):
+        layer, s = layer_of(i), row_of(i) * NX + side
         f = (1 - y if k == 0 else y) * NCORE + 1 - core
-        return remote(mine.at[:, span(s, f), :], cin.at[k, s], c_sem.at[0, k, s], c_sem.at[1, k, s], ctx, c_mate)
-
-    def to_y(s):
-        return remote(half.at[s], yin.at[s], y_sem.at[0, s], y_sem.at[1, s], ctx, y_mate)
-
-    def out(s):
-        return remote(full.at[s], o_ref.at[ctx], p_sem.at[0, s], p_sem.at[1, ctx], s, fsdp)
-
-    def out_in(s):
-        return remote(full.at[s], o_ref.at[s], p_sem.at[0, s], p_sem.at[1, s], s, fsdp)
+        return remote(mine.at[i % 3, :, span(side, f), :], cin.at[layer, k, s], c_sem.at[0, layer, k, s], c_sem.at[1, layer, k, s], ctx, c_mate)
+
+    def to_y(layer, s):
+        return remote(cin.at[layer, 0, s], yin.at[layer, s], y_sem.at[0, layer, s], y_sem.at[1, layer, s], ctx, y_mate)
+
+    def out(layer, s):
+        return remote(cin.at[layer, 1, s], o_ref.at[layer, ctx], p_sem.at[0, layer, s], p_sem.at[1, layer, ctx], s, fsdp)
+
+    def out_in(layer, s):
+        return remote(cin.at[layer, 1, s], o_ref.at[layer, s], p_sem.at[0, layer, s], p_sem.at[1, layer, s], s, fsdp)
+
+    def own(layer):
+        return pltpu.make_async_copy(cin.at[layer, 1, ctx], o_ref.at[layer, ctx], own_sem.at[layer])
 
     e_to_c = remote(e_ref.at[1 - core], e_cin, ec_sem.at[0], ec_sem.at[1], ctx, c_mate)
     e_to_y = remote(e_half.at[1 - y], e_yin, ey_sem.at[0], ey_sem.at[1], ctx, y_mate)
+    e_own = pltpu.make_async_copy(e_full.at[ctx], eo_ref.at[ctx], eown_sem)
 
     def e_out(s):
         return remote(e_full.at[s], eo_ref.at[ctx], ep_sem.at[0, s], ep_sem.at[1, ctx], s, fsdp)
@@ -1486,122 +1615,153 @@
         return remote(e_full.at[s], eo_ref.at[s], ep_sem.at[0, s], ep_sem.at[1, s], s, fsdp)
 
     e_to_c.start()
-    own = pltpu.make_async_copy(full.at[ctx], o_ref.at[ctx], own_sem)
-    e_own = pltpu.make_async_copy(e_full.at[ctx], eo_ref.at[ctx], eown_sem)
-
-    turn_of = line.far
-
-    def compute(row):
-        lanes = pl.ds(pl.multiple_of(row * slab, 128), slab)
-        tall = pl.ds(pl.multiple_of(row * slab, 16), slab)
-        mine[0, tall, pl.ds(0, proj)] = dot(normed_ref[:, lanes], dproj_ref[...], TN)[:, :proj].astype(BF)
-        mine[0, tall, pl.ds(proj, mine.shape[2] - proj)] = dot(middle_ref[:, lanes], attended_ref[...], TN).astype(BF)
-        moe = moe_ref[:, lanes]
+
+    def compute(i):
+        layer, slot, here = layer_of(i), i % 2, i % 3
+        mine[here, 0, :, pl.ds(0, proj)] = dot(tall[slot, 0], dproj[layer], TN)[:, :proj].astype(BF)
+        mine[here, 0, :, pl.ds(proj, mine.shape[3] - proj)] = dot(tall[slot, 1], attended[layer], TN).astype(BF)
         for e in range(2):
             part_of = pl.ds(e * units, units)
-            mine[1 + e, tall, :] = dot(moe, dgate_ref[:, part_of], TN).astype(BF)
-            mine[3 + e, tall, :] = dot(moe, dup_ref[:, part_of], TN).astype(BF)
-            mine[5 + e, tall, :] = dot(grad_ref[:, lanes], inner_ref[:, part_of], TN).astype(BF)
-
-    def first(s):
-        to_c(s, 0).wait_recv()
+            mine[here, 1 + e] = dot(tall[slot, 2], dgate[layer, :, part_of], TN).astype(BF)
+            mine[here, 3 + e] = dot(tall[slot, 2], dup[layer, :, part_of], TN).astype(BF)
+            mine[here, 5 + e] = dot(tall[slot, 3], inner[layer, :, part_of], TN).astype(BF)
+
+    def first(i, side):
+        layer, s = layer_of(i), row_of(i) * NX + side
+        to_c(i, side, 0).wait_recv()
 
         def one(m, _):
-            half[s, m] = (mine[m, span(s, y_mate), :].astype(F32) + cin[0, s, m].astype(F32)).astype(BF)
+            term = mine[i % 3, m, span(side, y_mate), :].astype(F32)
+            cin[layer, 0, s, m] = (term + cin[layer, 0, s, m].astype(F32)).astype(BF)
             return 0
 
         lax.fori_loop(0, mats, one, 0)
-        to_y(s).start()
-
-    def second(s):
-        to_c(s, 1).wait_recv()
-        to_y(s).wait_recv()
+        to_y(layer, s).start()
+
+    def second(i, side):
+        layer, s = layer_of(i), row_of(i) * NX + side
+        to_c(i, side, 1).wait_recv()
+        to_y(layer, s).wait_recv()
 
         def one(m, _):
-            full[s, m] = (mine[m, span(s, fsdp), :].astype(F32) + cin[1, s, m].astype(F32) + yin[s, m].astype(F32)).astype(BF)
+            term = mine[i % 3, m, span(side, fsdp), :].astype(F32) + yin[layer, s, m].astype(F32)
+            cin[layer, 1, s, m] = (term + cin[layer, 1, s, m].astype(F32)).astype(BF)
             return 0
 
         lax.fori_loop(0, mats, one, 0)
+        for k in range(2):
+            to_c(i, side, k).wait_send()
 
         @pl.when(s != ctx)
         def _():
-            out(s).start()
+            out(layer, s).start()
+
+        @pl.when(s == ctx)
+        def _():
+            own(layer).start()
 
     def step(i, carry):
-        @pl.when(i < nz)
-        def _():
-            row = turn_of(i)
-            compute(row)
+        @pl.when(i < items)
+        def _():
+            for layer in range(layers):
+
+                @pl.when(i == (layers - 1 - layer) * nz)
+                def _():
+                    for copy in wide_loads(layer):
+                        copy.wait()
+
+            for copy in tall_loads(i, 0):
+                copy.wait()
+
+            @pl.when(i + 1 < items)
+            def _():
+                load(i + 1)
+
+            compute(i)
             for k in range(2):
                 for side in range(NX):
-                    to_c(row * NX + side, k).start()
-
-        @pl.when((i >= 1) & (i < nz + 1))
+                    to_c(i, side, k).start()
+
+        @pl.when((i >= 1) & (i < items + 1))
         def _():
             for side in range(NX):
-                first(turn_of(i - 1) * NX + side)
-
-        @pl.when((i >= 2) & (i < nz + 2))
-        def _():
-            row = turn_of(i - 2)
+                first(i - 1, side)
+
+        @pl.when(i >= 2)
+        def _():
             for side in range(NX):
-                second(row * NX + side)
+                second(i - 2, side)
+
+        @pl.when(i == 1)
+        def _():
+            e_to_c.wait_recv()
+            e_half[...] = e_ref[core] + e_cin[...]
+            e_to_y.start()
+
+        @pl.when(i == 3)
+        def _():
+            e_to_y.wait_recv()
+            e_full[...] = e_half[y] + e_yin[...]
+            e_own.start()
+            for step_ in range(1, nctx):
+                e_out((ctx + step_) % nctx).start()
 
         return carry
 
-    lax.fori_loop(0, nz + 2, step, 0)
-    own.start()
-    e_to_c.wait_recv()
-    e_half[...] = e_ref[core] + e_cin[...]
-    e_to_y.start()
-    e_to_y.wait_recv()
-    e_full[...] = e_half[y] + e_yin[...]
-    e_own.start()
-    for step_ in range(1, nctx):
-        e_out((ctx + step_) % nctx).start()
+    lax.fori_loop(0, items + 2, step, 0)
+    for layer in range(layers):
+        own(layer).wait()
+        for s in range(nctx):
+            to_y(layer, s).wait_send()
+
+            @pl.when(s != ctx)
+            def _():
+                out(layer, s).wait_send()
+                out_in(layer, s).wait_recv()
+
     for s in range(nctx):
-        for k in range(2):
-            to_c(s, k).wait_send()
-        to_y(s).wait_send()
 
         @pl.when(s != ctx)
         def _():
-            out(s).wait_send()
-            out_in(s).wait_recv()
             e_out(s).wait_send()
             e_out_in(s).wait_recv()
 
     e_to_c.wait_send()
     e_to_y.wait_send()
     e_own.wait()
-    own.wait()
-
-
-def collect_grads(nctx, nfs, normed, dproj, middle, attended, moe, dgate, dup, grad, inner, extra):
-    width = normed.shape[1]
+
+
+def collect_grads(nctx, nfs, layer_args, extra):
+    layers = len(layer_args)
+    normed, dproj, middle, attended, moe, dgate, dup, grad, inner = layer_args[0]
+    group_rows, width = normed.shape
     rows = width // (nctx * nfs)
+    slab = NX * nfs * rows
     mats, cols = 7, dgate.shape[1] // 2
     blk = (mats, rows, cols)
     tile = extra.shape[3:]
+    held = [pltpu.VMEM((layers,) + part.shape, BF) for part in (dproj, attended, dgate, dup, inner)]
     return pl.pallas_call(
-        functools.partial(grads_kernel, nctx, nfs, rows),
-        out_shape=(jax.ShapeDtypeStruct((nctx,) + blk, BF), jax.ShapeDtypeStruct((nctx,) + tile, F32)),
-        in_specs=[VM] * 10,
+        functools.partial(grads_kernel, nctx, nfs, rows, layers),
+        out_shape=(jax.ShapeDtypeStruct((layers, nctx) + blk, BF), jax.ShapeDtypeStruct((nctx,) + tile, F32)),
+        in_specs=[ANY] * (9 * layers) + [VM],
         out_specs=(ANY, ANY),
-        scratch_shapes=[
-            pltpu.VMEM((mats, width, cols), BF),
-            pltpu.VMEM((2, nctx) + blk, BF),
-            pltpu.VMEM((nctx,) + blk, BF),
-            pltpu.VMEM((nctx,) + blk, BF),
-            pltpu.VMEM((nctx,) + blk, BF),
+        scratch_shapes=[pltpu.VMEM((2, 4, group_rows, slab), BF)]
+        + held
+        + [
+            pltpu.VMEM((3, mats, slab, cols), BF),
+            pltpu.VMEM((layers, 2, nctx) + blk, BF),
+            pltpu.VMEM((layers, nctx) + blk, BF),
             pltpu.VMEM((2, nctx) + tile, F32),
             pltpu.VMEM((2, nctx) + tile, F32),
             pltpu.VMEM((nctx,) + tile, F32),
             pltpu.VMEM((nctx,) + tile, F32),
-            DMA,
-            DMA((2, 2, nctx)),
-            DMA((2, nctx)),
-            DMA((2, nctx)),
+            DMA((2, 4)),
+            DMA((5, layers)),
+            DMA((layers,)),
+            DMA((2, layers, 2, nctx)),
+            DMA((2, layers, nctx)),
+            DMA((2, layers, nctx)),
             DMA,
             DMA((2,)),
             DMA((2,)),
@@ -1609,7 +1769,7 @@
         ],
         compiler_params=params(4, 63),
         name="collect_grads",
-    )(normed, dproj, middle, attended, moe, dgate, dup, grad, inner, extra)
+    )(*[part for args in layer_args for part in args], extra)
 
 
 def spin(values, cos_part, sin_part):
@@ -1625,7 +1785,7 @@
 
 def attention_kernel(nz, layer, x_ref, mats_ref, cos_ref, sin_ref, key_at_ref, query_at_ref,
                      o_ref, all_out, q_ref, k_ref, v_ref, peak_ref, share_ref, att_ref,
-                     attn, out_w, blocks, part, v_turned, probs, load_sem, save_sem, gsems, work, ssems):
+                     attn, out_w, blocks, part, v_turned, probs, load_sem, save_sem, gsems, work, ework, ssems, msems):
     line = Line(nz)
     rows, width = x_ref.shape
     pair_rows = NX * rows
@@ -1636,10 +1796,11 @@
     load.start()
     line.greet()
     ring = Gather(line, x_ref, blocks, gsems)
+    blocks[line.ctx] = x_ref[...]
     ring.start()
-    blocks[line.ctx] = x_ref[...]
     load.wait()
     out_w[...] = attn[:, o_at:]
+    ring.start_extras()
 
     def save(row):
         pair = pl.ds(row * NX, NX)
@@ -1673,7 +1834,7 @@
 
     lax.fori_loop(0, nz, project, 0)
     ring.finish()
-    sums = Scatter(line, part, o_ref, work, ssems)
+    sums = Scatter(line, part, o_ref, work, ework, ssems, msems)
 
     def attend(at):
         scores = dot(k_ref[...], q_ref[at], NT)
@@ -1750,7 +1911,7 @@
 
 def attention_back_kernel(nz, layer, x_ref, mats_ref, cos_ref, sin_ref, key_at_ref, query_at_ref, q_ref, k_ref, v_ref, peak_ref, share_ref,
                           o_ref, all_out, dproj_ref,
-                          attn, out_w, blocks, part, k_turned, probs, slopes, dq, dk, dv, load_sem, save_sem, gsems, work, ssems):
+                          attn, out_w, blocks, part, k_turned, probs, slopes, dq, dk, dv, load_sem, save_sem, gsems, work, ework, ssems, msems):
     line = Line(nz)
     rows, width = x_ref.shape
     pair_rows = NX * rows
@@ -1762,13 +1923,14 @@
     load.start()
     line.greet()
     ring = Gather(line, x_ref, blocks, gsems)
+    blocks[line.ctx] = x_ref[...]
     ring.start()
-    blocks[line.ctx] = x_ref[...]
     k_turned[...] = k_ref[...].astype(F32).T.astype(BF)
     dk[...] = jnp.zeros(dk.shape, F32)
     dv[...] = jnp.zeros(dv.shape, F32)
     load.wait()
     out_w[...] = attn[:, o_at:]
+    ring.start_extras()
 
     def save(row):
         pair = pl.ds(row * NX, NX)
@@ -1811,7 +1973,7 @@
 
     lax.fori_loop(0, nz, take, 0)
     ring.finish()
-    sums = Scatter(line, part, o_ref, work, ssems)
+    sums = Scatter(line, part, o_ref, work, ework, ssems, msems)
 
     def project(at):
         tall = pl.ds(pl.multiple_of(at * rows, rows), rows)
@@ -1978,7 +2140,7 @@
 
     output = hidden.astype(BF)
     grad = cotangent[0].astype(jnp.float32)
-    collected = [None] * LAYERS
+    layer_args, gain_grads = [None] * LAYERS, [None] * LAYERS
     for layer in reversed(range(LAYERS)):
         attn_gain, moe_gain, share = fetched[layer]
         hidden, normed_all, queries, keys, values, peaks, sums, attended, middle, moe_all, gate_act, up_act = records[layer]
@@ -1992,15 +2154,21 @@
         through, grad_attn_gain = norm_back(hidden, attn_gain, grad_normed)
         grad = grad_middle + through
 
-        extra = jnp.stack([grad_attn_gain, grad_moe_gain]).reshape(2, nctx, nfs // NCORE, NCORE, rows)
-        extra = jnp.pad(extra.transpose(3, 2, 1, 0, 4), ((0, 0), (0, 0), (0, 0), (0, 6), (0, 128 - rows)))
-        flat = [part.reshape(group_rows, -1) for part in (normed_all, d_proj, middle_all, attended, moe_all, d_gate, d_up, grad_all, inner)]
-        collected[layer] = collect_grads(nctx, nfs, *flat, extra)
+        layer_args[layer] = [
+            part.reshape(group_rows, -1)
+            for part in (normed_all, d_proj, middle_all, attended, moe_all, d_gate, d_up, grad_all, inner)
+        ]
+        gain_grads[layer] = [grad_attn_gain, grad_moe_gain]
+
+    extra = jnp.stack([part for pair in gain_grads for part in pair])
+    extra = extra.reshape(2 * LAYERS, nctx, nfs // NCORE, NCORE, rows).transpose(3, 2, 1, 0, 4)
+    extra = jnp.pad(extra, ((0, 0), (0, 0), (0, 0), (0, 8 - 2 * LAYERS), (0, 128 - rows)))
+    collected, gains_in = collect_grads(nctx, nfs, layer_args, extra)
 
     def attn_part(low, high):
         return jnp.stack(
             [
-                c[0][:, 0, :, low:high].transpose(1, 0, 2).reshape(c[0].shape[2], -1).astype(F32)
+                c[:, 0, :, low:high].transpose(1, 0, 2).reshape(rows, -1).astype(F32)
                 for c in collected
             ]
         )
@@ -2008,13 +2176,13 @@
     def expert_part(first):
         return jnp.stack(
             [
-                c[0][:, first : first + 2].reshape((EXPERTS,) + c[0].shape[2:]).astype(F32)
+                c[:, first : first + 2].reshape((EXPERTS,) + c.shape[2:]).astype(F32)
                 for c in collected
             ]
         )
 
     def gain_part(kind):
-        return jnp.stack([jnp.sum(c[1][:, kind, :rows], axis=0) for c in collected])
+        return jnp.stack([jnp.sum(gains_in[:, 2 * layer + kind, :rows], axis=0) for layer in range(LAYERS)])
 
     return (
         output[None],

time: 1060 us -> 991 us (0.935)
  Pallas kernels: 975 us -> 899 us
    pallas_call x2 -> x1, Pallas kernels: 224 us -> 183 us  [collect_grads(): pl.pallas_call(functools.partial(grads_kernel, nctx, nfs, rows, layers),...]
    pallas_call x2, Pallas kernels: 148 us -> 135 us  [experts_backward(): pl.pallas_call(functools.partial(experts_back_kernel, nz, layer), out_sha...]
where the time goes in v4:
time: 991 us; the launch traced here: 982 us
  Pallas kernels  899 us (91%)
  other arithmetic  48 us (5%)
  local copies, waits for them, and re-layouts  33.4 us (3%)
    pallas_call x1, Pallas kernels, collect_grads(): pl.pallas_call(functools.partial(grads_kernel, nctx, nfs, rows, layers),...  183 us
    pallas_call x1, Pallas kernels, spread_weights(): pl.pallas_call(functools.partial(weights_kernel, nctx, nfs, rows), out_sh...  161 us
    pallas_call x2, Pallas kernels, attention_rows(): pl.pallas_call(functools.partial(attention_kernel, nz, layer), out_shape=...  145 us
    pallas_call x2, Pallas kernels, attention_rows_back(): pl.pallas_call(functools.partial(attention_back_kernel, nz, layer), out_s...  144 us
    pallas_call x2, Pallas kernels, experts_backward(): pl.pallas_call(functools.partial(experts_back_kernel, nz, layer), out_sha...  135 us
    pallas_call x2, Pallas kernels, experts_forward(): pl.pallas_call(functools.partial(experts_kernel, nz, layer), out_shape=(j...  132 us

profile of v4, /device:TPU:11, one launch (start us, length us, event | category | flops | bytes accessed | tf_op | source)
XLA Modules:
  0.0 982.2 jit_solution(399493250555657539)
XLA Ops:
  0.6 2.1 convert.89
  2.8 1.0 fusion.40
  3.8 1.2 copy-done.4
  5.2 1.2 fusion.39
  6.5 1.2 copy-done.5
  7.9 1.3 fusion.38
  9.2 0.7 fusion.42
  10.2 0.7 fusion.41
  11.1 0.6 fusion.44
  11.9 0.6 fusion.43
  12.9 1.8 maximum_bitcast_fusion.1
  14.7 1.8 convert_element_type.330
  16.5 1.8 convert_element_type.327
  18.3 1.8 copy_bitcast_fusion.2
  20.1 1.6 convert_element_type.329
  21.7 1.6 convert_element_type.328
  23.3 1.0 copy_bitcast_fusion.6
  24.2 1.2 maximum_bitcast_fusion.2
  25.5 1.6 maximum_bitcast_fusion
  27.9 161.5 %spread_weights.1 = (bf16[2,7,1536,512]{3,2,1,0:T(8,128)(2,1)}, f32[32,16,128]{2,1,0:T(8,128)S(1)}) custom-call(bf16[2,8,7,48,512]{4,3,2,1,0:T(8,128)(2,1)S(1)} %pad_maximum_fusion.w_ref, f32[8,16,128]{2,1,0:T(8,128)S(1)} %pad_maximum_fusion.3.g_ref), custom_call_target="tpu_custom_call" | custom-call | tf_op jit(solution)/shard_map/spread_weights/pallas_call | solution.py:1509
  189.7 1.3 slice_bitcast_fusion.2
  191.4 0.9 fusion.4.x_ref
  192.8 1.9 fusion.13
  194.7 1.8 pad_maximum_fusion.1
  196.7 1.0 copy.93.key_at_ref
  197.8 0.6 pad_add_fusion.query_at_ref
  198.4 73.9 %attention_forward.2 = (f32[128,1536]{1,0:T(8,128)}, bf16[8,128,1536]{2,1,0:T(8,128)(2,1)}, bf16[8,384,64]{2,1,0:T(8,128)(2,1)}, bf16[1024,64]{1,0:T(8,128)(2,1)...) custom-call(bf16[128,1536]{1,0:T(8,128)(2,1)} %fusion.4.x_ref, ...), custom_call_target="tpu_custom_call" | custom-call | tf_op jit(solution)/shard_map/attention_forward/pallas_call | solution.py:1881
  272.3 1.3 multiply_reduce_fusion.8
  273.7 0.9 multiply_convert_fusion.2.x_ref
  274.6 66.8 %experts_forward.2 = (f32[128,1536]{1,0:T(8,128)}, bf16[8,128,1536]{2,1,0:T(8,128)(2,1)}, bf16[8,128,1024]{2,1,0:T(8,128)(2,1)}, bf16[8,128,1024]{2,1,0:T(8,128)(2,1)}) custom-call(bf16[128,1536]{1,0:T(8,128)(2,1)} %multiply_convert_fusion.2.x_ref, f32[8,128,2]{2,1,0:T(8,128)} %get-tuple-element.149.share_ref, ...), custom_call_target="tpu_custom_call" | custom-call | tf_op jit(solution)/shard_map/experts_forward/pallas_call | solution.py:1107
  341.4 1.3 multiply_reduce_fusion.7
  342.8 0.9 multiply_convert_fusion.1.x_ref
  343.7 70.6 %attention_forward.3 = (f32[128,1536]{1,0:T(8,128)}, bf16[8,128,1536]{2,1,0:T(8,128)(2,1)}, bf16[8,384,64]{2,1,0:T(8,128)(2,1)}, bf16[1024,64]{1,0:T(8,128)(2,1)...) custom-call(bf16[128,1536]{1,0:T(8,128)(2,1)} %multiply_convert_fusion., ...), custom_call_target="tpu_custom_call" | custom-call | tf_op jit(solution)/shard_map/attention_forward/pallas_call | solution.py:1881
  414.3 1.3 multiply_reduce_fusion.6
  415.7 0.9 multiply_convert_fusion.x_ref
  416.6 65.1 %experts_forward.3 = (f32[128,1536]{1,0:T(8,128)}, bf16[8,128,1536]{2,1,0:T(8,128)(2,1)}, bf16[8,128,1024]{2,1,0:T(8,128)(2,1)}, bf16[8,128,1024]{2,1,0:T(8,128)(2,1)}) custom-call(bf16[128,1536]{1,0:T(8,128)(2,1)} %multiply_convert_fusion.x_ref, f32[8,128,2]{2,1,0:T(8,128)} %get-tuple-element.148.share_ref, bf16[2,7,1536,512]{3,2,1,0:T(8,128)(2,1)} %get-tuple-element.56.mats_ref), custom_call_target="tpu_custom_call" | custom-call | tf_op jit(solution)/shard_map/experts_forward/pallas_call | solution.py:1107
  481.7 67.7 %experts_backward.2 = (f32[128,1536]{1,0:T(8,128)}, bf16[8,128,1536]{2,1,0:T(8,128)(2,1)}, bf16[8,128,1024]{2,1,0:T(8,128)(2,1)}, bf16[8,128,1024]{2,1,0:T(8,128)(2,1)}, bf16[8,128,1024]{2,1,0:T(8,128)(2,1)}) custom-call(bf16[128,1536]{1,0:T(8,128)(2,1)} %bitcast.145, f32[8,128,2]{2,1,0:T(8,128)} %get-tuple-element.148.share_ref, ...), custom_call_target="tpu_custom_call" | custom-call | tf_op jit(solution)/shard_map/experts_backward/pallas_call | solution.py:1211
  549.4 2.0 multiply_reduce_fusion
  551.4 2.1 fusion.33.x_ref
  553.6 71.7 %attention_backward.2 = (f32[128,1536]{1,0:T(8,128)}, bf16[8,128,1536]{2,1,0:T(8,128)(2,1)}, bf16[8,128,384]{2,1,0:T(8,128)(2,1)}) custom-call(bf16[128,1536]{1,0:T(8,128)(2,1)} %fusion.33.x_ref, bf16[2,7,1536,512]{3,2,1,0:T(8,128)(2,1)} %get-tuple-element.56.mats_ref, f32[1024,128]{1,0:T(8,128)} %get-tuple-element.179.cos_ref, ...), custom_call_target="tpu_custom_call" | custom-call | tf_op jit(solution)/shard_map/attention_backward/pallas_call | solution.py:2014
  625.3 2.0 multiply_reduce_fusion.1
  627.3 3.0 fusion.35
  630.2 67.0 %experts_backward.3 = (f32[128,1536]{1,0:T(8,128)}, bf16[8,128,1536]{2,1,0:T(8,128)(2,1)}, bf16[8,128,1024]{2,1,0:T(8,128)(2,1)}, bf16[8,128,1024]{2,1,0:T(8,128)(2,1)}, bf16[8,128,1024]{2,1,0:T(8,128)(2,1)}) custom-call(bf16[128,1536]{1,0:T(8,128)(2,1)} %get-tuple-element.117.x_ref, f32[8,128,2]{2,1,0:T(8,128)} %get-tuple-element.149.share_ref, ...), custom_call_target="tpu_custom_call" | custom-call | tf_op jit(solution)/shard_map/experts_backward/pallas_call | solution.py:1211
  697.3 1.4 multiply_reduce_fusion.2
  698.7 2.1 fusion.34
  700.8 71.9 %attention_backward.3 = (f32[128,1536]{1,0:T(8,128)}, bf16[8,128,1536]{2,1,0:T(8,128)(2,1)}, bf16[8,128,384]{2,1,0:T(8,128)(2,1)}) custom-call(bf16[128,1536]{1,0:T(8,128)(2,1)} %get-tuple-element.115.x_ref, bf16[2,7,1536,512]{3,2,1,0:T(8,128)(2,1)} %get-tuple-element.56.mats_ref, f32[1024,128]{1,0:T(8,128)} %get-tuple-element.179.cos_ref, ...), custom_call_target="tpu_custom_call" | custom-call | tf_op jit(solution)/shard_map/attention_backward/pallas_call | solution.py:2014
  772.7 1.4 fusion.10
  774.2 2.3 fusion.9
  777.1 0.7 pad.15.refs_18_
  777.7 182.9 %collect_grads.1 = (bf16[2,8,7,48,512]{4,3,2,1,0:T(8,128)(2,1)}, f32[8,8,128]{2,1,0:T(8,128)}) custom-call(bf16[1024,1536]{1,0:T(8,128)(2,1)} %bitcast.146, bf16[1024,384]{1,0:T(8,128)(2,1)} %bitcast.173, bf16[1024,1536]{1,0:T(8,128)(2,1)} %bitcast.153, bf16[1024,192]{1,0:T(8,128)(2,1)} %bitcast.174, bf16[1024,1536]{1,0:T(8,128)(2,1)} %bitcast.147, ...), custom_call_target="tpu_custom_call" | custom-call | tf_op jit(solution)/shard_map/collect_grads/pallas_call | solution.py:1744
  960.6 3.0 slice_bitcast_fusion.1
  963.7 1.5 copy-done
  965.8 0.8 convert_element_type.354
  966.6 1.8 maximum_convert_fusion.3
  968.4 1.0 slice_bitcast_fusion.8
  969.8 0.7 maximum_convert_fusion.5
  970.9 0.7 maximum_convert_fusion.6
  972.1 0.9 maximum_convert_fusion.4
  972.9 0.6 pad_maximum_fusion.4
  973.5 0.6 pad_maximum_fusion.5
  974.1 1.9 fusion.37
  976.2 1.9 maximum_convert_fusion
  978.1 1.9 maximum_convert_fusion.1
  979.9 1.9 maximum_convert_fusion.2
  (139 shorter events, 6.4 us)
Async XLA Ops:
  2.8 2.2 copy-start.4
  5.2 2.5 copy-start.5
  7.9 1.3 copy-start.7
  7.9 2.2 copy-start.8
  9.2 1.9 copy-start.9
  9.2 2.7 copy-start.10
  27.0 0.7 copy-start.18
  27.0 0.7 copy-start.19
  27.0 0.7 copy-start.27
  27.1 0.8 copy-start.28
  189.4 1.8 copy-start.1
  189.4 2.9 copy-start.26
  189.4 3.0 copy-start.29
  191.4 0.9 copy-start.22
  273.7 67.7 %copy-start.11 = (f32[1536]{0:T(1024)}, f32[1536]{0:T(1024)S(1)}, u32[]{:S(2)}) copy-start(f32[1536]{0:T(1024)S(1)} %mul.277) | copy-start | bytes 18436
  273.7 67.7 %copy-start.20 = (f32[128]{0:T(128)}, f32[128]{0:T(128)S(1)}, u32[]{:S(2)}) copy-start(f32[128]{0:T(128)S(1)} %add_rsqrt_fusion.2) | copy-start | bytes 1540
  342.8 71.5 %copy-start.13 = (f32[1536]{0:T(1024)}, f32[1536]{0:T(1024)S(1)}, u32[]{:S(2)}) copy-start(f32[1536]{0:T(1024)S(1)} %mul.283) | copy-start | bytes 18436
  342.8 71.5 %copy-start.24 = (f32[128]{0:T(128)}, f32[128]{0:T(128)S(1)}, u32[]{:S(2)}) copy-start(f32[128]{0:T(128)S(1)} %add_rsqrt_fusion.1) | copy-start | bytes 1540
  481.7 69.7 %copy-start.3 = (bf16[1,128,1536]{2,1,0:T(8,128)(2,1)S(1)}, bf16[1,128,1536]{2,1,0:T(8,128)(2,1)}, u32[]{:S(2)}) copy-start(bf16[1,128,1536]{2,1,0:T(8,128)(2,1)} %param.16) | copy-start | bytes 1179652
  553.6 71.7 %copy-start.14 = (f32[1536]{0:T(1024)S(1)}, f32[1536]{0:T(1024)}, u32[]{:S(2)}) copy-start(f32[1536]{0:T(1024)} %copy-done.13) | copy-start | bytes 18436
  553.6 71.7 %copy-start.25 = (f32[128]{0:T(128)S(1)}, f32[128]{0:T(128)}, u32[]{:S(2)}) copy-start(f32[128]{0:T(128)} %copy-done.24) | copy-start | bytes 1540
  553.6 73.7 %copy-start.2 = (f32[128,1536]{1,0:T(8,128)S(1)}, f32[128,1536]{1,0:T(8,128)}, u32[]{:S(2)}) copy-start(f32[128,1536]{1,0:T(8,128)} %get-tuple-element.63) | copy-start | bytes 2359300
  630.2 67.0 %copy-start.12 = (f32[1536]{0:T(1024)S(1)}, f32[1536]{0:T(1024)}, u32[]{:S(2)}) copy-start(f32[1536]{0:T(1024)} %copy-done.11) | copy-start | bytes 18436
  630.2 67.0 %copy-start.21 = (f32[128]{0:T(128)S(1)}, f32[128]{0:T(128)}, u32[]{:S(2)}) copy-start(f32[128]{0:T(128)} %copy-done.20) | copy-start | bytes 1540
  630.2 68.5 %copy-start.6 = (f32[128,1536]{1,0:T(8,128)S(1)}, f32[128,1536]{1,0:T(8,128)}, u32[]{:S(2)}) copy-start(f32[128,1536]{1,0:T(8,128)} %get-tuple-element.118) | copy-start | bytes 2359300
  700.8 71.9 %copy-start.23 = (f32[128]{0:T(128)S(1)}, f32[128]{0:T(128)}, u32[]{:S(2)}) copy-start(f32[128]{0:T(128)} %copy-done.22) | copy-start | bytes 1540
  772.7 3.8 copy-start.15
  772.7 3.9 copy-start.16
  963.6 1.5 copy-start
  970.5 2.4 copy-start.17

commit v5 on v4

--- a/solution.py
+++ b/solution.py
@@ -705,9 +705,11 @@
         self.above = (self.z + 1) * NX + self.x
         self.below = (self.z - 1) * NX + self.x
 
-    def greet(self):
+    def greet(self, others=()):
         barrier = pltpu.get_barrier_semaphore()
         greet(barrier, self.mate, self.fsdp)
+        for other in others:
+            greet(barrier, self.ctx, other)
 
         @pl.when(self.z > 0)
         def _():
@@ -718,7 +720,7 @@
             greet(barrier, self.above, self.fsdp)
 
         ends = jnp.where(self.z > 0, 1, 0) + jnp.where(self.z < self.nz - 1, 1, 0)
-        pl.semaphore_wait(barrier, 1 + ends)
+        pl.semaphore_wait(barrier, 1 + len(others) + ends)
 
     def near(self, i):
         z, nz = self.z, self.nz
@@ -1357,6 +1359,7 @@
     line = Line(nz)
     ctx, fsdp = line.ctx, line.fsdp
     layers = w_ref.shape[0]
+    spread = layers - 1
     y, core = fsdp // NCORE, fsdp % NCORE
     y_mate = (1 - y) * NCORE + core
     c_mate = y * NCORE + 1 - core
@@ -1394,17 +1397,22 @@
         for i in range(nz - 1):
             exchange.send(line.far(i))
         exchange.send(line.z)
-        over_y(layer, ctx, fsdp, w_ref.at[layer, ctx]).start()
-        over_c(layer, ctx, fsdp, 0, w_ref.at[layer, ctx]).start()
+        if layer < spread:
+            over_y(layer, ctx, fsdp, w_ref.at[layer, ctx]).start()
+            over_c(layer, ctx, fsdp, 0, w_ref.at[layer, ctx]).start()
         own(layer).start()
 
     def arrived(layer, frm):
-        over_y(layer, frm, fsdp).start()
-        over_c(layer, frm, fsdp, 0).start()
+        @pl.when(layer < spread)
+        def _():
+            over_y(layer, frm, fsdp).start()
+            over_c(layer, frm, fsdp, 0).start()
 
     def from_y(layer, frm):
-        over_y(layer, frm, y_mate).wait_recv()
-        over_c(layer, frm, y_mate, 1).start()
+        @pl.when(layer < spread)
+        def _():
+            over_y(layer, frm, y_mate).wait_recv()
+            over_c(layer, frm, y_mate, 1).start()
 
     def take(layer, i):
         exchange = swap(layer)
@@ -1471,7 +1479,7 @@
         lax.fori_loop(0, layers, each, 0)
         return carry
 
-    lax.fori_loop(0, steps + 1 + LAG * (layers - 1), step, 0)
+    lax.fori_loop(0, steps - 1 + LAG * (layers - 1), step, 0)
     small_own.wait()
     for k in range(nctx):
         if k:
@@ -1492,12 +1500,16 @@
 
     def close(layer, carry):
         own(layer).wait()
-        for frm in range(nctx):
-            over_c(layer, frm, c_mate, 0).wait_recv()
-            over_c(layer, frm, y_c_mate, 1).wait_recv()
-            over_c(layer, frm, fsdp, 0).wait_send()
-            over_c(layer, frm, y_mate, 1).wait_send()
-            over_y(layer, frm, fsdp).wait_send()
+
+        @pl.when(layer < spread)
+        def _():
+            for frm in range(nctx):
+                over_c(layer, frm, c_mate, 0).wait_recv()
+                over_c(layer, frm, y_c_mate, 1).wait_recv()
+                over_c(layer, frm, fsdp, 0).wait_send()
+                over_c(layer, frm, y_mate, 1).wait_send()
+                over_y(layer, frm, fsdp).wait_send()
+
         swap(layer).finish()
         return carry
 
@@ -1512,7 +1524,7 @@
             jax.ShapeDtypeStruct((layers, mats, nctx * nfs * rows, width), send.dtype),
             jax.ShapeDtypeStruct((nctx * nfs,) + small.shape[1:], small.dtype),
         ),
-        in_specs=[VM, VM],
+        in_specs=[ANY, VM],
         out_specs=(ANY, ANY),
         scratch_shapes=Exchange.scratch(nctx // NX, (mats, rows, width), (layers,))
         + [
@@ -1527,6 +1539,47 @@
         compiler_params=params(3, 40),
         name="spread_weights",
     )(send, small)
+
+
+class Spread:
+    @staticmethod
+    def scratch(nctx):
+        return [DMA((2, nctx)), DMA((2, 2, nctx))]
+
+    def __init__(self, line, mats, layer, nfs, y_sem, c_sem):
+        self.line, self.mats, self.layer, self.nfs, self.y_sem, self.c_sem = line, mats, layer, nfs, y_sem, c_sem
+        y, core = line.fsdp // NCORE, line.fsdp % NCORE
+        self.y_mate = (1 - y) * NCORE + core
+        self.c_mate = y * NCORE + 1 - core
+        self.nctx = line.nz * NX
+        self.rows = mats.shape[2] // (self.nctx * nfs)
+
+    def place(self, frm, f):
+        at = pl.multiple_of((frm * self.nfs + f) * self.rows, self.rows)
+        return self.mats.at[self.layer, :, pl.ds(at, self.rows), :]
+
+    def over_y(self, frm):
+        place = self.place(frm, self.line.fsdp)
+        return remote(place, place, self.y_sem.at[0, frm], self.y_sem.at[1, frm], self.line.ctx, self.y_mate)
+
+    def over_c(self, frm, k):
+        place = self.place(frm, self.y_mate if k else self.line.fsdp)
+        return remote(place, place, self.c_sem.at[0, k, frm], self.c_sem.at[1, k, frm], self.line.ctx, self.c_mate)
+
+    def start(self):
+        for frm in range(self.nctx):
+            self.over_y(frm).start()
+            self.over_c(frm, 0).start()
+
+    def take(self, frm):
+        self.over_y(frm).wait_recv()
+        self.over_c(frm, 1).start()
+
+    def finish(self):
+        for frm in range(self.nctx):
+            self.over_y(frm).wait_send()
+            for k in range(2):
+                self.over_c(frm, k).wait()
 
 
 def grads_kernel(nctx, nfs, rows, layers, *refs):
@@ -1783,10 +1836,15 @@
     return values * cos_part + swapped * sin_part
 
 
-def attention_kernel(nz, layer, x_ref, mats_ref, cos_ref, sin_ref, key_at_ref, query_at_ref,
-                     o_ref, all_out, q_ref, k_ref, v_ref, peak_ref, share_ref, att_ref,
-                     attn, out_w, blocks, part, v_turned, probs, load_sem, save_sem, gsems, work, ework, ssems, msems):
+def attention_kernel(nz, nfs, layer, x_ref, mats_ref, cos_ref, sin_ref, key_at_ref, query_at_ref,
+                     o_ref, all_out, q_ref, k_ref, v_ref, peak_ref, share_ref, att_ref, *refs):
     line = Line(nz)
+    spread = None
+    if layer == 0:
+        mats_ref, refs = refs[0], refs[1:]
+        spread = Spread(line, mats_ref, layer + 1, nfs, *refs[-2:])
+        refs = refs[:-2]
+    attn, out_w, blocks, part, v_turned, probs, load_sem, save_sem, gsems, work, ework, ssems, msems = refs
     rows, width = x_ref.shape
     pair_rows = NX * rows
     heads = q_ref.shape[1] // rows
@@ -1794,7 +1852,9 @@
     wide = -(-o_at // 128) * 128
     load = pltpu.make_async_copy(mats_ref.at[layer, 0], attn, load_sem)
     load.start()
-    line.greet()
+    line.greet((spread.y_mate, spread.c_mate) if spread else ())
+    if spread:
+        spread.start()
     ring = Gather(line, x_ref, blocks, gsems)
     blocks[line.ctx] = x_ref[...]
     ring.start()
@@ -1864,6 +1924,10 @@
         def _():
             sums.add(i - 1)
 
+        if spread:
+            for side in range(NX):
+                spread.take(i * NX + side)
+
         return carry
 
     lax.fori_loop(0, nz, step, 0)
@@ -1871,15 +1935,18 @@
     sums.finish()
     for row in range(nz):
         save(row).wait()
-
-
-def attention_rows(block, mats, layer, cos_part, sin_part, key_at, query_at, nz):
+    if spread:
+        spread.finish()
+
+
+def attention_rows(block, mats, layer, cos_part, sin_part, key_at, query_at, nz, nfs):
     rows, width = block.shape
+    spreads = layer == 0
     group = nz * NX
     group_rows = group * rows
     heads = 3
     return pl.pallas_call(
-        functools.partial(attention_kernel, nz, layer),
+        functools.partial(attention_kernel, nz, nfs, layer),
         out_shape=(
             jax.ShapeDtypeStruct((rows, width), F32),
             jax.ShapeDtypeStruct((group, rows, width), BF),
@@ -1889,9 +1956,11 @@
             jax.ShapeDtypeStruct((group, 1, heads * rows), F32),
             jax.ShapeDtypeStruct((group, 1, heads * rows), F32),
             jax.ShapeDtypeStruct((group, rows, heads * HEAD_DIM), BF),
-        ),
+        )
+        + ((jax.ShapeDtypeStruct(mats.shape, BF),) if spreads else ()),
         in_specs=[VM, ANY, VM, VM, VM, VM],
-        out_specs=(VM, ANY, VM, VM, VM, VM, VM, VM),
+        out_specs=(VM, ANY, VM, VM, VM, VM, VM, VM) + ((ANY,) if spreads else ()),
+        input_output_aliases={1: 8} if spreads else {},
         scratch_shapes=[
             pltpu.VMEM(mats.shape[2:], BF),
             pltpu.VMEM((width, heads * HEAD_DIM), BF),
@@ -1903,7 +1972,8 @@
             DMA((nz,)),
         ]
         + Gather.scratch(nz)
-        + Scatter.scratch(nz, rows, width),
+        + Scatter.scratch(nz, rows, width)
+        + (Spread.scratch(group) if spreads else []),
         compiler_params=params(9 + 2 * layer, 60),
         name="attention_forward",
     )(block, mats, cos_part, sin_part, key_at, query_at)
@@ -2128,9 +2198,10 @@
     for layer in range(LAYERS):
         attn_gain, moe_gain, share = fetched[layer]
         normed = rms_norm(hidden, attn_gain).astype(BF)
-        mixed, normed_all, queries, keys, values, peaks, sums, attended = attention_rows(
-            normed, mats_all, layer, cos_part, sin_part, key_at, query_at, nz
+        mixed, normed_all, queries, keys, values, peaks, sums, attended, *rest = attention_rows(
+            normed, mats_all, layer, cos_part, sin_part, key_at, query_at, nz, nfs
         )
+        mats_all = rest[0] if rest else mats_all
         middle = hidden + mixed
 
         moe_in = rms_norm(middle, moe_gain).astype(BF)

time: 991 us -> 972 us (0.981)
  Pallas kernels: 899 us -> 879 us
    pallas_call x1, Pallas kernels: 161 us -> 140 us  [spread_weights(): pl.pallas_call(functools.partial(weights_kernel, nctx, nfs, rows), out_sh...]
where the time goes in v5:
time: 972 us; the launch traced here: 963 us
  Pallas kernels  879 us (90%)
  other arithmetic  48 us (5%)
  local copies, waits for them, and re-layouts  33.4 us (3%)
    pallas_call x1, Pallas kernels, collect_grads(): pl.pallas_call(functools.partial(grads_kernel, nctx, nfs, rows, layers),...  185 us
    pallas_call x2, Pallas kernels, attention_rows(): pl.pallas_call(functools.partial(attention_kernel, nz, nfs, layer), out_s...  148 us
    pallas_call x2, Pallas kernels, attention_rows_back(): pl.pallas_call(functools.partial(attention_back_kernel, nz, layer), out_s...  142 us
    pallas_call x1, Pallas kernels, spread_weights(): pl.pallas_call(functools.partial(weights_kernel, nctx, nfs, rows), out_sh...  140 us
    pallas_call x2, Pallas kernels, experts_backward(): pl.pallas_call(functools.partial(experts_back_kernel, nz, layer), out_sha...  133 us
    pallas_call x2, Pallas kernels, experts_forward(): pl.pallas_call(functools.partial(experts_kernel, nz, layer), out_shape=(j...  131 us

profile of v5, /device:TPU:11, one launch (start us, length us, event | category | flops | bytes accessed | tf_op | source)
XLA Modules:
  0.0 962.7 jit_solution(18216854790920881598)
XLA Ops:
  0.6 2.1 convert.89
  2.8 1.0 fusion.40
  3.8 1.2 copy-done.4
  5.2 1.2 fusion.39
  6.5 1.2 copy-done.5
  7.9 1.3 fusion.38
  9.2 0.7 fusion.42
  10.2 0.7 fusion.41
  11.1 0.6 fusion.44
  11.9 0.6 fusion.43
  12.9 1.8 maximum_bitcast_fusion.1
  14.7 1.8 convert_element_type.330
  16.5 1.8 convert_element_type.327
  18.3 1.8 copy_bitcast_fusion.2
  20.1 1.6 convert_element_type.329
  21.7 1.6 convert_element_type.328
  23.3 1.0 copy_bitcast_fusion.6
  24.2 1.2 maximum_bitcast_fusion.2
  25.5 1.6 maximum_bitcast_fusion
  27.9 140.3 %spread_weights.1 = (bf16[2,7,1536,512]{3,2,1,0:T(8,128)(2,1)}, f32[32,16,128]{2,1,0:T(8,128)S(1)}) custom-call(bf16[2,8,7,48,512]{4,3,2,1,0:T(8,128)(2,1)S(1)} %pad_maximum_fusion.w_ref, f32[8,16,128]{2,1,0:T(8,128)S(1)} %pad_maximum_fusion.3.g_ref), custom_call_target="tpu_custom_call" | custom-call | tf_op jit(solution)/shard_map/spread_weights/pallas_call | solution.py:1521
  168.5 1.3 slice_bitcast_fusion.2
  170.3 0.9 fusion.4.x_ref
  171.7 1.9 fusion.13
  173.6 1.8 pad_maximum_fusion.1
  175.5 1.0 copy.94.key_at_ref
  176.6 0.6 pad_add_fusion.query_at_ref
  177.3 79.4 %attention_forward.2 = (f32[128,1536]{1,0:T(8,128)}, bf16[8,128,1536]{2,1,0:T(8,128)(2,1)}, bf16[8,384,64]{2,1,0:T(8,128)(2,1)}, bf16[1024,64]{1,0:T(8,128)(2,1)...) custom-call(bf16[128,1536]{1,0:T(8,128)(2,1)} %fusion.4.x_ref, ...), custom_call_target="tpu_custom_call", output_to_operand_aliasing={{8}: (1, {})} | custom-call | tf_op jit(solution)/shard_map/attention_forward/pallas_call | solution.py:1948
  256.6 1.3 multiply_reduce_fusion.8
  258.1 0.9 multiply_convert_fusion.2.x_ref
  258.9 67.6 %experts_forward.2 = (f32[128,1536]{1,0:T(8,128)}, bf16[8,128,1536]{2,1,0:T(8,128)(2,1)}, bf16[8,128,1024]{2,1,0:T(8,128)(2,1)}, bf16[8,128,1024]{2,1,0:T(8,128)(2,1)}) custom-call(bf16[128,1536]{1,0:T(8,128)(2,1)} %multiply_convert_fusion.2.x_ref, f32[8,128,2]{2,1,0:T(8,128)} %get-tuple-element.151.share_ref, ...), custom_call_target="tpu_custom_call" | custom-call | tf_op jit(solution)/shard_map/experts_forward/pallas_call | solution.py:1109
  326.6 1.3 multiply_reduce_fusion.7
  328.0 0.9 multiply_convert_fusion.1.x_ref
  328.8 68.9 %attention_forward.3 = (f32[128,1536]{1,0:T(8,128)}, bf16[8,128,1536]{2,1,0:T(8,128)(2,1)}, bf16[8,384,64]{2,1,0:T(8,128)(2,1)}, bf16[1024,64]{1,0:T(8,128)(2,1)...) custom-call(bf16[128,1536]{1,0:T(8,128)(2,1)} %multiply_convert_fusion., ...), custom_call_target="tpu_custom_call" | custom-call | tf_op jit(solution)/shard_map/attention_forward/pallas_call | solution.py:1948
  397.7 1.3 multiply_reduce_fusion.6
  399.1 0.9 multiply_convert_fusion.x_ref
  400.0 63.1 %experts_forward.3 = (f32[128,1536]{1,0:T(8,128)}, bf16[8,128,1536]{2,1,0:T(8,128)(2,1)}, bf16[8,128,1024]{2,1,0:T(8,128)(2,1)}, bf16[8,128,1024]{2,1,0:T(8,128)(2,1)}) custom-call(bf16[128,1536]{1,0:T(8,128)(2,1)} %multiply_convert_fusion.x_ref, f32[8,128,2]{2,1,0:T(8,128)} %get-tuple-element.150.share_ref, bf16[2,7,1536,512]{3,2,1,0:T(8,128)(2,1)} %get-tuple-element.59.mats_ref), custom_call_target="tpu_custom_call" | custom-call | tf_op jit(solution)/shard_map/experts_forward/pallas_call | solution.py:1109
  463.1 67.5 %experts_backward.2 = (f32[128,1536]{1,0:T(8,128)}, bf16[8,128,1536]{2,1,0:T(8,128)(2,1)}, bf16[8,128,1024]{2,1,0:T(8,128)(2,1)}, bf16[8,128,1024]{2,1,0:T(8,128)(2,1)}, bf16[8,128,1024]{2,1,0:T(8,128)(2,1)}) custom-call(bf16[128,1536]{1,0:T(8,128)(2,1)} %bitcast.145, f32[8,128,2]{2,1,0:T(8,128)} %get-tuple-element.150.share_ref, ...), custom_call_target="tpu_custom_call" | custom-call | tf_op jit(solution)/shard_map/experts_backward/pallas_call | solution.py:1213
  530.6 2.0 multiply_reduce_fusion
  532.7 2.1 fusion.33.x_ref
  534.8 71.2 %attention_backward.2 = (f32[128,1536]{1,0:T(8,128)}, bf16[8,128,1536]{2,1,0:T(8,128)(2,1)}, bf16[8,128,384]{2,1,0:T(8,128)(2,1)}) custom-call(bf16[128,1536]{1,0:T(8,128)(2,1)} %fusion.33.x_ref, bf16[2,7,1536,512]{3,2,1,0:T(8,128)(2,1)} %get-tuple-element.59.mats_ref, f32[1024,128]{1,0:T(8,128)} %get-tuple-element.181.cos_ref, ...), custom_call_target="tpu_custom_call" | custom-call | tf_op jit(solution)/shard_map/attention_backward/pallas_call | solution.py:2084
  606.1 2.0 multiply_reduce_fusion.1
  608.1 3.0 fusion.35
  611.0 65.7 %experts_backward.3 = (f32[128,1536]{1,0:T(8,128)}, bf16[8,128,1536]{2,1,0:T(8,128)(2,1)}, bf16[8,128,1024]{2,1,0:T(8,128)(2,1)}, bf16[8,128,1024]{2,1,0:T(8,128)(2,1)}, bf16[8,128,1024]{2,1,0:T(8,128)(2,1)}) custom-call(bf16[128,1536]{1,0:T(8,128)(2,1)} %get-tuple-element.119.x_ref, f32[8,128,2]{2,1,0:T(8,128)} %get-tuple-element.151.share_ref, ...), custom_call_target="tpu_custom_call" | custom-call | tf_op jit(solution)/shard_map/experts_backward/pallas_call | solution.py:1213
  676.8 1.4 multiply_reduce_fusion.2
  678.2 2.1 fusion.34
  680.4 70.6 %attention_backward.3 = (f32[128,1536]{1,0:T(8,128)}, bf16[8,128,1536]{2,1,0:T(8,128)(2,1)}, bf16[8,128,384]{2,1,0:T(8,128)(2,1)}) custom-call(bf16[128,1536]{1,0:T(8,128)(2,1)} %get-tuple-element.117.x_ref, bf16[2,7,1536,512]{3,2,1,0:T(8,128)(2,1)} %get-tuple-element.59.mats_ref, f32[1024,128]{1,0:T(8,128)} %get-tuple-element.181.cos_ref, ...), custom_call_target="tpu_custom_call" | custom-call | tf_op jit(solution)/shard_map/attention_backward/pallas_call | solution.py:2084
  751.0 1.4 fusion.10
  752.5 2.3 fusion.9
  755.4 0.7 pad.15.refs_18_
  756.1 185.1 %collect_grads.1 = (bf16[2,8,7,48,512]{4,3,2,1,0:T(8,128)(2,1)}, f32[8,8,128]{2,1,0:T(8,128)}) custom-call(bf16[1024,1536]{1,0:T(8,128)(2,1)} %bitcast.146, bf16[1024,384]{1,0:T(8,128)(2,1)} %bitcast.173, bf16[1024,1536]{1,0:T(8,128)(2,1)} %bitcast.153, bf16[1024,192]{1,0:T(8,128)(2,1)} %bitcast.174, bf16[1024,1536]{1,0:T(8,128)(2,1)} %bitcast.147, ...), custom_call_target="tpu_custom_call" | custom-call | tf_op jit(solution)/shard_map/collect_grads/pallas_call | solution.py:1797
  941.1 3.0 slice_bitcast_fusion.1
  944.1 1.5 copy-done
  946.3 0.8 convert_element_type.354
  947.1 1.8 maximum_convert_fusion.3
  948.9 1.0 slice_bitcast_fusion.8
  950.3 0.7 maximum_convert_fusion.5
  951.4 0.7 maximum_convert_fusion.6
  952.5 0.9 maximum_convert_fusion.4
  953.4 0.6 pad_maximum_fusion.4
  954.0 0.6 pad_maximum_fusion.5
  954.6 1.9 fusion.37
  956.7 1.9 maximum_convert_fusion
  958.5 1.9 maximum_convert_fusion.1
  960.4 1.9 maximum_convert_fusion.2
  (139 shorter events, 6.4 us)
Async XLA Ops:
  2.8 2.2 copy-start.4
  5.2 2.5 copy-start.5
  7.9 1.3 copy-start.7
  7.9 2.2 copy-start.8
  9.2 1.9 copy-start.9
  9.2 2.7 copy-start.10
  27.0 0.7 copy-start.18
  27.0 0.7 copy-start.19
  27.0 0.7 copy-start.27
  27.1 0.8 copy-start.28
  168.3 1.8 copy-start.1
  168.3 2.9 copy-start.26
  168.3 3.0 copy-start.29
  170.3 0.9 copy-start.22
  258.0 68.5 %copy-start.11 = (f32[1536]{0:T(1024)}, f32[1536]{0:T(1024)S(1)}, u32[]{:S(2)}) copy-start(f32[1536]{0:T(1024)S(1)} %mul.277) | copy-start | bytes 18436
  258.1 68.5 %copy-start.20 = (f32[128]{0:T(128)}, f32[128]{0:T(128)S(1)}, u32[]{:S(2)}) copy-start(f32[128]{0:T(128)S(1)} %add_rsqrt_fusion.2) | copy-start | bytes 1540
  327.9 69.8 %copy-start.13 = (f32[1536]{0:T(1024)}, f32[1536]{0:T(1024)S(1)}, u32[]{:S(2)}) copy-start(f32[1536]{0:T(1024)S(1)} %mul.283) | copy-start | bytes 18436
  327.9 69.8 %copy-start.24 = (f32[128]{0:T(128)}, f32[128]{0:T(128)S(1)}, u32[]{:S(2)}) copy-start(f32[128]{0:T(128)S(1)} %add_rsqrt_fusion.1) | copy-start | bytes 1540
  463.1 69.5 %copy-start.3 = (bf16[1,128,1536]{2,1,0:T(8,128)(2,1)S(1)}, bf16[1,128,1536]{2,1,0:T(8,128)(2,1)}, u32[]{:S(2)}) copy-start(bf16[1,128,1536]{2,1,0:T(8,128)(2,1)} %param.16) | copy-start | bytes 1179652
  534.8 71.2 %copy-start.14 = (f32[1536]{0:T(1024)S(1)}, f32[1536]{0:T(1024)}, u32[]{:S(2)}) copy-start(f32[1536]{0:T(1024)} %copy-done.13) | copy-start | bytes 18436
  534.8 71.2 %copy-start.25 = (f32[128]{0:T(128)S(1)}, f32[128]{0:T(128)}, u32[]{:S(2)}) copy-start(f32[128]{0:T(128)} %copy-done.24) | copy-start | bytes 1540
  534.8 73.3 %copy-start.2 = (f32[128,1536]{1,0:T(8,128)S(1)}, f32[128,1536]{1,0:T(8,128)}, u32[]{:S(2)}) copy-start(f32[128,1536]{1,0:T(8,128)} %get-tuple-element.65) | copy-start | bytes 2359300
  611.0 65.7 %copy-start.12 = (f32[1536]{0:T(1024)S(1)}, f32[1536]{0:T(1024)}, u32[]{:S(2)}) copy-start(f32[1536]{0:T(1024)} %copy-done.11) | copy-start | bytes 18436
  611.0 65.7 %copy-start.21 = (f32[128]{0:T(128)S(1)}, f32[128]{0:T(128)}, u32[]{:S(2)}) copy-start(f32[128]{0:T(128)} %copy-done.20) | copy-start | bytes 1540
  611.0 67.2 %copy-start.6 = (f32[128,1536]{1,0:T(8,128)S(1)}, f32[128,1536]{1,0:T(8,128)}, u32[]{:S(2)}) copy-start(f32[128,1536]{1,0:T(8,128)} %get-tuple-element.120) | copy-start | bytes 2359300
  680.4 70.7 %copy-start.23 = (f32[128]{0:T(128)S(1)}, f32[128]{0:T(128)}, u32[]{:S(2)}) copy-start(f32[128]{0:T(128)} %copy-done.22) | copy-start | bytes 1540
  751.0 3.8 copy-start.15
  751.0 3.9 copy-start.16
  944.1 1.5 copy-start
  951.0 2.4 copy-start.17

commit v6 on v5

--- a/solution.py
+++ b/solution.py
@@ -1038,19 +1038,34 @@
                 self.extra_down(row).wait_send()
 
 
+def normed_rows(values_ref, gain_ref):
+    values = values_ref[...]
+    scale = lax.rsqrt(jnp.mean(values * values, axis=1, keepdims=True) + EPSILON)
+    return (values * scale * gain_ref[...]).astype(BF)
+
+
+def norm_back_rows(grad_ref, values_ref, gain_ref, sums_ref, gain_out):
+    values, sums = values_ref[...], sums_ref[...]
+    scale = lax.rsqrt(jnp.mean(values * values, axis=1, keepdims=True) + EPSILON)
+    unit = values * scale
+    gain_out[...] = jnp.sum(sums * unit, axis=0, keepdims=True)
+    pulled = sums * gain_ref[...]
+    sums_ref[...] = grad_ref[...] + scale * (pulled - unit * jnp.mean(pulled * unit, axis=1, keepdims=True))
+
+
 def params(collective, vmem_mib):
     return pltpu.CompilerParams(collective_id=collective, has_side_effects=True, vmem_limit_bytes=vmem_mib << 20)
 
 
-def experts_kernel(nz, layer, x_ref, share_ref, mats_ref, o_ref, all_out, gate_out, up_out,
+def experts_kernel(nz, layer, x_ref, gain_ref, share_ref, mats_ref, o_ref, all_out, gate_out, up_out,
                    mats, blocks, part, gate, up, load_sem, save_sem, gsems, work, ework, ssems, msems):
     line = Line(nz)
     rows, width = x_ref.shape
     load = pltpu.make_async_copy(mats_ref.at[layer, pl.ds(1, 6)], mats, load_sem)
     load.start()
+    blocks[line.ctx] = normed_rows(x_ref, gain_ref)
     line.greet()
-    ring = Gather(line, x_ref, blocks, gsems)
-    blocks[line.ctx] = x_ref[...]
+    ring = Gather(line, blocks.at[line.ctx], blocks, gsems)
     ring.start()
     load.wait()
     ring.start_extras()
@@ -1096,12 +1111,13 @@
     for i in range(nz):
         sums.add(i)
     sums.finish()
+    o_ref[...] += x_ref[...]
     for row in range(nz):
         for save in saves(row):
             save.wait()
 
 
-def experts_forward(block, share, mats, layer, nz):
+def experts_forward(block, gain, share, mats, layer, nz):
     rows, width = block.shape
     units = mats.shape[3]
     group = nz * NX
@@ -1114,7 +1130,7 @@
             acts,
             acts,
         ),
-        in_specs=[VM, VM, ANY],
+        in_specs=[VM, VM, VM, ANY],
         out_specs=(VM, ANY, ANY, ANY),
         scratch_shapes=[
             pltpu.VMEM((6, width, units), BF),
@@ -1129,10 +1145,10 @@
         + Scatter.scratch(nz, rows, width),
         compiler_params=params(5 + 2 * layer, 60),
         name="experts_forward",
-    )(block, share, mats)
-
-
-def experts_back_kernel(nz, layer, x_ref, share_ref, mats_ref, gate_ref, up_ref, o_ref, all_out, dgate_out, dup_out, inner_out,
+    )(block, gain, share, mats)
+
+
+def experts_back_kernel(nz, layer, x_ref, values_ref, gain_ref, share_ref, mats_ref, gate_ref, up_ref, o_ref, gain_out, all_out, dgate_out, dup_out, inner_out,
                         mats, blocks, part, gate, up, inners, load_sem, save_sem, gsems, work, ework, ssems, msems):
     line = Line(nz)
     rows, width = x_ref.shape
@@ -1143,9 +1159,9 @@
     )
     for load in loads:
         load.start()
+    blocks[line.ctx] = x_ref[...].astype(BF)
     line.greet()
-    ring = Gather(line, x_ref, blocks, gsems)
-    blocks[line.ctx] = x_ref[...]
+    ring = Gather(line, blocks.at[line.ctx], blocks, gsems)
     ring.start()
     for load in loads:
         load.wait()
@@ -1199,12 +1215,13 @@
     for i in range(nz):
         sums.add(i)
     sums.finish()
+    norm_back_rows(x_ref, values_ref, gain_ref, o_ref, gain_out)
     for row in range(nz):
         for save in saves(row):
             save.wait()
 
 
-def experts_backward(block, share, mats, layer, gate_act, up_act, nz):
+def experts_backward(block, values, gain, share, mats, layer, gate_act, up_act, nz):
     rows, width = block.shape
     units = mats.shape[3]
     group = nz * NX
@@ -1214,13 +1231,14 @@
         functools.partial(experts_back_kernel, nz, layer),
         out_shape=(
             jax.ShapeDtypeStruct((rows, width), F32),
+            jax.ShapeDtypeStruct((1, width), F32),
             jax.ShapeDtypeStruct((group, rows, width), BF),
             acts,
             acts,
             acts,
         ),
-        in_specs=[VM, VM, ANY, ANY, ANY],
-        out_specs=(VM, ANY, ANY, ANY, ANY),
+        in_specs=[VM, VM, VM, VM, ANY, ANY, ANY],
+        out_specs=(VM, VM, ANY, ANY, ANY, ANY),
         scratch_shapes=[
             pltpu.VMEM((6, width, units), BF),
             pltpu.VMEM((group, rows, width), BF),
@@ -1235,7 +1253,7 @@
         + Scatter.scratch(nz, rows, width),
         compiler_params=params(6 + 2 * layer, 60),
         name="experts_backward",
-    )(block, share, mats, gate_act, up_act)
+    )(block, values, gain, share, mats, gate_act, up_act)
 
 
 def far_of(nz, z, i):
@@ -1354,7 +1372,7 @@
 LAG = 3
 
 
-def weights_kernel(nctx, nfs, rows, w_ref, g_ref, o_ref, go_ref, passing, for_mate, zs, xs, own_sem, y_sem, c_sem, gown_sem, gp_sem, gy_sem, gc_sem):
+def weights_kernel(nctx, nfs, rows, attn_ref, gate_ref, up_ref, down_ref, g_ref, o_ref, go_ref, w_ref, stage, stage_sem, passing, for_mate, zs, xs, own_sem, y_sem, c_sem, gown_sem, gp_sem, gy_sem, gc_sem):
     nz = nctx // NX
     line = Line(nz)
     ctx, fsdp = line.ctx, line.fsdp
@@ -1364,6 +1382,31 @@
     y_mate = (1 - y) * NCORE + core
     c_mate = y * NCORE + 1 - core
     y_c_mate = (1 - y) * NCORE + 1 - core
+
+    def load(layer):
+        return [
+            pltpu.make_async_copy(src.at[layer], stage.at[layer, k], stage_sem.at[layer, k])
+            for k, src in enumerate((gate_ref, up_ref, down_ref))
+        ]
+
+    for layer in range(layers):
+        for copy in load(layer):
+            copy.start()
+
+    def pack(layer):
+        for copy in load(layer):
+            copy.wait()
+
+        def one(to, carry):
+            w_ref[layer, to, 0] = attn_ref[layer, to]
+            for k in range(3):
+                for e in range(2):
+                    w_ref[layer, to, 1 + 2 * k + e] = stage[layer, k, 2 * to + e].astype(BF)
+            return carry
+
+        lax.fori_loop(0, nctx, one, 0)
+
+    pack(0)
     barrier = pltpu.get_barrier_semaphore()
     for step in range(1, nctx):
         greet(barrier, (ctx + step) % nctx, fsdp)
@@ -1393,6 +1436,8 @@
         return pltpu.make_async_copy(w_ref.at[layer, ctx], place(layer, ctx, fsdp), own_sem.at[layer])
 
     def begin(layer):
+        if layer:
+            pack(layer)
         exchange = swap(layer)
         for i in range(nz - 1):
             exchange.send(line.far(i))
@@ -1516,17 +1561,23 @@
     lax.fori_loop(0, layers, close, 0)
 
 
-def spread_weights(send, small, nfs):
-    layers, nctx, mats, rows, width = send.shape
+def spread_weights(attn, gate, up, down, small, nfs):
+    layers, nctx, rows, width = attn.shape
+    mats = 7
     return pl.pallas_call(
         functools.partial(weights_kernel, nctx, nfs, rows),
         out_shape=(
-            jax.ShapeDtypeStruct((layers, mats, nctx * nfs * rows, width), send.dtype),
+            jax.ShapeDtypeStruct((layers, mats, nctx * nfs * rows, width), BF),
             jax.ShapeDtypeStruct((nctx * nfs,) + small.shape[1:], small.dtype),
         ),
-        in_specs=[ANY, VM],
+        in_specs=[VM, ANY, ANY, ANY, VM],
         out_specs=(ANY, ANY),
-        scratch_shapes=Exchange.scratch(nctx // NX, (mats, rows, width), (layers,))
+        scratch_shapes=[
+            pltpu.VMEM((layers, nctx, mats, rows, width), BF),
+            pltpu.VMEM((layers, 3) + gate.shape[1:], F32),
+            DMA((layers, 3)),
+        ]
+        + Exchange.scratch(nctx // NX, (mats, rows, width), (layers,))
         + [
             DMA((layers,)),
             DMA((2, layers, nctx)),
@@ -1536,9 +1587,9 @@
             DMA((2, nctx)),
             DMA((2, 2, nctx)),
         ],
-        compiler_params=params(3, 40),
+        compiler_params=params(3, 63),
         name="spread_weights",
-    )(send, small)
+    )(attn, gate, up, down, small)
 
 
 class Spread:
@@ -1836,7 +1887,7 @@
     return values * cos_part + swapped * sin_part
 
 
-def attention_kernel(nz, nfs, layer, x_ref, mats_ref, cos_ref, sin_ref, key_at_ref, query_at_ref,
+def attention_kernel(nz, nfs, layer, x_ref, gain_ref, mats_ref, cos_ref, sin_ref, key_at_ref, query_at_ref,
                      o_ref, all_out, q_ref, k_ref, v_ref, peak_ref, share_ref, att_ref, *refs):
     line = Line(nz)
     spread = None
@@ -1852,11 +1903,11 @@
     wide = -(-o_at // 128) * 128
     load = pltpu.make_async_copy(mats_ref.at[layer, 0], attn, load_sem)
     load.start()
+    blocks[line.ctx] = normed_rows(x_ref, gain_ref)
     line.greet((spread.y_mate, spread.c_mate) if spread else ())
     if spread:
         spread.start()
-    ring = Gather(line, x_ref, blocks, gsems)
-    blocks[line.ctx] = x_ref[...]
+    ring = Gather(line, blocks.at[line.ctx], blocks, gsems)
     ring.start()
     load.wait()
     out_w[...] = attn[:, o_at:]
@@ -1933,13 +1984,14 @@
     lax.fori_loop(0, nz, step, 0)
     sums.add(nz - 1)
     sums.finish()
+    o_ref[...] += x_ref[...]
     for row in range(nz):
         save(row).wait()
     if spread:
         spread.finish()
 
 
-def attention_rows(block, mats, layer, cos_part, sin_part, key_at, query_at, nz, nfs):
+def attention_rows(block, gain, mats, layer, cos_part, sin_part, key_at, query_at, nz, nfs):
     rows, width = block.shape
     spreads = layer == 0
     group = nz * NX
@@ -1958,9 +2010,9 @@
             jax.ShapeDtypeStruct((group, rows, heads * HEAD_DIM), BF),
         )
         + ((jax.ShapeDtypeStruct(mats.shape, BF),) if spreads else ()),
-        in_specs=[VM, ANY, VM, VM, VM, VM],
+        in_specs=[VM, VM, ANY, VM, VM, VM, VM],
         out_specs=(VM, ANY, VM, VM, VM, VM, VM, VM) + ((ANY,) if spreads else ()),
-        input_output_aliases={1: 8} if spreads else {},
+        input_output_aliases={2: 8} if spreads else {},
         scratch_shapes=[
             pltpu.VMEM(mats.shape[2:], BF),
             pltpu.VMEM((width, heads * HEAD_DIM), BF),
@@ -1976,11 +2028,11 @@
         + (Spread.scratch(group) if spreads else []),
         compiler_params=params(9 + 2 * layer, 60),
         name="attention_forward",
-    )(block, mats, cos_part, sin_part, key_at, query_at)
-
-
-def attention_back_kernel(nz, layer, x_ref, mats_ref, cos_ref, sin_ref, key_at_ref, query_at_ref, q_ref, k_ref, v_ref, peak_ref, share_ref,
-                          o_ref, all_out, dproj_ref,
+    )(block, gain, mats, cos_part, sin_part, key_at, query_at)
+
+
+def attention_back_kernel(nz, layer, x_ref, values_ref, gain_ref, mats_ref, cos_ref, sin_ref, key_at_ref, query_at_ref, q_ref, k_ref, v_ref, peak_ref, share_ref,
+                          o_ref, gain_out, all_out, dproj_ref,
                           attn, out_w, blocks, part, k_turned, probs, slopes, dq, dk, dv, load_sem, save_sem, gsems, work, ework, ssems, msems):
     line = Line(nz)
     rows, width = x_ref.shape
@@ -1991,9 +2043,9 @@
     scale = HEAD_DIM**-0.5
     load = pltpu.make_async_copy(mats_ref.at[layer, 0], attn, load_sem)
     load.start()
+    blocks[line.ctx] = x_ref[...].astype(BF)
     line.greet()
-    ring = Gather(line, x_ref, blocks, gsems)
-    blocks[line.ctx] = x_ref[...]
+    ring = Gather(line, blocks.at[line.ctx], blocks, gsems)
     ring.start()
     k_turned[...] = k_ref[...].astype(F32).T.astype(BF)
     dk[...] = jnp.zeros(dk.shape, F32)
@@ -2071,11 +2123,12 @@
     lax.fori_loop(0, nz, step, 0)
     sums.add(nz - 1)
     sums.finish()
+    norm_back_rows(x_ref, values_ref, gain_ref, o_ref, gain_out)
     for row in range(nz):
         save(row).wait()
 
 
-def attention_rows_back(block, mats, layer, cos_part, sin_part, key_at, query_at, queries, keys, values, peaks, shares, nz):
+def attention_rows_back(block, values_in, gain, mats, layer, cos_part, sin_part, key_at, query_at, queries, keys, values, peaks, shares, nz):
     rows, width = block.shape
     group = nz * NX
     group_rows = group * rows
@@ -2085,11 +2138,12 @@
         functools.partial(attention_back_kernel, nz, layer),
         out_shape=(
             jax.ShapeDtypeStruct((rows, width), F32),
+            jax.ShapeDtypeStruct((1, width), F32),
             jax.ShapeDtypeStruct((group, rows, width), BF),
             jax.ShapeDtypeStruct((group, rows, wide), BF),
         ),
-        in_specs=[VM, ANY] + [VM] * 9,
-        out_specs=(VM, ANY, VM),
+        in_specs=[VM, VM, VM, ANY] + [VM] * 9,
+        out_specs=(VM, VM, ANY, VM),
         scratch_shapes=[
             pltpu.VMEM(mats.shape[2:], BF),
             pltpu.VMEM((width, heads * HEAD_DIM), BF),
@@ -2108,7 +2162,7 @@
         + Scatter.scratch(nz, rows, width),
         compiler_params=params(10 + 2 * layer, 60),
         name="attention_backward",
-    )(block, mats, cos_part, sin_part, key_at, query_at, queries, keys, values, peaks, shares)
+    )(block, values_in, gain, mats, cos_part, sin_part, key_at, query_at, queries, keys, values, peaks, shares)
 
 
 def rope_tables(places):
@@ -2119,35 +2173,18 @@
     return jnp.cos(angles), jnp.sin(angles)
 
 
-def pack_weights(master_set, layer, nctx):
-    query_weight, key_weight, value_weight, out_weight, attn_gain, moe_gain, gate_weight, up_weight, down_weight = master_set
-    rows = query_weight.shape[1]
+def pack_weights(master_set, nctx):
+    query_weight, key_weight, value_weight, out_weight, attn_gain, moe_gain = master_set[:6]
+    layers, rows = query_weight.shape[:2]
 
     def columns(master):
-        low = master[layer].astype(BF).reshape(rows, nctx, -1)
-        return low.transpose(1, 0, 2)
+        return master.astype(BF).reshape(layers, rows, nctx, -1).transpose(0, 2, 1, 3)
 
     attn = jnp.concatenate(
         [columns(query_weight), columns(key_weight), columns(value_weight), columns(out_weight)], axis=-1
     )
-
-    def experts(master):
-        low = master[layer].astype(BF)
-        return low.reshape(nctx, -1, rows, low.shape[-1])
-
-    send = jnp.concatenate(
-        [attn[:, None], experts(gate_weight), experts(up_weight), experts(down_weight)], axis=1
-    )
-    gains = jnp.stack([attn_gain[layer], moe_gain[layer]]).astype(BF).astype(F32)
-    return send, jnp.pad(gains, ((0, 0), (0, 128 - rows)))
-
-
-def norm_back(values, gain, grad):
-    scale = lax.rsqrt(jnp.mean(values * values, axis=-1, keepdims=True) + EPSILON)
-    unit = values * scale
-    grad_gain = jnp.sum(grad * unit, axis=0)
-    pulled = grad * gain
-    return scale * (pulled - unit * jnp.mean(pulled * unit, axis=-1, keepdims=True)), grad_gain
+    gains = jnp.stack([attn_gain, moe_gain], axis=1).reshape(2 * layers, rows).astype(BF).astype(F32)
+    return attn, jnp.pad(gains, ((0, 0), (0, 128 - rows)))
 
 
 def fast_body(nctx, nfs, *args):
@@ -2173,21 +2210,21 @@
     table = jnp.sum(
         jnp.where(routes[:, 0, :, :, None] == expert_ids, gates[:, 0, :, :, None], 0.0), axis=-2
     )
-    packed = [pack_weights(master_set, layer, nctx) for layer in range(LAYERS)]
-    rows = packed[0][0].shape[2]
-    gains = jnp.broadcast_to(jnp.concatenate([gain for _, gain in packed])[None], (nctx, 2 * LAYERS, 128))
+    attn, gains = pack_weights(master_set, nctx)
+    rows = attn.shape[2]
+    gains = jnp.broadcast_to(gains[None], (nctx, 2 * LAYERS, 128))
     shares = table.transpose(2, 0, 1).reshape(nctx, 2, LAYERS, rows_here).transpose(0, 2, 1, 3)
     shares = shares.reshape(nctx, 2 * LAYERS, rows_here)
     pad = jnp.zeros((nctx, 8 - 2 * LAYERS, 128), F32)
     small = jnp.concatenate([gains, pad, shares, pad], axis=1)
-    mats_all, small_all = spread_weights(jnp.stack([send for send, _ in packed]), small, nfs)
+    mats_all, small_all = spread_weights(attn, *master_set[6:], small, nfs)
     shares = lax.dynamic_index_in_dim(
         small_all.reshape(nctx, nfs, 16, 128), lax.axis_index("fsdp"), 1, keepdims=False
     )
     fetched = [
         (
-            small_all[:, 2 * layer, :rows].reshape(-1),
-            small_all[:, 2 * layer + 1, :rows].reshape(-1),
+            small_all[:, 2 * layer, :rows].reshape(1, -1),
+            small_all[:, 2 * layer + 1, :rows].reshape(1, -1),
             shares[:, 8 + 2 * layer : 10 + 2 * layer].transpose(0, 2, 1),
         )
         for layer in range(LAYERS)
@@ -2197,17 +2234,13 @@
     records = []
     for layer in range(LAYERS):
         attn_gain, moe_gain, share = fetched[layer]
-        normed = rms_norm(hidden, attn_gain).astype(BF)
-        mixed, normed_all, queries, keys, values, peaks, sums, attended, *rest = attention_rows(
-            normed, mats_all, layer, cos_part, sin_part, key_at, query_at, nz, nfs
+        middle, normed_all, queries, keys, values, peaks, sums, attended, *rest = attention_rows(
+            hidden, attn_gain, mats_all, layer, cos_part, sin_part, key_at, query_at, nz, nfs
         )
         mats_all = rest[0] if rest else mats_all
-        middle = hidden + mixed
-
-        moe_in = rms_norm(middle, moe_gain).astype(BF)
-        moved, moe_all, gate_act, up_act = experts_forward(moe_in, share, mats_all, layer, nz)
+        moved, moe_all, gate_act, up_act = experts_forward(middle, moe_gain, share, mats_all, layer, nz)
         records.append((hidden, normed_all, queries, keys, values, peaks, sums, attended, middle, moe_all, gate_act, up_act))
-        hidden = middle + moved
+        hidden = moved
 
     output = hidden.astype(BF)
     grad = cotangent[0].astype(jnp.float32)
@@ -2215,16 +2248,12 @@
     for layer in reversed(range(LAYERS)):
         attn_gain, moe_gain, share = fetched[layer]
         hidden, normed_all, queries, keys, values, peaks, sums, attended, middle, moe_all, gate_act, up_act = records[layer]
-        grad_moe_in, grad_all, d_gate, d_up, inner = experts_backward(grad.astype(BF), share, mats_all, layer, gate_act, up_act, nz)
-        through, grad_moe_gain = norm_back(middle, moe_gain, grad_moe_in)
-        grad_middle = grad + through
-
-        grad_normed, middle_all, d_proj = attention_rows_back(
-            grad_middle.astype(BF), mats_all, layer, cos_part, sin_part, key_at, query_at, queries, keys, values, peaks, sums, nz
+        grad_middle, grad_moe_gain, grad_all, d_gate, d_up, inner = experts_backward(
+            grad, middle, moe_gain, share, mats_all, layer, gate_act, up_act, nz
         )
-        through, grad_attn_gain = norm_back(hidden, attn_gain, grad_normed)
-        grad = grad_middle + through
-
+        grad, grad_attn_gain, middle_all, d_proj = attention_rows_back(
+            grad_middle, hidden, attn_gain, mats_all, layer, cos_part, sin_part, key_at, query_at, queries, keys, values, peaks, sums, nz
+        )
         layer_args[layer] = [
             part.reshape(group_rows, -1)
             for part in (normed_all, d_proj, middle_all, attended, moe_all, d_gate, d_up, grad_all, inner)
@@ -2237,23 +2266,17 @@
     collected, gains_in = collect_grads(nctx, nfs, layer_args, extra)
 
     def attn_part(low, high):
-        return jnp.stack(
-            [
-                c[:, 0, :, low:high].transpose(1, 0, 2).reshape(rows, -1).astype(F32)
-                for c in collected
-            ]
-        )
+        part = collected[:, :, 0, :, low:high].transpose(0, 2, 1, 3)
+        return part.reshape(LAYERS, rows, -1).astype(F32)
 
     def expert_part(first):
-        return jnp.stack(
-            [
-                c[:, first : first + 2].reshape((EXPERTS,) + c.shape[2:]).astype(F32)
-                for c in collected
-            ]
-        )
+        part = collected[:, :, first : first + 2]
+        return part.reshape((LAYERS, EXPERTS) + part.shape[3:]).astype(F32)
+
+    gain_sums = jnp.sum(gains_in[:, : 2 * LAYERS, :rows], axis=0).reshape(LAYERS, 2, rows)
 
     def gain_part(kind):
-        return jnp.stack([jnp.sum(gains_in[:, 2 * layer + kind, :rows], axis=0) for layer in range(LAYERS)])
+        return gain_sums[:, kind]
 
     return (
         output[None],

time: 972 us -> 948 us (0.975)
  other arithmetic: 48 us -> 22.7 us
  Pallas kernels: 879 us -> 898 us
  local copies, waits for them, and re-layouts: 33.4 us -> 18.9 us
    another operation x23 -> x3, other arithmetic: 17.5 us -> 0.19 us  [the longest x3 5.61 us: expert_part(): jnp.stack([c[:, first:first + 2].reshape((EXPERTS,) + c.shape[2:]).astype...]
    reduce_sum x9 -> x1, other arithmetic: 11 us -> 0.02 us  [fast_body(): jnp.sum(gains_in[:, :2 * LAYERS, :rows], axis=0).reshape(LAYERS, 2, rows)]
where the time goes in v6:
time: 948 us; the launch traced here: 941 us
  Pallas kernels  898 us (95%)
  other arithmetic  22.7 us (2%)
  local copies, waits for them, and re-layouts  18.9 us (2%)
    pallas_call x1, Pallas kernels, collect_grads(): pl.pallas_call(functools.partial(grads_kernel, nctx, nfs, rows, layers),...  186 us
    pallas_call x2, Pallas kernels, attention_rows(): pl.pallas_call(functools.partial(attention_kernel, nz, nfs, layer), out_s...  150 us
    pallas_call x2, Pallas kernels, attention_rows_back(): pl.pallas_call(functools.partial(attention_back_kernel, nz, layer), out_s...  148 us
    pallas_call x1, Pallas kernels, spread_weights(): pl.pallas_call(functools.partial(weights_kernel, nctx, nfs, rows), out_sh...  145 us
    pallas_call x2, Pallas kernels, experts_backward(): pl.pallas_call(functools.partial(experts_back_kernel, nz, layer), out_sha...  136 us
    pallas_call x2, Pallas kernels, experts_forward(): pl.pallas_call(functools.partial(experts_kernel, nz, layer), out_shape=(j...  134 us

profile of v6, /device:TPU:11, one launch (start us, length us, event | category | flops | bytes accessed | tf_op | source)
XLA Modules:
  0.0 941.3 jit_solution(12536886843155046516)
XLA Ops:
  0.7 2.0 bitcast_convert_fusion.1.x_ref.values_ref
  2.7 1.1 convert_element_type.116
  3.8 0.3 reshape.355
  4.2 0.3 reshape.352
  4.5 0.2 copy_bitcast_fusion
  4.7 0.0 copy-done.3
  4.7 0.2 reshape.354
  4.9 0.2 reshape.353
  5.1 0.1 copy_bitcast_fusion.2
  5.1 1.3 pad_maximum_fusion.attn_ref
  6.6 0.6 pad_maximum_fusion.3.g_ref
  7.2 144.8 %spread_weights.1 = (bf16[2,7,1536,512]{3,2,1,0:T(8,128)(2,1)}, f32[32,16,128]{2,1,0:T(8,128)}) custom-call(bf16[2,8,48,512]{3,2,1,0:T(8,128)(2,1)} %pad_maximum_fusion.attn_ref, f32[2,16,48,512]{3,2,1,0:T(8,128)} %gate_ref.1, f32[2,16,48,512]{3,2,1,0:T(8,128)} %up_ref.1, f32[2,16,48,512]{3,2,1,0:T(8,128)} %down_ref.1, f32[8,16,128]{2,1,0:T(8,128)} %pad_maximum_fusion.3.g_ref), custom_call_target="tpu_custom_call" | custom-call | tf_op jit(solution)/shard_map/spread_weights/pallas_call | solution.py:1567
  152.0 1.4 slice_reduce_fusion.1
  153.4 0.7 reshape_squeeze.12.gain_ref
  154.1 0.1 select_reduce_fusion.1
  154.2 0.2 reduce-window.4
  154.4 0.1 convert_reduce_fusion
  154.5 0.1 select_reduce_fusion.2
  154.6 1.9 fusion
  156.5 1.8 pad_maximum_fusion.1
  158.4 0.1 iota_add_fusion.1
  158.4 1.0 copy.77.key_at_ref
  159.5 0.1 fusion.12
  159.5 0.6 pad_add_fusion.query_at_ref
  160.1 79.6 %attention_forward.2 = (f32[128,1536]{1,0:T(8,128)}, bf16[8,128,1536]{2,1,0:T(8,128)(2,1)}, bf16[8,384,64]{2,1,0:T(8,128)(2,1)}, bf16[1024,64]{1,0:T(8,128)(2,1)...) custom-call(f32[128,1536]{1,0:T(8,128)} %bitcast_convert_fusion.1.x_, ...), custom_call_target="tpu_custom_call", output_to_operand_aliasing={{8}: (2, {})} | custom-call | tf_op jit(solution)/shard_map/attention_forward/pallas_call | solution.py:2000
  239.7 0.7 reshape_squeeze.13.gain_ref
  240.4 0.8 constant_dynamic-slice_fusion
  241.2 0.2 copy.90
  241.5 1.3 slice_bitcast_fusion
  242.8 69.0 %experts_forward.2 = (f32[128,1536]{1,0:T(8,128)}, bf16[8,128,1536]{2,1,0:T(8,128)(2,1)}, bf16[8,128,1024]{2,1,0:T(8,128)(2,1)}, bf16[8,128,1024]{2,1,0:T(8,128)(2,1)}) custom-call(f32[128,1536]{1,0:T(8,128)} %get-tuple-element.62.x_ref.values_ref, f32[1,1536]{1,0:T(1,128)} %reshape_squeeze.13.gain_ref, f32[8,128,2]{2,1,0:T(8,128)} %get-tuple-element.121.share_ref, ...), custom_call_target="tpu_custom_call" | custom-call | tf_op jit(solution)/shard_map/experts_forward/pallas_call | solution.py:1125
  311.8 0.7 reshape_squeeze.14.gain_ref
  312.5 70.3 %attention_forward.3 = (f32[128,1536]{1,0:T(8,128)}, bf16[8,128,1536]{2,1,0:T(8,128)(2,1)}, bf16[8,384,64]{2,1,0:T(8,128)(2,1)}, bf16[1024,64]{1,0:T(8,128)(2,1)...) custom-call(f32[128,1536]{1,0:T(8,128)} %get-tuple-element.64.x_ref.val, ...), custom_call_target="tpu_custom_call" | custom-call | tf_op jit(solution)/shard_map/attention_forward/pallas_call | solution.py:2000
  382.7 0.7 reshape_squeeze.15.gain_ref
  383.4 64.6 %experts_forward.3 = (f32[128,1536]{1,0:T(8,128)}, bf16[8,128,1536]{2,1,0:T(8,128)(2,1)}, bf16[8,128,1024]{2,1,0:T(8,128)(2,1)}, bf16[8,128,1024]{2,1,0:T(8,128)(2,1)}) custom-call(f32[128,1536]{1,0:T(8,128)} %get-tuple-element.65.x_ref.values_ref, f32[1,1536]{1,0:T(1,128)} %reshape_squeeze.15.gain_ref, f32[8,128,2]{2,1,0:T(8,128)} %get-tuple-element.120.share_ref, ...), custom_call_target="tpu_custom_call" | custom-call | tf_op jit(solution)/shard_map/experts_forward/pallas_call | solution.py:1125
  448.0 1.9 convert_bitcast_fusion.4
  449.9 1.0 bitcast_convert_fusion.x_ref
  450.9 67.3 %experts_backward.2 = (f32[128,1536]{1,0:T(8,128)}, f32[1,1536]{1,0:T(1,128)}, bf16[8,128,1536]{2,1,0:T(8,128)(2,1)}, bf16[8,128,1024]{2,1,0:T(8,128)(2,1)}, bf1...) custom-call(f32[128,1536]{1,0:T(8,128)} %bitcast_convert_fusion.x_ref, ...), custom_call_target="tpu_custom_call" | custom-call | tf_op jit(solution)/shard_map/experts_backward/pallas_call | solution.py:1230
  518.2 74.6 %attention_backward.2 = (f32[128,1536]{1,0:T(8,128)}, f32[1,1536]{1,0:T(1,128)}, bf16[8,128,1536]{2,1,0:T(8,128)(2,1)}, bf16[8,128,384]{2,1,0:T(8,128)(2,1)}) custom-call(f32[128,1536]{1,0:T(8,128)} %get-tuple-element.69.x_ref, f32[128,1536]{1,0:T(8,128)} %get-tuple-element.64.x_ref.values_ref, f32[1,1536]{1,0:T(1,128)} %reshape_squeeze.14.gain_ref, ...), custom_call_target="tpu_custom_call" | custom-call | tf_op jit(solution)/shard_map/attention_backward/pallas_call | solution.py:2137
  592.8 68.6 %experts_backward.3 = (f32[128,1536]{1,0:T(8,128)}, f32[1,1536]{1,0:T(1,128)}, bf16[8,128,1536]{2,1,0:T(8,128)(2,1)}, bf16[8,128,1024]{2,1,0:T(8,128)(2,1)}, bf1...) custom-call(f32[128,1536]{1,0:T(8,128)} %get-tuple-element.75.x_ref, ...), custom_call_target="tpu_custom_call" | custom-call | tf_op jit(solution)/shard_map/experts_backward/pallas_call | solution.py:1230
  661.4 73.7 %attention_backward.3 = (f32[128,1536]{1,0:T(8,128)}, f32[1,1536]{1,0:T(1,128)}, bf16[8,128,1536]{2,1,0:T(8,128)(2,1)}, bf16[8,128,384]{2,1,0:T(8,128)(2,1)}) custom-call(f32[128,1536]{1,0:T(8,128)} %get-tuple-element.78.x_ref, f32[128,1536]{1,0:T(8,128)} %bitcast_convert_fusion.1.x_ref.values_ref, f32[1,1536]{1,0:T(1,128)} %reshape_squeeze.12.gain_ref, ...), custom_call_target="tpu_custom_call" | custom-call | tf_op jit(solution)/shard_map/attention_backward/pallas_call | solution.py:2137
  735.2 0.1 stack.37
  735.4 0.1 stack.36
  735.5 0.1 stack.35
  735.6 0.7 reduce.4
  736.4 0.1 stack.34
  736.5 0.1 maximum_bitcast_fusion
  736.6 0.7 pad.13.refs_18_
  737.2 185.7 %collect_grads.1 = (bf16[2,8,7,48,512]{4,3,2,1,0:T(8,128)(2,1)}, f32[8,8,128]{2,1,0:T(8,128)}) custom-call(bf16[1024,1536]{1,0:T(8,128)(2,1)} %bitcast.110, bf16[1024,384]{1,0:T(8,128)(2,1)} %bitcast.126, bf16[1024,1536]{1,0:T(8,128)(2,1)} %bitcast.117, bf16[1024,192]{1,0:T(8,128)(2,1)} %bitcast.127, bf16[1024,1536]{1,0:T(8,128)(2,1)} %bitcast.111, ...), custom_call_target="tpu_custom_call" | custom-call | tf_op jit(solution)/shard_map/collect_grads/pallas_call | solution.py:1848
  922.9 1.4 convert_bitcast_fusion
  924.3 0.5 copy.86
  924.8 1.1 reshape.382
  925.8 1.2 convert_bitcast_fusion.2
  927.0 0.1 copy.87
  927.1 0.8 reshape.383
  927.9 0.1 copy.88
  928.1 0.8 reshape.384
  928.9 0.5 copy.89
  929.3 1.1 reshape.385
  930.4 0.6 fusion.15
  931.0 2.7 fusion.14
  933.7 2.1 convert.36
  935.8 2.1 convert.37
  937.9 2.1 convert.38
  940.0 0.9 copy.97
  (54 shorter events, 0.4 us)
Async XLA Ops:
  0.6 3.5 copy-start.1
  3.8 0.9 copy-start.3
  3.8 1.1 copy-start.4
  4.6 1.8 copy-start.6
  4.7 1.8 copy-start.7
  4.7 1.8 copy-start.11
  4.7 1.8 copy-start.12
  7.2 146.9 %copy-start.13 = (s32[1,8]{1,0:T(1,128)S(1)}, s32[1,8]{1,0:T(1,128)}, u32[]{:S(2)}) copy-start(s32[1,8]{1,0:T(1,128)} %param.18) | copy-start | bytes 100
  7.2 147.0 %copy-start.14 = (s32[1,4]{1,0:T(1,128)S(1)}, s32[1,4]{1,0:T(1,128)}, u32[]{:S(2)}) copy-start(s32[1,4]{1,0:T(1,128)} %param.17) | copy-start | bytes 52
  383.4 66.5 %copy-start.2 = (bf16[1,128,1536]{2,1,0:T(8,128)(2,1)S(1)}, bf16[1,128,1536]{2,1,0:T(8,128)(2,1)}, u32[]{:S(2)}) copy-start(bf16[1,128,1536]{2,1,0:T(8,128)(2,1)} %param.16) | copy-start | bytes 1179652
  661.4 73.8 %copy-start.8 = (f32[1,1536]{1,0:T(1,128)S(1)}, f32[1,1536]{1,0:T(1,128)}, u32[]{:S(2)}) copy-start(f32[1,1536]{1,0:T(1,128)} %get-tuple-element.106) | copy-start | bytes 18436
  661.4 73.9 %copy-start.9 = (f32[1,1536]{1,0:T(1,128)S(1)}, f32[1,1536]{1,0:T(1,128)}, u32[]{:S(2)}) copy-start(f32[1,1536]{1,0:T(1,128)} %get-tuple-element.105) | copy-start | bytes 18436
  661.4 74.0 %copy-start.10 = (f32[1,1536]{1,0:T(1,128)S(1)}, f32[1,1536]{1,0:T(1,128)}, u32[]{:S(2)}) copy-start(f32[1,1536]{1,0:T(1,128)} %get-tuple-element.104) | copy-start | bytes 18436
  927.9 2.5 copy-start.5
  937.9 2.1 copy-start
